TPU v7x, 8 devices: a whole 2x2x1 slice. The times are simulated.
8 devices in a mesh: mat: 2 (over z, y), row: 4 (over x, core).
Axes of the slice: x: 2, y: 2, z: 1, core: 2. Of those that a mesh axis runs over, the one named last changes fastest.
Arguments:
- a_mat: bfloat16 [28672, 1024], P(('mat', 'row')), parts along dimension 0
Outputs:
- output: float32 [8, 3, 3584, 3584], P(('mat', 'row')), parts along dimension 0
There are 2 independent parts. A program takes and returns all parts, laid end to end along the dimension named above; each array names one.
All inputs are finite; a program needn't handle non-finite values.
Results may differ from a plain program's by a relative error of at most 0.001.
Values are sent between devices in bfloat16 or wider.
A program may use at most 1 GiB of HBM per device.

v0:
```python
import math
import jax
import jax.numpy as jnp
from jax import lax
from jax.sharding import PartitionSpec as P


def slot_offsets(group_size):
    half_group = group_size // 2
    low_count = 2 ** (int(math.log2(half_group)) // 2)
    low_off = [low_count - 1 - (slot_idx - 1) % low_count for slot_idx in range(1, half_group + 1)]
    high_off = [((slot_idx - 1) // low_count + 1) * low_count for slot_idx in range(1, half_group + 1)]
    return low_count, low_off, high_off


def slot_masks(dev_idx, group_size):
    half_group = group_size // 2
    low_count, low_off, high_off = slot_offsets(group_size)
    low_blk = (dev_idx + jnp.array(low_off)) % group_size
    high_blk = (dev_idx + jnp.array(high_off)) % group_size
    flip_slot = high_blk < low_blk
    keep_slot = (jnp.arange(half_group) < half_group - 1) | (low_blk < half_group)
    return flip_slot, keep_slot


def solution(mesh):
    group_size = mesh.shape["row"]
    half_group = group_size // 2
    low_count, low_off, high_off = slot_offsets(group_size)
    low_shifts = [low_count - 1 - col_idx for col_idx in range(low_count)]
    high_shifts = [low_count * (high_idx + 1) for high_idx in range(half_group // low_count)]

    def fetch_block(a_local, blk_shift):
        if blk_shift == 0:
            return a_local
        send_pairs = [((dest_idx + blk_shift) % group_size, dest_idx) for dest_idx in range(group_size)]
        return lax.ppermute(a_local, "row", send_pairs)

    def local_gram(a_local):
        low_stack = jnp.stack([fetch_block(a_local, blk_shift) for blk_shift in low_shifts])
        high_stack = jnp.stack([fetch_block(a_local, blk_shift) for blk_shift in high_shifts])
        blk_rows = a_local.shape[0]
        diag_blk = jnp.einsum("xk,yk->xy", a_local, a_local, preferred_element_type=jnp.float32)
        grid_prod = jnp.einsum("jxk,cyk->jcxy", high_stack, low_stack, preferred_element_type=jnp.float32)
        off_diag = grid_prod.reshape(half_group, blk_rows, blk_rows)
        flip_slot, keep_slot = slot_masks(lax.axis_index("row"), group_size)
        oriented = jnp.where(flip_slot[:, None, None], jnp.swapaxes(off_diag, 1, 2), off_diag)
        oriented = jnp.where(keep_slot[:, None, None], oriented, 0.0)
        return jnp.concatenate([diag_blk[None], oriented])[None]

    return jax.shard_map(local_gram, mesh=mesh, in_specs=(P(("mat", "row"), None),), out_specs=P(("mat", "row"), None, None, None), check_vma=False)
```

profile of v0, /device:TPU:0, one launch (start us, length us, event | category | flops | bytes accessed | tf_op | source)
XLA Modules:
  0.0 594.7 jit_solution(1587590109183133917)
XLA Ops:
  0.0 2.8 collective-permute-start
  2.8 0.6 collective-permute-start.1
  3.3 1.2 compare_or_fusion
  4.6 35.4 %convolution_bitcast_fusion = f32[1,3584,3584]{2,1,0:T(8,128)} fusion(bf16[3584,1024]{1,0:T(8,128)(2,1)} %param.3), kind=kOutput, calls=%fused_computation.3 | convolution fusion | flops 26306674688 | bytes 58720256 | tf_op jit(solution)/shard_map/xk,yk->xy/dot_general | solution.py:43
  40.0 121.1 %collective-permute-done = bf16[3584,1024]{1,0:T(8,128)(2,1)} collective-permute-done((bf16[3584,1024]{1,0:T(8,128)(2,1)}, bf16[3584,1024]{1,0:T(8,128)(2,1)}, u32[]{:S(2)}, u32[]{:S(2)}) %collective-permute-start) | collective-permute-done | bytes 7340064 | tf_op jit(solution)/shard_map/ppermute | solution.py:37
  161.0 79.6 %collective-permute-done.1 = bf16[3584,1024]{1,0:T(8,128)(2,1)} collective-permute-done((bf16[3584,1024]{1,0:T(8,128)(2,1)}, bf16[3584,1024]{1,0:T(8,128)(2,1)}, u32[]{:S(2)}, u32[]{:S(2)}) %collective-permute-start.1) | collective-permute-done | bytes 7340064 | tf_op jit(solution)/shard_map/ppermute | solution.py:37
  240.6 63.3 %fusion.1 = f32[2,3584,3584]{2,1,0:T(8,128)} fusion(bf16[1,3584,1024]{2,1,0:T(8,128)(2,1)} %bitcast.2, bf16[1,3584,1024]{2,1,0:T(8,128)(2,1)} %bitcast.1, bf16[3584,1024]{1,0:T(8,128)(2,1)} %param.3), kind=kOutput, calls=%fused_computation.4 | convolution fusion | flops 52620689408 | bytes 124780544 | tf_op jit(solution)/shard_map/jxk,cyk->jcxy/dot_general | solution.py:44
  304.0 0.0 copy-start
  304.0 0.0 copy-start.1
  304.0 94.1 %copy.4 = f32[2,3584,3584]{1,2,0:T(8,128)} copy(f32[2,3584,3584]{2,1,0:T(8,128)} %fusion.1) | data formatting | bytes 205520896 | tf_op jit(solution)/shard_map/jxk,cyk->jcxy/dot_general | solution.py:44
  398.1 0.0 copy-done
  398.1 0.0 copy-done.1
  398.1 97.5 %fusion = f32[2,3584,3584]{2,1,0:T(8,128)} fusion(f32[2,3584,3584]{2,1,0:T(8,128)} %fusion.1, f32[2,3584,3584]{1,2,0:T(8,128)} %copy.4, pred[2]{0:T(512)(128)(4,1)S(1)} %copy-done.1, pred[2]{0:T(512)(128)(4,1)S(1)} %copy-done), kind=kLoop, calls=%fused_computation.2 | loop fusion | flops 51380224 | bytes 308281344 | tf_op jit(solution)/shard_map/jit(_where)/select_n | solution.py:48
  495.7 99.0 %maximum_bitcast_fusion = f32[1,3,3584,3584]{3,2,1,0:T(8,128)} fusion(f32[2,3584,3584]{2,1,0:T(8,128)} %fusion, f32[1,3584,3584]{2,1,0:T(8,128)} %convolution_bitcast_fusion), kind=kLoop, calls=%fused_computation | loop fusion | flops 38535168 | bytes 308281344 | tf_op jit(solution)/shard_map/broadcast_in_dim | solution.py:49
Async XLA Ops:
  0.0 161.0 %collective-permute-start = (bf16[3584,1024]{1,0:T(8,128)(2,1)}, bf16[3584,1024]{1,0:T(8,128)(2,1)}, u32[]{:S(2)}, u32[]{:S(2)}) collective-permute-start(bf16[3584,1024]{1,0:T(8,128)(2,1)} %param.3), channel_id=1, source_target_pairs={{1,0},{2,1},{3,2},{0,3},{5,4},{6,5},{7,6},{4,7}} | collective-permute-start | bytes 22020104 | tf_op jit(solution)/shard_map/ppermute | solution.py:37
  2.8 237.9 %collective-permute-start.1 = (bf16[3584,1024]{1,0:T(8,128)(2,1)}, bf16[3584,1024]{1,0:T(8,128)(2,1)}, u32[]{:S(2)}, u32[]{:S(2)}) collective-permute-start(bf16[3584,1024]{1,0:T(8,128)(2,1)} %param.3), channel_id=1, source_target_pairs={{2,0},{3,1},{0,2},{1,3},{6,4},{7,5},{4,6},{5,7}} | collective-permute-start | bytes 22020104 | tf_op jit(solution)/shard_map/ppermute | solution.py:37
  304.0 94.2 %copy-start = (pred[2]{0:T(512)(128)(4,1)S(1)}, pred[2]{0:T(512)(128)(4,1)}, u32[]{:S(2)}) copy-start(pred[2]{0:T(512)(128)(4,1)} %get-tuple-element.5) | copy-start | bytes 10
  304.0 94.2 %copy-start.1 = (pred[2]{0:T(512)(128)(4,1)S(1)}, pred[2]{0:T(512)(128)(4,1)}, u32[]{:S(2)}) copy-start(pred[2]{0:T(512)(128)(4,1)} %get-tuple-element.6) | copy-start | bytes 10
where the time goes:
time: 596 us; the launch traced here: 595 us
  waiting for transfers between devices  201 us (34%)
  other arithmetic  198 us (33%)
  matrix products  98.7 us (17%)
  local copies, waits for them, and re-layouts  94.2 us (16%)
    ppermute x2, waiting for transfers between devices, fetch_block(): return lax.ppermute(a_local, 'row', send_pairs)  201 us
    broadcast_in_dim x1, other arithmetic, local_gram(): return jnp.concatenate([diag_blk[None], oriented])[None]  99 us
    select_n x1, other arithmetic, local_gram(): oriented = jnp.where(keep_slot[:, None, None], oriented, 0.0)  97.5 us
    dot_general x1, local copies, waits for them, and re-layouts, local_gram(): jnp.einsum('jxk,cyk->jcxy', high_stack, low_stack, preferred_element_type...  94.1 us
    dot_general x1, matrix products, local_gram(): jnp.einsum('jxk,cyk->jcxy', high_stack, low_stack, preferred_element_type...  63.3 us
    dot_general x1, matrix products, local_gram(): jnp.einsum('xk,yk->xy', a_local, a_local, preferred_element_type=jnp.floa...  35.4 us
  transfers between devices with their start and end apart: 2, of which 2 were waited for; matrix products, arithmetic and copies ran while one was open for 6% of the time, Pallas kernels for 0%

commit v1 on v0

v1 whole, which is shorter than its diff:
```python
import jax
import jax.numpy as jnp
from jax import lax
from jax.experimental import pallas as pl
from jax.experimental.pallas import tpu as pltpu
from jax.sharding import PartitionSpec as P


TILE = 512
NEXT = [(1, 0), (2, 1), (3, 2), (0, 3)]
FAR = [(3, 1)]
PASS = [(1, 0)]
PARTS = [(0, 512), (512, 1536), (2048, 1024), (3072, 512)]
FARS = [(0, 512), (512, 1024), (1536, 512), (2048, 1024), (3072, 256), (3328, 256)]
DEPTH = 3


def dot_t(x, y):
    return lax.dot_general(x, y, (((1,), (1,)), ((), ())), preferred_element_type=jnp.float32)


def tiles(ref, index, size):
    return ref[pl.ds(pl.multiple_of(index * size, size), size), :]


def stream(steps, buf, sem, value, place):
    def copy(s):
        return pltpu.make_async_copy(buf.at[lax.rem(s, DEPTH)], place(s), sem.at[lax.rem(s, DEPTH)])

    @pl.loop(0, steps)
    def _(s):
        @pl.when(s >= DEPTH)
        def _():
            copy(s - DEPTH).wait()

        buf[lax.rem(s, DEPTH)] = value(s)
        copy(s).start()

    for s in range(max(steps - DEPTH, 0), steps):
        copy(s).wait()


def call(kernel, rows, cols, depth, out, refs, scratch, tile):
    made = isinstance(out, jax.ShapeDtypeStruct)
    args = [a for a, _ in refs] + ([] if made else [out])
    return pl.pallas_call(
        kernel,
        in_specs=[pl.BlockSpec(memory_space=space) for _, space in refs] + ([] if made else [pl.BlockSpec(memory_space=pl.ANY)]),
        out_specs=pl.BlockSpec(memory_space=pl.ANY),
        out_shape=jax.ShapeDtypeStruct(out.shape, out.dtype),
        input_output_aliases={} if made else {len(args) - 1: 0},
        scratch_shapes=[pltpu.VMEM((DEPTH, *tile), jnp.float32), pltpu.SemaphoreType.DMA((DEPTH,)), *scratch],
        cost_estimate=pl.CostEstimate(
            flops=2 * rows * cols * depth, bytes_accessed=4 * rows * cols + 2 * rows * depth, transcendentals=0
        ),
        compiler_params=pltpu.CompilerParams(vmem_limit_bytes=24 << 20),
    )(*args)


def diag(own):
    rows, depth = own.shape

    def kernel(own_ref, out_ref, buf, sem):
        wide = rows // TILE

        def place(s):
            return out_ref.at[0, 0, pl.ds(s // wide * TILE, TILE), pl.ds(lax.rem(s, wide) * TILE, TILE)]

        def value(s):
            return dot_t(tiles(own_ref, s // wide, TILE), tiles(own_ref, lax.rem(s, wide), TILE))

        stream(wide * wide, buf, sem, value, place)

    out = jax.ShapeDtypeStruct((1, 3, rows, rows), jnp.float32)
    return call(kernel, rows, rows, depth, out, [(own, pltpu.VMEM)], [], (TILE, TILE))


def slot1(first, size, part, own, out):
    rows, depth = own.shape

    def kernel(part_ref, own_ref, _, out_ref, buf, sem, held, held_sem):
        p = lax.axis_index("row")
        load = pltpu.make_async_copy(part_ref, held, held_sem)
        load.start()
        load.wait()
        tall = size // TILE
        steps = tall * (rows // TILE)

        @pl.when(p < 3)
        def _():
            stream(
                steps, buf, sem,
                lambda s: dot_t(tiles(held, lax.rem(s, tall), TILE), tiles(own_ref, s // tall, TILE)),
                lambda s: out_ref.at[0, 1, pl.ds(first + lax.rem(s, tall) * TILE, TILE), pl.ds(s // tall * TILE, TILE)],
            )

        @pl.when(p == 3)
        def _():
            stream(
                steps, buf, sem,
                lambda s: dot_t(tiles(own_ref, s // tall, TILE), tiles(held, lax.rem(s, tall), TILE)),
                lambda s: out_ref.at[0, 1, pl.ds(s // tall * TILE, TILE), pl.ds(first + lax.rem(s, tall) * TILE, TILE)],
            )

    scratch = [pltpu.VMEM((size, depth), jnp.bfloat16), pltpu.SemaphoreType.DMA]
    return call(kernel, size, rows, depth, out, [(part, pl.ANY), (own, pltpu.VMEM)], scratch, (TILE, TILE))


def slot2(first, size, near_first, near, far, own, out):
    rows, depth = own.shape
    high = min(size, TILE)

    def kernel(near_ref, far_ref, own_ref, _, out_ref, buf, sem, held, held_sem):
        p = lax.axis_index("row")
        tall = size // high
        steps = tall * (rows // TILE)

        def place(s):
            return out_ref.at[0, 2, pl.ds(first + lax.rem(s, tall) * high, high), pl.ds(s // tall * TILE, TILE)]

        @pl.when(p == 0)
        def _():
            load = pltpu.make_async_copy(near_ref.at[pl.ds(first - near_first, size), :], held, held_sem)
            load.start()
            load.wait()

        @pl.when(p == 1)
        def _():
            load = pltpu.make_async_copy(far_ref, held, held_sem)
            load.start()
            load.wait()

        @pl.when(p < 2)
        def _():
            stream(steps, buf, sem, lambda s: dot_t(tiles(held, lax.rem(s, tall), high), tiles(own_ref, s // tall, TILE)), place)

        @pl.when(p >= 2)
        def _():
            stream(steps, buf, sem, lambda s: jnp.zeros((high, TILE), jnp.float32), place)

    scratch = [pltpu.VMEM((size, depth), jnp.bfloat16), pltpu.SemaphoreType.DMA]
    refs = [(near, pl.ANY), (far, pl.ANY), (own, pltpu.VMEM)]
    return call(kernel, size, rows, depth, out, refs, scratch, (high, TILE))


def solution(mesh):
    assert mesh.shape["row"] == 4

    def send(a, pairs):
        return lax.ppermute(a, "row", pairs)

    def local(a):
        parts = [send(a[first:first + size], NEXT) for first, size in PARTS]
        out = diag(a)
        passed = [send(part, PASS) for part in parts]
        far = [send(a[first:first + size], FAR) for first, size in FARS]
        for k, (first, size) in enumerate(PARTS):
            out = slot1(first, size, parts[k], a, out)
        for j, (first, size) in enumerate(FARS):
            near = max(k for k, (start, _) in enumerate(PARTS) if start <= first)
            out = slot2(first, size, PARTS[near][0], passed[near], far[j], a, out)
        return out

    return jax.shard_map(
        local, mesh=mesh, in_specs=(P(("mat", "row"), None),), out_specs=P(("mat", "row"), None, None, None), check_vma=False
    )
```

time: 596 us -> 207 us (0.35)
  the two profiles are of different devices: /device:TPU:0 before, /device:TPU:1 now
where the time goes in v1:
time: 207 us; the launch traced here: 206 us
  Pallas kernels  137 us (66%)
  waiting for transfers between devices  35.7 us (17%)
  starting transfers between devices  23.4 us (11%)
  local copies, waits for them, and re-layouts  9.88 us (5%)
    pallas_call x11, Pallas kernels, call(): pl.pallas_call(kernel, in_specs=[pl.BlockSpec(memory_space=space) for _,...  137 us
    ppermute x14, waiting for transfers between devices, send(): return lax.ppermute(a, 'row', pairs)  35.7 us
    ppermute x14, starting transfers between devices, send(): return lax.ppermute(a, 'row', pairs)  23.4 us
    slice x2, local copies, waits for them, and re-layouts, local(): parts = [send(a[first:first + size], NEXT) for first, size in PARTS]  6.36 us
  transfers between devices with their start and end apart: 14, of which 1 were waited for; matrix products, arithmetic and copies ran while one was open for 4% of the time, Pallas kernels for 64%

profile of v1, /device:TPU:1, one launch (start us, length us, event | category | flops | bytes accessed | tf_op | source)
XLA Modules:
  0.0 206.1 jit_solution(12076496052357078824)
XLA Ops:
  0.0 0.0 copy-start
  0.0 2.4 %slice.30 = bf16[1536,1024]{1,0:T(8,128)(2,1)S(1)} slice(bf16[3584,1024]{1,0:T(8,128)(2,1)} %own_ref.21), slice={[512:2048], [0:1024]} | slice | bytes 6291456 | tf_op jit(solution)/shard_map/slice | solution.py:153
  2.4 0.0 collective-permute-start.7
  2.4 4.0 %fusion = (bf16[512,1024]{1,0:T(8,128)(2,1)}, bf16[512,1024]{1,0:T(8,128)(2,1)}, bf16[512,1024]{1,0:T(8,128)(2,1)}) fusion(bf16[3584,1024]{1,0:T(8,128)(2,1)} %own_ref.21), kind=kLoop, calls=%fused_computation | loop fusion | bytes 6291456 | tf_op jit(solution)/shard_map/slice | solution.py:153
  6.4 2.0 collective-permute-start.11
  8.4 1.3 collective-permute-start.13
  9.7 0.0 copy-done
  9.7 2.4 %fusion.1 = (bf16[1024,1024]{1,0:T(8,128)(2,1)}, bf16[1024,1024]{1,0:T(8,128)(2,1)}) fusion(bf16[3584,1024]{1,0:T(8,128)(2,1)S(1)} %copy-done), kind=kLoop, calls=%fused_computation.1 | loop fusion | bytes 8388608 | tf_op jit(solution)/shard_map/slice | solution.py:156
  12.1 1.0 collective-permute-start.4
  13.2 2.4 %collective-permute-start = (bf16[512,1024]{1,0:T(8,128)(2,1)}, bf16[512,1024]{1,0:T(8,128)(2,1)}, u32[]{:S(2)}, u32[]{:S(2)}) collective-permute-start(bf16[512,1024]{1,0:T(8,128)(2,1)} %get-tuple-element.7), channel_id=1, source_target_pairs={{1,0},{2,1},{3,2},{0,3},{5,4},{6,5},{7,6},{4,7}} | collective-permute-start | bytes 3145736 | tf_op jit(solution)/shard_map/ppermute | solution.py:150
  15.6 35.7 %collective-permute-done.7.part_ref = bf16[1536,1024]{1,0:T(8,128)(2,1)} collective-permute-done((bf16[1536,1024]{1,0:T(8,128)(2,1)S(1)}, bf16[1536,1024]{1,0:T(8,128)(2,1)}, u32[]{:S(2)}, u32[]{:S(2)}) %collective-permute-start.7) | collective-permute-done | bytes 3145760 | tf_op jit(solution)/shard_map/ppermute | solution.py:150
  51.3 3.0 %collective-permute-start.8 = (bf16[1536,1024]{1,0:T(8,128)(2,1)}, bf16[1536,1024]{1,0:T(8,128)(2,1)}, u32[]{:S(2)}, u32[]{:S(2)}) collective-permute-start(bf16[1536,1024]{1,0:T(8,128)(2,1)} %collective-permute-done.7.part_ref), channel_id=1, source_target_pairs={{1,0},{5,4}} | collective-permute-start | bytes 9437192 | tf_op jit(solution)/shard_map/ppermute | solution.py:150
  54.2 38.1 %shard_map.17._ = f32[1,3,3584,3584]{3,2,1,0:T(8,128)} custom-call(bf16[3584,1024]{1,0:T(8,128)(2,1)S(1)} %copy-done), custom_call_target="tpu_custom_call" | custom-call | flops 26306674688 | bytes 58720256 | tf_op jit(solution)/shard_map/pallas_call | solution.py:46
  92.4 1.1 fusion.2
  93.5 0.0 collective-permute-done.11.part_ref
  93.5 1.3 collective-permute-start.10
  94.8 7.5 %shard_map.18._ = f32[1,3,3584,3584]{3,2,1,0:T(8,128)} custom-call(bf16[512,1024]{1,0:T(8,128)(2,1)} %collective-permute-done.11.part_ref, bf16[3584,1024]{1,0:T(8,128)(2,1)S(1)} %copy-done, f32[1,3,3584,3584]{3,2,1,0:T(8,128)} %shard_map.17._), custom_call_target="tpu_custom_call", output_to_operand_aliasing={{}: (2, {})} | custom-call | flops 3758096384 | bytes 8388608 | tf_op jit(solution)/shard_map/pallas_call | solution.py:46
  102.2 18.8 %shard_map.19._ = f32[1,3,3584,3584]{3,2,1,0:T(8,128)} custom-call(bf16[1536,1024]{1,0:T(8,128)(2,1)} %collective-permute-done.7.part_ref, bf16[3584,1024]{1,0:T(8,128)(2,1)S(1)} %copy-done, f32[1,3,3584,3584]{3,2,1,0:T(8,128)} %shard_map.18._), custom_call_target="tpu_custom_call", output_to_operand_aliasing={{}: (2, {})} | custom-call | flops 11274289152 | bytes 25165824 | tf_op jit(solution)/shard_map/pallas_call | solution.py:46
  121.1 0.0 collective-permute-done.part_ref
  121.1 1.3 collective-permute-start.6
  122.4 0.0 collective-permute-done.13.far_ref
  122.4 2.3 %collective-permute-start.12 = (bf16[512,1024]{1,0:T(8,128)(2,1)}, bf16[512,1024]{1,0:T(8,128)(2,1)}, u32[]{:S(2)}, u32[]{:S(2)}) collective-permute-start(bf16[512,1024]{1,0:T(8,128)(2,1)} %collective-permute-done.11.part_ref), channel_id=1, source_target_pairs={{1,0},{5,4}} | collective-permute-start | bytes 3145736 | tf_op jit(solution)/shard_map/ppermute | solution.py:150
  124.7 0.0 collective-permute-done.4.part_ref
  124.7 2.6 %collective-permute-start.5 = (bf16[1024,1024]{1,0:T(8,128)(2,1)}, bf16[1024,1024]{1,0:T(8,128)(2,1)}, u32[]{:S(2)}, u32[]{:S(2)}) collective-permute-start(bf16[1024,1024]{1,0:T(8,128)(2,1)} %collective-permute-done.4.part_ref), channel_id=1, source_target_pairs={{1,0},{5,4}} | collective-permute-start | bytes 6291464 | tf_op jit(solution)/shard_map/ppermute | solution.py:150
  127.3 13.2 %shard_map.20._ = f32[1,3,3584,3584]{3,2,1,0:T(8,128)} custom-call(bf16[1024,1024]{1,0:T(8,128)(2,1)} %collective-permute-done.4.part_ref, bf16[3584,1024]{1,0:T(8,128)(2,1)S(1)} %copy-done, f32[1,3,3584,3584]{3,2,1,0:T(8,128)} %shard_map.19._), custom_call_target="tpu_custom_call", output_to_operand_aliasing={{}: (2, {})} | custom-call | flops 7516192768 | bytes 16777216 | tf_op jit(solution)/shard_map/pallas_call | solution.py:46
  140.4 7.5 %shard_map.21._ = f32[1,3,3584,3584]{3,2,1,0:T(8,128)} custom-call(bf16[512,1024]{1,0:T(8,128)(2,1)} %collective-permute-done.part_ref, bf16[3584,1024]{1,0:T(8,128)(2,1)S(1)} %copy-done, f32[1,3,3584,3584]{3,2,1,0:T(8,128)} %shard_map.20._), custom_call_target="tpu_custom_call", output_to_operand_aliasing={{}: (2, {})} | custom-call | flops 3758096384 | bytes 8388608 | tf_op jit(solution)/shard_map/pallas_call | solution.py:46
  147.9 0.0 collective-permute-done.12.near_ref
  147.9 1.3 collective-permute-start.9
  149.2 7.5 %shard_map.22._ = f32[1,3,3584,3584]{3,2,1,0:T(8,128)} custom-call(bf16[512,1024]{1,0:T(8,128)(2,1)} %collective-permute-done.12.near_ref, bf16[512,1024]{1,0:T(8,128)(2,1)} %collective-permute-done.13.far_ref, bf16[3584,1024]{1,0:T(8,128)(2,1)S(1)} %copy-done, f32[1,3,3584,3584]{3,2,1,0:T(8,128)} %shard_map.21._), custom_call_target="tpu_custom_call", output_to_operand_aliasing={{}: (3, {})} | custom-call | flops 3758096384 | bytes 8388608 | tf_op jit(solution)/shard_map/pallas_call | solution.py:46
  156.7 0.0 collective-permute-done.10.far_ref
  156.7 1.3 collective-permute-start.3
  158.0 0.0 collective-permute-done.8.near_ref
  158.1 1.3 collective-permute-start.2
  159.4 13.2 %shard_map.23._ = f32[1,3,3584,3584]{3,2,1,0:T(8,128)} custom-call(bf16[1536,1024]{1,0:T(8,128)(2,1)} %collective-permute-done.8.near_ref, bf16[1024,1024]{1,0:T(8,128)(2,1)} %collective-permute-done.10.far_ref, bf16[3584,1024]{1,0:T(8,128)(2,1)S(1)} %copy-done, f32[1,3,3584,3584]{3,2,1,0:T(8,128)} %shard_map.22._), custom_call_target="tpu_custom_call", output_to_operand_aliasing={{}: (3, {})} | custom-call | flops 7516192768 | bytes 16777216 | tf_op jit(solution)/shard_map/pallas_call | solution.py:46
  172.6 0.0 collective-permute-done.9.far_ref
  172.6 2.3 %collective-permute-start.1 = (bf16[512,1024]{1,0:T(8,128)(2,1)}, bf16[512,1024]{1,0:T(8,128)(2,1)}, u32[]{:S(2)}, u32[]{:S(2)}) collective-permute-start(bf16[512,1024]{1,0:T(8,128)(2,1)} %collective-permute-done.part_ref), channel_id=1, source_target_pairs={{1,0},{5,4}} | collective-permute-start | bytes 3145736 | tf_op jit(solution)/shard_map/ppermute | solution.py:150
  174.9 7.5 %shard_map.24._ = f32[1,3,3584,3584]{3,2,1,0:T(8,128)} custom-call(bf16[1536,1024]{1,0:T(8,128)(2,1)} %collective-permute-done.8.near_ref, bf16[512,1024]{1,0:T(8,128)(2,1)} %collective-permute-done.9.far_ref, bf16[3584,1024]{1,0:T(8,128)(2,1)S(1)} %copy-done, f32[1,3,3584,3584]{3,2,1,0:T(8,128)} %shard_map.23._), custom_call_target="tpu_custom_call", output_to_operand_aliasing={{}: (3, {})} | custom-call | flops 3758096384 | bytes 8388608 | tf_op jit(solution)/shard_map/pallas_call | solution.py:46
  182.4 0.0 collective-permute-done.6.far_ref
  182.4 0.0 collective-permute-done.5.near_ref
  182.4 13.2 %shard_map.25._ = f32[1,3,3584,3584]{3,2,1,0:T(8,128)} custom-call(bf16[1024,1024]{1,0:T(8,128)(2,1)} %collective-permute-done.5.near_ref, bf16[1024,1024]{1,0:T(8,128)(2,1)} %collective-permute-done.6.far_ref, bf16[3584,1024]{1,0:T(8,128)(2,1)S(1)} %copy-done, f32[1,3,3584,3584]{3,2,1,0:T(8,128)} %shard_map.24._), custom_call_target="tpu_custom_call", output_to_operand_aliasing={{}: (3, {})} | custom-call | flops 7516192768 | bytes 16777216 | tf_op jit(solution)/shard_map/pallas_call | solution.py:46
  195.6 0.0 collective-permute-done.3.far_ref
  195.6 0.0 collective-permute-done.1.near_ref
  195.6 5.2 %shard_map.26._ = f32[1,3,3584,3584]{3,2,1,0:T(8,128)} custom-call(bf16[512,1024]{1,0:T(8,128)(2,1)} %collective-permute-done.1.near_ref, bf16[256,1024]{1,0:T(8,128)(2,1)} %collective-permute-done.3.far_ref, bf16[3584,1024]{1,0:T(8,128)(2,1)S(1)} %copy-done, f32[1,3,3584,3584]{3,2,1,0:T(8,128)} %shard_map.25._), custom_call_target="tpu_custom_call", output_to_operand_aliasing={{}: (3, {})} | custom-call | flops 1879048192 | bytes 4194304 | tf_op jit(solution)/shard_map/pallas_call | solution.py:46
  200.9 0.0 collective-permute-done.2.far_ref
  200.9 5.2 %shard_map.27 = f32[1,3,3584,3584]{3,2,1,0:T(8,128)} custom-call(bf16[512,1024]{1,0:T(8,128)(2,1)} %collective-permute-done.1.near_ref, bf16[256,1024]{1,0:T(8,128)(2,1)} %collective-permute-done.2.far_ref, bf16[3584,1024]{1,0:T(8,128)(2,1)S(1)} %copy-done, f32[1,3,3584,3584]{3,2,1,0:T(8,128)} %shard_map.26._), custom_call_target="tpu_custom_call", output_to_operand_aliasing={{}: (3, {})} | custom-call | flops 1879048192 | bytes 4194304 | tf_op jit(solution)/shard_map/pallas_call | solution.py:46
Async XLA Ops:
  0.0 9.7 %copy-start = (bf16[3584,1024]{1,0:T(8,128)(2,1)S(1)}, bf16[3584,1024]{1,0:T(8,128)(2,1)}, u32[]{:S(2)}) copy-start(bf16[3584,1024]{1,0:T(8,128)(2,1)} %own_ref.21) | copy-start | bytes 22020100
  2.4 48.9 %collective-permute-start.7 = (bf16[1536,1024]{1,0:T(8,128)(2,1)S(1)}, bf16[1536,1024]{1,0:T(8,128)(2,1)}, u32[]{:S(2)}, u32[]{:S(2)}) collective-permute-start(bf16[1536,1024]{1,0:T(8,128)(2,1)S(1)} %slice.30), channel_id=1, source_target_pairs={{1,0},{2,1},{3,2},{0,3},{5,4},{6,5},{7,6},{4,7}} | collective-permute-start | bytes 9437192 | tf_op jit(solution)/shard_map/ppermute | solution.py:150
  6.4 87.1 %collective-permute-start.11 = (bf16[512,1024]{1,0:T(8,128)(2,1)}, bf16[512,1024]{1,0:T(8,128)(2,1)}, u32[]{:S(2)}, u32[]{:S(2)}) collective-permute-start(bf16[512,1024]{1,0:T(8,128)(2,1)} %get-tuple-element.5), channel_id=1, source_target_pairs={{1,0},{2,1},{3,2},{0,3},{5,4},{6,5},{7,6},{4,7}} | collective-permute-start | bytes 3145736 | tf_op jit(solution)/shard_map/ppermute | solution.py:150
  8.4 113.9 %collective-permute-start.13 = (bf16[512,1024]{1,0:T(8,128)(2,1)}, bf16[512,1024]{1,0:T(8,128)(2,1)}, u32[]{:S(2)}, u32[]{:S(2)}) collective-permute-start(bf16[512,1024]{1,0:T(8,128)(2,1)} %get-tuple-element.5), channel_id=1, source_target_pairs={{3,1},{7,5}} | collective-permute-start | bytes 3145736 | tf_op jit(solution)/shard_map/ppermute | solution.py:150
  12.1 112.5 %collective-permute-start.4 = (bf16[1024,1024]{1,0:T(8,128)(2,1)}, bf16[1024,1024]{1,0:T(8,128)(2,1)}, u32[]{:S(2)}, u32[]{:S(2)}) collective-permute-start(bf16[1024,1024]{1,0:T(8,128)(2,1)} %get-tuple-element.9), channel_id=1, source_target_pairs={{1,0},{2,1},{3,2},{0,3},{5,4},{6,5},{7,6},{4,7}} | collective-permute-start | bytes 6291464 | tf_op jit(solution)/shard_map/ppermute | solution.py:150
  13.2 107.9 %collective-permute-start = (bf16[512,1024]{1,0:T(8,128)(2,1)}, bf16[512,1024]{1,0:T(8,128)(2,1)}, u32[]{:S(2)}, u32[]{:S(2)}) collective-permute-start(bf16[512,1024]{1,0:T(8,128)(2,1)} %get-tuple-element.7), channel_id=1, source_target_pairs={{1,0},{2,1},{3,2},{0,3},{5,4},{6,5},{7,6},{4,7}} | collective-permute-start | bytes 3145736 | tf_op jit(solution)/shard_map/ppermute | solution.py:150
  51.3 106.8 %collective-permute-start.8 = (bf16[1536,1024]{1,0:T(8,128)(2,1)}, bf16[1536,1024]{1,0:T(8,128)(2,1)}, u32[]{:S(2)}, u32[]{:S(2)}) collective-permute-start(bf16[1536,1024]{1,0:T(8,128)(2,1)} %collective-permute-done.7.part_ref), channel_id=1, source_target_pairs={{1,0},{5,4}} | collective-permute-start | bytes 9437192 | tf_op jit(solution)/shard_map/ppermute | solution.py:150
  93.5 63.3 %collective-permute-start.10 = (bf16[1024,1024]{1,0:T(8,128)(2,1)}, bf16[1024,1024]{1,0:T(8,128)(2,1)}, u32[]{:S(2)}, u32[]{:S(2)}) collective-permute-start(bf16[1024,1024]{1,0:T(8,128)(2,1)} %get-tuple-element.8), channel_id=1, source_target_pairs={{3,1},{7,5}} | collective-permute-start | bytes 6291464 | tf_op jit(solution)/shard_map/ppermute | solution.py:150
  121.1 61.3 %collective-permute-start.6 = (bf16[1024,1024]{1,0:T(8,128)(2,1)}, bf16[1024,1024]{1,0:T(8,128)(2,1)}, u32[]{:S(2)}, u32[]{:S(2)}) collective-permute-start(bf16[1024,1024]{1,0:T(8,128)(2,1)} %get-tuple-element.9), channel_id=1, source_target_pairs={{3,1},{7,5}} | collective-permute-start | bytes 6291464 | tf_op jit(solution)/shard_map/ppermute | solution.py:150
  122.4 25.6 %collective-permute-start.12 = (bf16[512,1024]{1,0:T(8,128)(2,1)}, bf16[512,1024]{1,0:T(8,128)(2,1)}, u32[]{:S(2)}, u32[]{:S(2)}) collective-permute-start(bf16[512,1024]{1,0:T(8,128)(2,1)} %collective-permute-done.11.part_ref), channel_id=1, source_target_pairs={{1,0},{5,4}} | collective-permute-start | bytes 3145736 | tf_op jit(solution)/shard_map/ppermute | solution.py:150
  124.7 57.7 %collective-permute-start.5 = (bf16[1024,1024]{1,0:T(8,128)(2,1)}, bf16[1024,1024]{1,0:T(8,128)(2,1)}, u32[]{:S(2)}, u32[]{:S(2)}) collective-permute-start(bf16[1024,1024]{1,0:T(8,128)(2,1)} %collective-permute-done.4.part_ref), channel_id=1, source_target_pairs={{1,0},{5,4}} | collective-permute-start | bytes 6291464 | tf_op jit(solution)/shard_map/ppermute | solution.py:150
  147.9 24.6 %collective-permute-start.9 = (bf16[512,1024]{1,0:T(8,128)(2,1)}, bf16[512,1024]{1,0:T(8,128)(2,1)}, u32[]{:S(2)}, u32[]{:S(2)}) collective-permute-start(bf16[512,1024]{1,0:T(8,128)(2,1)} %get-tuple-element.6), channel_id=1, source_target_pairs={{3,1},{7,5}} | collective-permute-start | bytes 3145736 | tf_op jit(solution)/shard_map/ppermute | solution.py:150
  156.7 38.9 %collective-permute-start.3 = (bf16[256,1024]{1,0:T(8,128)(2,1)}, bf16[256,1024]{1,0:T(8,128)(2,1)}, u32[]{:S(2)}, u32[]{:S(2)}) collective-permute-start(bf16[256,1024]{1,0:T(8,128)(2,1)} %get-tuple-element.10), channel_id=1, source_target_pairs={{3,1},{7,5}} | collective-permute-start | bytes 1572872 | tf_op jit(solution)/shard_map/ppermute | solution.py:150
  158.1 42.8 %collective-permute-start.2 = (bf16[256,1024]{1,0:T(8,128)(2,1)}, bf16[256,1024]{1,0:T(8,128)(2,1)}, u32[]{:S(2)}, u32[]{:S(2)}) collective-permute-start(bf16[256,1024]{1,0:T(8,128)(2,1)} %get-tuple-element.11), channel_id=1, source_target_pairs={{3,1},{7,5}} | collective-permute-start | bytes 1572872 | tf_op jit(solution)/shard_map/ppermute | solution.py:150
  172.6 23.0 %collective-permute-start.1 = (bf16[512,1024]{1,0:T(8,128)(2,1)}, bf16[512,1024]{1,0:T(8,128)(2,1)}, u32[]{:S(2)}, u32[]{:S(2)}) collective-permute-start(bf16[512,1024]{1,0:T(8,128)(2,1)} %collective-permute-done.part_ref), channel_id=1, source_target_pairs={{1,0},{5,4}} | collective-permute-start | bytes 3145736 | tf_op jit(solution)/shard_map/ppermute | solution.py:150

commit v2 on v1

v2 whole, which is shorter than its diff:
```python
import jax
import jax.numpy as jnp
from jax import lax
from jax.experimental import pallas as pl
from jax.experimental.pallas import tpu as pltpu
from jax.sharding import PartitionSpec as P


TILE = 512
WIDE = 896
NEXT = [(1, 0), (2, 1), (3, 2), (0, 3)]
FAR = [(3, 1)]
PASS = [(1, 0)]
PARTS = [(0, 512), (512, 1536), (2048, 1024), (3072, 512)]
FARS = [(0, 1024), (1024, 1024), (2048, 640), (2688, 448), (3136, 256), (3392, 192)]
DEPTH = 3


def dot_t(x, y):
    return lax.dot_general(x, y, (((1,), (1,)), ((), ())), preferred_element_type=jnp.float32)


def tiles(ref, index, size):
    return ref[pl.ds(pl.multiple_of(index * size, size), size), :]


def stream(steps, buf, sem, value, place):
    def copy(s):
        return pltpu.make_async_copy(buf.at[lax.rem(s, DEPTH)], place(s), sem.at[lax.rem(s, DEPTH)])

    @pl.loop(0, steps)
    def _(s):
        @pl.when(s >= DEPTH)
        def _():
            copy(s - DEPTH).wait()

        buf[lax.rem(s, DEPTH)] = value(s)
        copy(s).start()

    for s in range(max(steps - DEPTH, 0), steps):
        copy(s).wait()


def load(src, dst, sem):
    copy = pltpu.make_async_copy(src, dst, sem)
    copy.start()
    copy.wait()


def call(kernel, rows, cols, depth, out, refs, scratch):
    made = isinstance(out, jax.ShapeDtypeStruct)
    args = [a for a, _ in refs] + ([] if made else [out])
    return pl.pallas_call(
        kernel,
        in_specs=[pl.BlockSpec(memory_space=space) for _, space in refs] + ([] if made else [pl.BlockSpec(memory_space=pl.ANY)]),
        out_specs=pl.BlockSpec(memory_space=pl.ANY),
        out_shape=jax.ShapeDtypeStruct(out.shape, out.dtype),
        input_output_aliases={} if made else {len(args) - 1: 0},
        scratch_shapes=[pltpu.SemaphoreType.DMA((DEPTH,)), pltpu.SemaphoreType.DMA, *scratch],
        cost_estimate=pl.CostEstimate(
            flops=2 * rows * cols * depth, bytes_accessed=4 * rows * cols + 2 * rows * depth, transcendentals=0
        ),
        compiler_params=pltpu.CompilerParams(vmem_limit_bytes=32 << 20),
    )(*args)


def diag(own):
    rows, depth = own.shape
    wide = rows // WIDE

    def kernel(own_ref, out_ref, sem, _, buf):
        stream(
            rows // TILE * wide, buf, sem,
            lambda s: dot_t(tiles(own_ref, s // wide, TILE), tiles(own_ref, lax.rem(s, wide), WIDE)),
            lambda s: out_ref.at[0, 0, pl.ds(s // wide * TILE, TILE), pl.ds(lax.rem(s, wide) * WIDE, WIDE)],
        )

    out = jax.ShapeDtypeStruct((1, 3, rows, rows), jnp.float32)
    scratch = [pltpu.VMEM((DEPTH, TILE, WIDE), jnp.float32)]
    return call(kernel, rows, rows, depth, out, [(own, pltpu.VMEM)], scratch)


def slot1(first, size, part, own, out):
    rows, depth = own.shape
    tall = size // TILE
    steps = tall * (rows // WIDE)

    def kernel(part_ref, own_ref, _, out_ref, sem, load_sem, held, buf, turned):
        p = lax.axis_index("row")
        load(part_ref, held, load_sem)

        @pl.when(p < 3)
        def _():
            stream(
                steps, buf, sem,
                lambda s: dot_t(tiles(held, lax.rem(s, tall), TILE), tiles(own_ref, s // tall, WIDE)),
                lambda s: out_ref.at[0, 1, pl.ds(first + lax.rem(s, tall) * TILE, TILE), pl.ds(s // tall * WIDE, WIDE)],
            )

        @pl.when(p == 3)
        def _():
            stream(
                steps, turned, sem,
                lambda s: dot_t(tiles(own_ref, s // tall, WIDE), tiles(held, lax.rem(s, tall), TILE)),
                lambda s: out_ref.at[0, 1, pl.ds(s // tall * WIDE, WIDE), pl.ds(first + lax.rem(s, tall) * TILE, TILE)],
            )

    scratch = [
        pltpu.VMEM((size, depth), jnp.bfloat16),
        pltpu.VMEM((DEPTH, TILE, WIDE), jnp.float32),
        pltpu.VMEM((DEPTH, WIDE, TILE), jnp.float32),
    ]
    return call(kernel, size, rows, depth, out, [(part, pl.ANY), (own, pltpu.VMEM)], scratch)


def slot2(first, size, passed, far, own, out):
    rows, depth = own.shape
    tall = -(-size // TILE)
    high = size // tall
    wide = WIDE if high > 256 else 2 * WIDE
    steps = tall * (rows // wide)
    near = []
    for (start, count), part in zip(PARTS, passed):
        low, end = max(first, start), min(first + size, start + count)
        if low < end:
            near.append((part, low - start, low - first, end - low))

    def kernel(*refs):
        near_refs, (far_ref, own_ref, _, out_ref, sem, load_sem, held, buf) = refs[:len(near)], refs[len(near):]
        p = lax.axis_index("row")

        def place(s):
            return out_ref.at[0, 2, pl.ds(first + lax.rem(s, tall) * high, high), pl.ds(s // tall * wide, wide)]

        @pl.when(p == 0)
        def _():
            for ref, (_, src, dst, count) in zip(near_refs, near):
                load(ref.at[pl.ds(src, count), :], held.at[pl.ds(dst, count), :], load_sem)

        @pl.when(p == 1)
        def _():
            load(far_ref, held, load_sem)

        @pl.when(p < 2)
        def _():
            stream(steps, buf, sem, lambda s: dot_t(tiles(held, lax.rem(s, tall), high), tiles(own_ref, s // tall, wide)), place)

        @pl.when(p >= 2)
        def _():
            stream(steps, buf, sem, lambda s: jnp.zeros((high, wide), jnp.float32), place)

    scratch = [pltpu.VMEM((size, depth), jnp.bfloat16), pltpu.VMEM((DEPTH, high, wide), jnp.float32)]
    refs = [(part, pl.ANY) for part, *_ in near] + [(far, pl.ANY), (own, pltpu.VMEM)]
    return call(kernel, size, rows, depth, out, refs, scratch)


def solution(mesh):
    assert mesh.shape["row"] == 4

    def send(a, pairs):
        return lax.ppermute(a, "row", pairs)

    def rows_of(a, chunk):
        return a[chunk[0]:chunk[0] + chunk[1]]

    def local(a):
        head = rows_of(a, PARTS[0])
        rest, head = lax.optimization_barrier((a, head))
        parts = [send(head, NEXT)]
        parts += [send(rows_of(rest, PARTS[k]), NEXT) for k in range(1, len(PARTS))]
        out = diag(a)
        passed = [send(part, PASS) for part in parts]
        later, _ = lax.optimization_barrier((a, parts[0]))
        far = [send(rows_of(later, chunk), FAR) for chunk in FARS]
        for k, chunk in enumerate(PARTS):
            out = slot1(*chunk, parts[k], a, out)
        for j, chunk in enumerate(FARS):
            out = slot2(*chunk, passed, far[j], a, out)
        return out

    return jax.shard_map(
        local, mesh=mesh, in_specs=(P(("mat", "row"), None),), out_specs=P(("mat", "row"), None, None, None), check_vma=False
    )
```

time: 207 us -> 204 us (0.986)
  the two profiles are of different devices: /device:TPU:1 before, /device:TPU:0 now
where the time goes in v2:
time: 204 us; the launch traced here: 202 us
  Pallas kernels  139 us (68%)
  waiting for transfers between devices  31.2 us (15%)
  starting transfers between devices  19.3 us (9%)
  local copies, waits for them, and re-layouts  12.8 us (6%)
    pallas_call x11, Pallas kernels, call(): pl.pallas_call(kernel, in_specs=[pl.BlockSpec(memory_space=space) for _,...  139 us
    ppermute x14, waiting for transfers between devices, send(): return lax.ppermute(a, 'row', pairs)  31.2 us
    ppermute x14, starting transfers between devices, send(): return lax.ppermute(a, 'row', pairs)  19.3 us
    slice x9, local copies, waits for them, and re-layouts, rows_of(): return a[chunk[0]:chunk[0] + chunk[1]]  12.8 us
  transfers between devices with their start and end apart: 14, of which 1 were waited for; matrix products, arithmetic and copies ran while one was open for 4% of the time, Pallas kernels for 66%

profile of v2, /device:TPU:0, one launch (start us, length us, event | category | flops | bytes accessed | tf_op | source)
XLA Modules:
  0.0 202.3 jit_solution(10100968084193366475)
XLA Ops:
  0.0 0.0 copy-start
  0.0 1.4 slice.30
  1.4 2.5 %slice.37 = bf16[1536,1024]{1,0:T(8,128)(2,1)S(1)} slice(bf16[3584,1024]{1,0:T(8,128)(2,1)} %refs_2_.7), slice={[512:2048], [0:1024]} | slice | bytes 6291456 | tf_op jit(solution)/shard_map/slice | solution.py:164
  3.9 2.8 %collective-permute-start.9 = (bf16[1536,1024]{1,0:T(8,128)(2,1)S(1)}, bf16[1536,1024]{1,0:T(8,128)(2,1)}, u32[]{:S(2)}, u32[]{:S(2)}) collective-permute-start(bf16[1536,1024]{1,0:T(8,128)(2,1)S(1)} %slice.37), channel_id=1, source_target_pairs={{1,0},{2,1},{3,2},{0,3},{5,4},{6,5},{7,6},{4,7}} | collective-permute-start | bytes 9437192 | tf_op jit(solution)/shard_map/ppermute | solution.py:161
  6.7 0.7 collective-permute-start.2
  7.4 0.0 copy-done
  7.4 1.5 slice.34
  8.9 0.0 collective-permute-start.5
  8.9 1.0 slice.31
  10.0 0.4 collective-permute-start
  10.4 31.1 %collective-permute-done.9.part_ref = bf16[1536,1024]{1,0:T(8,128)(2,1)} collective-permute-done((bf16[1536,1024]{1,0:T(8,128)(2,1)S(1)}, bf16[1536,1024]{1,0:T(8,128)(2,1)}, u32[]{:S(2)}, u32[]{:S(2)}) %collective-permute-start.9) | collective-permute-done | bytes 3145760 | tf_op jit(solution)/shard_map/ppermute | solution.py:161
  41.5 1.3 collective-permute-start.10
  42.8 37.4 %shard_map.17._ = f32[1,3,3584,3584]{3,2,1,0:T(8,128)} custom-call(bf16[3584,1024]{1,0:T(8,128)(2,1)S(1)} %copy-done), custom_call_target="tpu_custom_call" | custom-call | flops 26306674688 | bytes 58720256 | tf_op jit(solution)/shard_map/pallas_call | solution.py:53
  80.2 0.0 collective-permute-done.2.part_ref
  80.2 1.2 slice.36
  81.3 1.0 slice.35
  82.3 0.9 slice.33
  83.2 0.8 slice.32
  84.0 2.5 %fusion = (bf16[1024,1024]{1,0:T(8,128)(2,1)}, bf16[1024,1024]{1,0:T(8,128)(2,1)}) fusion(bf16[3584,1024]{1,0:T(8,128)(2,1)S(1)} %copy-done), kind=kLoop, calls=%fused_computation | loop fusion | bytes 8388608 | tf_op jit(solution)/shard_map/slice | solution.py:164
  86.5 2.0 collective-permute-start.13
  88.5 2.0 collective-permute-start.11
  90.4 7.6 %shard_map.18._ = f32[1,3,3584,3584]{3,2,1,0:T(8,128)} custom-call(bf16[512,1024]{1,0:T(8,128)(2,1)} %collective-permute-done.2.part_ref, bf16[3584,1024]{1,0:T(8,128)(2,1)S(1)} %copy-done, f32[1,3,3584,3584]{3,2,1,0:T(8,128)} %shard_map.17._), custom_call_target="tpu_custom_call", output_to_operand_aliasing={{}: (2, {})} | custom-call | flops 3758096384 | bytes 8388608 | tf_op jit(solution)/shard_map/pallas_call | solution.py:53
  98.1 18.8 %shard_map.19._ = f32[1,3,3584,3584]{3,2,1,0:T(8,128)} custom-call(bf16[1536,1024]{1,0:T(8,128)(2,1)} %collective-permute-done.9.part_ref, bf16[3584,1024]{1,0:T(8,128)(2,1)S(1)} %copy-done, f32[1,3,3584,3584]{3,2,1,0:T(8,128)} %shard_map.18._), custom_call_target="tpu_custom_call", output_to_operand_aliasing={{}: (2, {})} | custom-call | flops 11274289152 | bytes 25165824 | tf_op jit(solution)/shard_map/pallas_call | solution.py:53
  116.8 0.0 collective-permute-done.part_ref
  116.9 1.3 collective-permute-start.12
  118.2 0.0 collective-permute-done.5.part_ref
  118.2 1.3 collective-permute-start.6
  119.5 13.2 %shard_map.20._ = f32[1,3,3584,3584]{3,2,1,0:T(8,128)} custom-call(bf16[1024,1024]{1,0:T(8,128)(2,1)} %collective-permute-done.5.part_ref, bf16[3584,1024]{1,0:T(8,128)(2,1)S(1)} %copy-done, f32[1,3,3584,3584]{3,2,1,0:T(8,128)} %shard_map.19._), custom_call_target="tpu_custom_call", output_to_operand_aliasing={{}: (2, {})} | custom-call | flops 7516192768 | bytes 16777216 | tf_op jit(solution)/shard_map/pallas_call | solution.py:53
  132.7 7.6 %shard_map.21.refs_4_ = f32[1,3,3584,3584]{3,2,1,0:T(8,128)} custom-call(bf16[512,1024]{1,0:T(8,128)(2,1)} %collective-permute-done.part_ref, bf16[3584,1024]{1,0:T(8,128)(2,1)S(1)} %copy-done, f32[1,3,3584,3584]{3,2,1,0:T(8,128)} %shard_map.20._), custom_call_target="tpu_custom_call", output_to_operand_aliasing={{}: (2, {})} | custom-call | flops 3758096384 | bytes 8388608 | tf_op jit(solution)/shard_map/pallas_call | solution.py:53
  140.3 0.0 collective-permute-done.12.refs_0_
  140.3 1.7 collective-permute-start.8
  142.1 0.0 collective-permute-done.13.refs_2_
  142.1 1.6 collective-permute-start.7
  143.7 0.0 collective-permute-done.10.refs_1_.refs_0_
  143.7 1.5 collective-permute-start.4
  145.1 14.1 %shard_map.22.refs_3_ = f32[1,3,3584,3584]{3,2,1,0:T(8,128)} custom-call(bf16[512,1024]{1,0:T(8,128)(2,1)} %collective-permute-done.12.refs_0_, bf16[1536,1024]{1,0:T(8,128)(2,1)} %collective-permute-done.10.refs_1_.refs_0_, bf16[1024,1024]{1,0:T(8,128)(2,1)} %collective-permute-done.13.refs_2_, ...), custom_call_target="tpu_custom_call", output_to_operand_aliasing={{}: (4, {})} | custom-call | flops 7516192768 | bytes 16777216 | tf_op jit(solution)/shard_map/pallas_call | solution.py:53
  159.2 0.0 collective-permute-done.11.refs_1_
  159.2 1.5 collective-permute-start.1
  160.7 13.2 %shard_map.23.refs_3_ = f32[1,3,3584,3584]{3,2,1,0:T(8,128)} custom-call(bf16[1536,1024]{1,0:T(8,128)(2,1)} %collective-permute-done.10.refs_1_.refs_0_, bf16[1024,1024]{1,0:T(8,128)(2,1)} %collective-permute-done.11.refs_1_, bf16[3584,1024]{1,0:T(8,128)(2,1)S(1)} %copy-done, f32[1,3,3584,3584]{3,2,1,0:T(8,128)} %shard_map.22.refs_3_), custom_call_target="tpu_custom_call", output_to_operand_aliasing={{}: (3, {})} | custom-call | flops 7516192768 | bytes 16777216 | tf_op jit(solution)/shard_map/pallas_call | solution.py:53
  173.9 0.0 collective-permute-done.8.refs_1_
  173.9 1.4 collective-permute-start.3
  175.3 0.0 collective-permute-done.6.refs_0_
  175.3 9.4 %shard_map.24.refs_4_ = f32[1,3,3584,3584]{3,2,1,0:T(8,128)} custom-call(bf16[1024,1024]{1,0:T(8,128)(2,1)} %collective-permute-done.6.refs_0_, bf16[640,1024]{1,0:T(8,128)(2,1)} %collective-permute-done.8.refs_1_, bf16[3584,1024]{1,0:T(8,128)(2,1)S(1)} %copy-done, f32[1,3,3584,3584]{3,2,1,0:T(8,128)} %shard_map.23.refs_3_), custom_call_target="tpu_custom_call", output_to_operand_aliasing={{}: (3, {})} | custom-call | flops 4697620480 | bytes 10485760 | tf_op jit(solution)/shard_map/pallas_call | solution.py:53
  184.8 0.0 collective-permute-done.7.refs_2_
  184.8 0.0 collective-permute-done.1.refs_1_.refs_0_
  184.8 7.8 %shard_map.25.refs_3_ = f32[1,3,3584,3584]{3,2,1,0:T(8,128)} custom-call(bf16[1024,1024]{1,0:T(8,128)(2,1)} %collective-permute-done.6.refs_0_, bf16[512,1024]{1,0:T(8,128)(2,1)} %collective-permute-done.1.refs_1_.refs_0_, bf16[448,1024]{1,0:T(8,128)(2,1)} %collective-permute-done.7.refs_2_, ...), custom_call_target="tpu_custom_call", output_to_operand_aliasing={{}: (4, {})} | custom-call | flops 3288334336 | bytes 7340032 | tf_op jit(solution)/shard_map/pallas_call | solution.py:53
  192.7 0.0 collective-permute-done.4.refs_1_
  192.7 4.6 %shard_map.26.refs_3_ = f32[1,3,3584,3584]{3,2,1,0:T(8,128)} custom-call(bf16[512,1024]{1,0:T(8,128)(2,1)} %collective-permute-done.1.refs_1_.refs_0_, bf16[256,1024]{1,0:T(8,128)(2,1)} %collective-permute-done.4.refs_1_, bf16[3584,1024]{1,0:T(8,128)(2,1)S(1)} %copy-done, f32[1,3,3584,3584]{3,2,1,0:T(8,128)} %shard_map.25.refs_3_), custom_call_target="tpu_custom_call", output_to_operand_aliasing={{}: (3, {})} | custom-call | flops 1879048192 | bytes 4194304 | tf_op jit(solution)/shard_map/pallas_call | solution.py:53
  197.3 0.0 collective-permute-done.3.refs_1_
  197.3 4.8 %shard_map.27 = f32[1,3,3584,3584]{3,2,1,0:T(8,128)} custom-call(bf16[512,1024]{1,0:T(8,128)(2,1)} %collective-permute-done.1.refs_1_.refs_0_, bf16[192,1024]{1,0:T(8,128)(2,1)} %collective-permute-done.3.refs_1_, bf16[3584,1024]{1,0:T(8,128)(2,1)S(1)} %copy-done, f32[1,3,3584,3584]{3,2,1,0:T(8,128)} %shard_map.26.refs_3_), custom_call_target="tpu_custom_call", output_to_operand_aliasing={{}: (3, {})} | custom-call | flops 1409286144 | bytes 3145728 | tf_op jit(solution)/shard_map/pallas_call | solution.py:53
Async XLA Ops:
  0.0 7.4 %copy-start = (bf16[3584,1024]{1,0:T(8,128)(2,1)S(1)}, bf16[3584,1024]{1,0:T(8,128)(2,1)}, u32[]{:S(2)}) copy-start(bf16[3584,1024]{1,0:T(8,128)(2,1)} %refs_2_.7) | copy-start | bytes 22020100
  3.9 37.6 %collective-permute-start.9 = (bf16[1536,1024]{1,0:T(8,128)(2,1)S(1)}, bf16[1536,1024]{1,0:T(8,128)(2,1)}, u32[]{:S(2)}, u32[]{:S(2)}) collective-permute-start(bf16[1536,1024]{1,0:T(8,128)(2,1)S(1)} %slice.37), channel_id=1, source_target_pairs={{1,0},{2,1},{3,2},{0,3},{5,4},{6,5},{7,6},{4,7}} | collective-permute-start | bytes 9437192 | tf_op jit(solution)/shard_map/ppermute | solution.py:161
  6.7 73.5 %collective-permute-start.2 = (bf16[512,1024]{1,0:T(8,128)(2,1)S(1)}, bf16[512,1024]{1,0:T(8,128)(2,1)}, u32[]{:S(2)}, u32[]{:S(2)}) collective-permute-start(bf16[512,1024]{1,0:T(8,128)(2,1)S(1)} %slice.30), channel_id=1, source_target_pairs={{1,0},{2,1},{3,2},{0,3},{5,4},{6,5},{7,6},{4,7}} | collective-permute-start | bytes 3145736 | tf_op jit(solution)/shard_map/ppermute | solution.py:161
  8.9 109.3 %collective-permute-start.5 = (bf16[1024,1024]{1,0:T(8,128)(2,1)}, bf16[1024,1024]{1,0:T(8,128)(2,1)}, u32[]{:S(2)}, u32[]{:S(2)}) collective-permute-start(bf16[1024,1024]{1,0:T(8,128)(2,1)} %slice.34), channel_id=1, source_target_pairs={{1,0},{2,1},{3,2},{0,3},{5,4},{6,5},{7,6},{4,7}} | collective-permute-start | bytes 6291464 | tf_op jit(solution)/shard_map/ppermute | solution.py:161
  10.0 106.9 %collective-permute-start = (bf16[512,1024]{1,0:T(8,128)(2,1)}, bf16[512,1024]{1,0:T(8,128)(2,1)}, u32[]{:S(2)}, u32[]{:S(2)}) collective-permute-start(bf16[512,1024]{1,0:T(8,128)(2,1)} %slice.31), channel_id=1, source_target_pairs={{1,0},{2,1},{3,2},{0,3},{5,4},{6,5},{7,6},{4,7}} | collective-permute-start | bytes 3145736 | tf_op jit(solution)/shard_map/ppermute | solution.py:161
  41.5 102.2 %collective-permute-start.10 = (bf16[1536,1024]{1,0:T(8,128)(2,1)}, bf16[1536,1024]{1,0:T(8,128)(2,1)}, u32[]{:S(2)}, u32[]{:S(2)}) collective-permute-start(bf16[1536,1024]{1,0:T(8,128)(2,1)} %collective-permute-done.9.part_ref), channel_id=1, source_target_pairs={{1,0},{5,4}} | collective-permute-start | bytes 9437192 | tf_op jit(solution)/shard_map/ppermute | solution.py:161
  86.5 55.6 %collective-permute-start.13 = (bf16[1024,1024]{1,0:T(8,128)(2,1)}, bf16[1024,1024]{1,0:T(8,128)(2,1)}, u32[]{:S(2)}, u32[]{:S(2)}) collective-permute-start(bf16[1024,1024]{1,0:T(8,128)(2,1)} %get-tuple-element.11), channel_id=1, source_target_pairs={{3,1},{7,5}} | collective-permute-start | bytes 6291464 | tf_op jit(solution)/shard_map/ppermute | solution.py:161
  88.5 70.7 %collective-permute-start.11 = (bf16[1024,1024]{1,0:T(8,128)(2,1)}, bf16[1024,1024]{1,0:T(8,128)(2,1)}, u32[]{:S(2)}, u32[]{:S(2)}) collective-permute-start(bf16[1024,1024]{1,0:T(8,128)(2,1)} %get-tuple-element.12), channel_id=1, source_target_pairs={{3,1},{7,5}} | collective-permute-start | bytes 6291464 | tf_op jit(solution)/shard_map/ppermute | solution.py:161
  116.9 23.5 %collective-permute-start.12 = (bf16[512,1024]{1,0:T(8,128)(2,1)}, bf16[512,1024]{1,0:T(8,128)(2,1)}, u32[]{:S(2)}, u32[]{:S(2)}) collective-permute-start(bf16[512,1024]{1,0:T(8,128)(2,1)} %collective-permute-done.2.part_ref), channel_id=1, source_target_pairs={{1,0},{5,4}} | collective-permute-start | bytes 3145736 | tf_op jit(solution)/shard_map/ppermute | solution.py:161
  118.2 57.2 %collective-permute-start.6 = (bf16[1024,1024]{1,0:T(8,128)(2,1)}, bf16[1024,1024]{1,0:T(8,128)(2,1)}, u32[]{:S(2)}, u32[]{:S(2)}) collective-permute-start(bf16[1024,1024]{1,0:T(8,128)(2,1)} %collective-permute-done.5.part_ref), channel_id=1, source_target_pairs={{1,0},{5,4}} | collective-permute-start | bytes 6291464 | tf_op jit(solution)/shard_map/ppermute | solution.py:161
  140.3 33.6 %collective-permute-start.8 = (bf16[640,1024]{1,0:T(8,128)(2,1)}, bf16[640,1024]{1,0:T(8,128)(2,1)}, u32[]{:S(2)}, u32[]{:S(2)}) collective-permute-start(bf16[640,1024]{1,0:T(8,128)(2,1)} %slice.36), channel_id=1, source_target_pairs={{3,1},{7,5}} | collective-permute-start | bytes 3932168 | tf_op jit(solution)/shard_map/ppermute | solution.py:161
  142.1 42.7 %collective-permute-start.7 = (bf16[448,1024]{1,0:T(8,128)(2,1)}, bf16[448,1024]{1,0:T(8,128)(2,1)}, u32[]{:S(2)}, u32[]{:S(2)}) collective-permute-start(bf16[448,1024]{1,0:T(8,128)(2,1)} %slice.35), channel_id=1, source_target_pairs={{3,1},{7,5}} | collective-permute-start | bytes 2752520 | tf_op jit(solution)/shard_map/ppermute | solution.py:161
  143.7 49.0 %collective-permute-start.4 = (bf16[256,1024]{1,0:T(8,128)(2,1)}, bf16[256,1024]{1,0:T(8,128)(2,1)}, u32[]{:S(2)}, u32[]{:S(2)}) collective-permute-start(bf16[256,1024]{1,0:T(8,128)(2,1)} %slice.33), channel_id=1, source_target_pairs={{3,1},{7,5}} | collective-permute-start | bytes 1572872 | tf_op jit(solution)/shard_map/ppermute | solution.py:161
  159.2 25.6 %collective-permute-start.1 = (bf16[512,1024]{1,0:T(8,128)(2,1)}, bf16[512,1024]{1,0:T(8,128)(2,1)}, u32[]{:S(2)}, u32[]{:S(2)}) collective-permute-start(bf16[512,1024]{1,0:T(8,128)(2,1)} %collective-permute-done.part_ref), channel_id=1, source_target_pairs={{1,0},{5,4}} | collective-permute-start | bytes 3145736 | tf_op jit(solution)/shard_map/ppermute | solution.py:161
  173.9 23.4 %collective-permute-start.3 = (bf16[192,1024]{1,0:T(8,128)(2,1)}, bf16[192,1024]{1,0:T(8,128)(2,1)}, u32[]{:S(2)}, u32[]{:S(2)}) collective-permute-start(bf16[192,1024]{1,0:T(8,128)(2,1)} %slice.32), channel_id=1, source_target_pairs={{3,1},{7,5}} | collective-permute-start | bytes 1179656 | tf_op jit(solution)/shard_map/ppermute | solution.py:161

commit v3 on v2

--- a/solution.py
+++ b/solution.py
@@ -6,14 +6,16 @@
 from jax.sharding import PartitionSpec as P
 
 
-TILE = 512
-WIDE = 896
+WIDE = 512
+HIGH = 1792
 NEXT = [(1, 0), (2, 1), (3, 2), (0, 3)]
 FAR = [(3, 1)]
 PASS = [(1, 0)]
 PARTS = [(0, 512), (512, 1536), (2048, 1024), (3072, 512)]
-FARS = [(0, 1024), (1024, 1024), (2048, 640), (2688, 448), (3136, 256), (3392, 192)]
+FARS = [(0, 1024), (1024, 1024), (2048, 640), (2688, 384), (3072, 256), (3328, 256)]
 DEPTH = 3
+FEW = 384
+PIECES = [(0, 1536), (1536, 1536), (3072, 512)]
 
 
 def dot_t(x, y):
@@ -70,55 +72,45 @@
 
     def kernel(own_ref, out_ref, sem, _, buf):
         stream(
-            rows // TILE * wide, buf, sem,
-            lambda s: dot_t(tiles(own_ref, s // wide, TILE), tiles(own_ref, lax.rem(s, wide), WIDE)),
-            lambda s: out_ref.at[0, 0, pl.ds(s // wide * TILE, TILE), pl.ds(lax.rem(s, wide) * WIDE, WIDE)],
+            rows // HIGH * wide, buf, sem,
+            lambda s: dot_t(tiles(own_ref, s // wide, HIGH), tiles(own_ref, lax.rem(s, wide), WIDE)),
+            lambda s: out_ref.at[0, 0, pl.ds(s // wide * HIGH, HIGH), pl.ds(lax.rem(s, wide) * WIDE, WIDE)],
         )
 
     out = jax.ShapeDtypeStruct((1, 3, rows, rows), jnp.float32)
-    scratch = [pltpu.VMEM((DEPTH, TILE, WIDE), jnp.float32)]
-    return call(kernel, rows, rows, depth, out, [(own, pltpu.VMEM)], scratch)
+    return call(kernel, rows, rows, depth, out, [(own, pltpu.VMEM)], [pltpu.VMEM((DEPTH, HIGH, WIDE), jnp.float32)])
 
 
 def slot1(first, size, part, own, out):
     rows, depth = own.shape
-    tall = size // TILE
-    steps = tall * (rows // WIDE)
-
-    def kernel(part_ref, own_ref, _, out_ref, sem, load_sem, held, buf, turned):
+    tall = size // WIDE
+
+    def kernel(part_ref, own_ref, _, out_ref, sem, load_sem, held, buf):
         p = lax.axis_index("row")
         load(part_ref, held, load_sem)
 
         @pl.when(p < 3)
         def _():
             stream(
-                steps, buf, sem,
-                lambda s: dot_t(tiles(held, lax.rem(s, tall), TILE), tiles(own_ref, s // tall, WIDE)),
-                lambda s: out_ref.at[0, 1, pl.ds(first + lax.rem(s, tall) * TILE, TILE), pl.ds(s // tall * WIDE, WIDE)],
+                rows // WIDE, buf.at[:, :size], sem,
+                lambda s: dot_t(held[...], tiles(own_ref, s, WIDE)),
+                lambda s: out_ref.at[0, 1, pl.ds(first, size), pl.ds(s * WIDE, WIDE)],
             )
 
         @pl.when(p == 3)
         def _():
             stream(
-                steps, turned, sem,
-                lambda s: dot_t(tiles(own_ref, s // tall, WIDE), tiles(held, lax.rem(s, tall), TILE)),
-                lambda s: out_ref.at[0, 1, pl.ds(s // tall * WIDE, WIDE), pl.ds(first + lax.rem(s, tall) * TILE, TILE)],
+                rows // HIGH * tall, buf, sem,
+                lambda s: dot_t(tiles(own_ref, s // tall, HIGH), tiles(held, lax.rem(s, tall), WIDE)),
+                lambda s: out_ref.at[0, 1, pl.ds(s // tall * HIGH, HIGH), pl.ds(first + lax.rem(s, tall) * WIDE, WIDE)],
             )
 
-    scratch = [
-        pltpu.VMEM((size, depth), jnp.bfloat16),
-        pltpu.VMEM((DEPTH, TILE, WIDE), jnp.float32),
-        pltpu.VMEM((DEPTH, WIDE, TILE), jnp.float32),
-    ]
+    scratch = [pltpu.VMEM((size, depth), jnp.bfloat16), pltpu.VMEM((DEPTH, HIGH, WIDE), jnp.float32)]
     return call(kernel, size, rows, depth, out, [(part, pl.ANY), (own, pltpu.VMEM)], scratch)
 
 
 def slot2(first, size, passed, far, own, out):
     rows, depth = own.shape
-    tall = -(-size // TILE)
-    high = size // tall
-    wide = WIDE if high > 256 else 2 * WIDE
-    steps = tall * (rows // wide)
     near = []
     for (start, count), part in zip(PARTS, passed):
         low, end = max(first, start), min(first + size, start + count)
@@ -129,8 +121,8 @@
         near_refs, (far_ref, own_ref, _, out_ref, sem, load_sem, held, buf) = refs[:len(near)], refs[len(near):]
         p = lax.axis_index("row")
 
-        def place(s):
-            return out_ref.at[0, 2, pl.ds(first + lax.rem(s, tall) * high, high), pl.ds(s // tall * wide, wide)]
+        def place(start, wide):
+            return out_ref.at[0, 2, pl.ds(first, size), pl.ds(start, wide)]
 
         @pl.when(p == 0)
         def _():
@@ -141,15 +133,41 @@
         def _():
             load(far_ref, held, load_sem)
 
-        @pl.when(p < 2)
-        def _():
-            stream(steps, buf, sem, lambda s: dot_t(tiles(held, lax.rem(s, tall), high), tiles(own_ref, s // tall, wide)), place)
+        def zeros(wide):
+            stream(
+                rows // wide, buf.at[:, :, :wide], sem,
+                lambda s: jnp.zeros((size, wide), jnp.float32),
+                lambda s: place(s * wide, wide),
+            )
+
+        if size > FEW:
+
+            @pl.when(p < 2)
+            def _():
+                stream(
+                    rows // WIDE, buf, sem,
+                    lambda s: dot_t(held[...], tiles(own_ref, s, WIDE)),
+                    lambda s: place(s * WIDE, WIDE),
+                )
+
+        else:
+
+            @pl.when(p < 2)
+            def _():
+                copies = []
+                for k, (start, wide) in enumerate(PIECES):
+                    buf[k, :, :wide] = dot_t(held[...], own_ref[start:start + wide, :])
+                    copies.append(pltpu.make_async_copy(buf.at[k, :, :wide], place(start, wide), sem.at[k]))
+                    copies[-1].start()
+                for copy in copies:
+                    copy.wait()
 
         @pl.when(p >= 2)
         def _():
-            stream(steps, buf, sem, lambda s: jnp.zeros((high, wide), jnp.float32), place)
-
-    scratch = [pltpu.VMEM((size, depth), jnp.bfloat16), pltpu.VMEM((DEPTH, high, wide), jnp.float32)]
+            zeros(WIDE)
+
+    width = WIDE if size > FEW else PIECES[0][1]
+    scratch = [pltpu.VMEM((size, depth), jnp.bfloat16), pltpu.VMEM((DEPTH, size, width), jnp.float32)]
     refs = [(part, pl.ANY) for part, *_ in near] + [(far, pl.ANY), (own, pltpu.VMEM)]
     return call(kernel, size, rows, depth, out, refs, scratch)
 

time: 204 us -> 188 us (0.922)
  Pallas kernels: 139 us -> 122 us
    pallas_call x11, Pallas kernels: 139 us -> 122 us  [call(): pl.pallas_call(kernel, in_specs=[pl.BlockSpec(memory_space=space) for _,...]
    slice x9 -> x8, local copies, waits for them, and re-layouts: 12.8 us -> 12.2 us  [rows_of(): return a[chunk[0]:chunk[0] + chunk[1]]]
  transfers between devices with their start and end apart: 14 -> 14, of which waited for: 1 -> 1; matrix products, arithmetic and copies ran while one was open for 4% -> 4% of each run, Pallas kernels for 66% -> 64%
where the time goes in v3:
time: 188 us; the launch traced here: 185 us
  Pallas kernels  122 us (65%)
  waiting for transfers between devices  31.2 us (17%)
  starting transfers between devices  19.2 us (10%)
  local copies, waits for them, and re-layouts  12.2 us (6%)
    pallas_call x11, Pallas kernels, call(): pl.pallas_call(kernel, in_specs=[pl.BlockSpec(memory_space=space) for _,...  122 us
    ppermute x14, waiting for transfers between devices, send(): return lax.ppermute(a, 'row', pairs)  31.2 us
    ppermute x14, starting transfers between devices, send(): return lax.ppermute(a, 'row', pairs)  19.2 us
    slice x8, local copies, waits for them, and re-layouts, rows_of(): return a[chunk[0]:chunk[0] + chunk[1]]  12.2 us
  transfers between devices with their start and end apart: 14, of which 1 were waited for; matrix products, arithmetic and copies ran while one was open for 4% of the time, Pallas kernels for 64%

profile of v3, /device:TPU:0, one launch (start us, length us, event | category | flops | bytes accessed | tf_op | source)
XLA Modules:
  0.0 185.4 jit_solution(1062647144732704531)
XLA Ops:
  0.0 0.0 copy-start
  0.0 1.4 slice.30
  1.4 2.5 %slice.37 = bf16[1536,1024]{1,0:T(8,128)(2,1)S(1)} slice(bf16[3584,1024]{1,0:T(8,128)(2,1)} %refs_2_.9), slice={[512:2048], [0:1024]} | slice | bytes 6291456 | tf_op jit(solution)/shard_map/slice | solution.py:182
  3.9 2.8 %collective-permute-start.9 = (bf16[1536,1024]{1,0:T(8,128)(2,1)S(1)}, bf16[1536,1024]{1,0:T(8,128)(2,1)}, u32[]{:S(2)}, u32[]{:S(2)}) collective-permute-start(bf16[1536,1024]{1,0:T(8,128)(2,1)S(1)} %slice.37), channel_id=1, source_target_pairs={{1,0},{2,1},{3,2},{0,3},{5,4},{6,5},{7,6},{4,7}} | collective-permute-start | bytes 9437192 | tf_op jit(solution)/shard_map/ppermute | solution.py:179
  6.7 0.7 collective-permute-start.2
  7.4 0.0 copy-done
  7.4 1.5 slice.34
  8.9 0.0 collective-permute-start.5
  8.9 1.0 slice.31
  10.0 0.4 collective-permute-start
  10.3 31.1 %collective-permute-done.9.part_ref = bf16[1536,1024]{1,0:T(8,128)(2,1)} collective-permute-done((bf16[1536,1024]{1,0:T(8,128)(2,1)S(1)}, bf16[1536,1024]{1,0:T(8,128)(2,1)}, u32[]{:S(2)}, u32[]{:S(2)}) %collective-permute-start.9) | collective-permute-done | bytes 3145760 | tf_op jit(solution)/shard_map/ppermute | solution.py:179
  41.5 1.3 collective-permute-start.10
  42.8 31.7 %shard_map.17._ = f32[1,3,3584,3584]{3,2,1,0:T(8,128)} custom-call(bf16[3584,1024]{1,0:T(8,128)(2,1)S(1)} %copy-done), custom_call_target="tpu_custom_call" | custom-call | flops 26306674688 | bytes 58720256 | tf_op jit(solution)/shard_map/pallas_call | solution.py:55
  74.5 0.0 collective-permute-done.2.part_ref
  74.5 1.2 slice.36
  75.7 0.9 slice.35
  76.6 2.5 %fusion = (bf16[1024,1024]{1,0:T(8,128)(2,1)}, bf16[1024,1024]{1,0:T(8,128)(2,1)}) fusion(bf16[3584,1024]{1,0:T(8,128)(2,1)S(1)} %copy-done), kind=kLoop, calls=%fused_computation | loop fusion | bytes 8388608 | tf_op jit(solution)/shard_map/slice | solution.py:182
  79.1 2.0 %collective-permute-start.13 = (bf16[1024,1024]{1,0:T(8,128)(2,1)}, bf16[1024,1024]{1,0:T(8,128)(2,1)}, u32[]{:S(2)}, u32[]{:S(2)}) collective-permute-start(bf16[1024,1024]{1,0:T(8,128)(2,1)} %get-tuple-element.11), channel_id=1, source_target_pairs={{3,1},{7,5}} | collective-permute-start | bytes 6291464 | tf_op jit(solution)/shard_map/ppermute | solution.py:179
  81.0 2.0 %collective-permute-start.11 = (bf16[1024,1024]{1,0:T(8,128)(2,1)}, bf16[1024,1024]{1,0:T(8,128)(2,1)}, u32[]{:S(2)}, u32[]{:S(2)}) collective-permute-start(bf16[1024,1024]{1,0:T(8,128)(2,1)} %get-tuple-element.12), channel_id=1, source_target_pairs={{3,1},{7,5}} | collective-permute-start | bytes 6291464 | tf_op jit(solution)/shard_map/ppermute | solution.py:179
  83.0 1.1 fusion.1
  84.2 7.5 %shard_map.18._ = f32[1,3,3584,3584]{3,2,1,0:T(8,128)} custom-call(bf16[512,1024]{1,0:T(8,128)(2,1)} %collective-permute-done.2.part_ref, bf16[3584,1024]{1,0:T(8,128)(2,1)S(1)} %copy-done, f32[1,3,3584,3584]{3,2,1,0:T(8,128)} %shard_map.17._), custom_call_target="tpu_custom_call", output_to_operand_aliasing={{}: (2, {})} | custom-call | flops 3758096384 | bytes 8388608 | tf_op jit(solution)/shard_map/pallas_call | solution.py:55
  91.6 16.5 %shard_map.19._ = f32[1,3,3584,3584]{3,2,1,0:T(8,128)} custom-call(bf16[1536,1024]{1,0:T(8,128)(2,1)} %collective-permute-done.9.part_ref, bf16[3584,1024]{1,0:T(8,128)(2,1)S(1)} %copy-done, f32[1,3,3584,3584]{3,2,1,0:T(8,128)} %shard_map.18._), custom_call_target="tpu_custom_call", output_to_operand_aliasing={{}: (2, {})} | custom-call | flops 11274289152 | bytes 25165824 | tf_op jit(solution)/shard_map/pallas_call | solution.py:55
  108.1 0.0 collective-permute-done.part_ref
  108.2 1.3 collective-permute-start.12
  109.5 0.0 collective-permute-done.5.part_ref
  109.5 1.3 collective-permute-start.6
  110.8 12.0 %shard_map.20._ = f32[1,3,3584,3584]{3,2,1,0:T(8,128)} custom-call(bf16[1024,1024]{1,0:T(8,128)(2,1)} %collective-permute-done.5.part_ref, bf16[3584,1024]{1,0:T(8,128)(2,1)S(1)} %copy-done, f32[1,3,3584,3584]{3,2,1,0:T(8,128)} %shard_map.19._), custom_call_target="tpu_custom_call", output_to_operand_aliasing={{}: (2, {})} | custom-call | flops 7516192768 | bytes 16777216 | tf_op jit(solution)/shard_map/pallas_call | solution.py:55
  122.7 7.5 %shard_map.21.refs_4_ = f32[1,3,3584,3584]{3,2,1,0:T(8,128)} custom-call(bf16[512,1024]{1,0:T(8,128)(2,1)} %collective-permute-done.part_ref, bf16[3584,1024]{1,0:T(8,128)(2,1)S(1)} %copy-done, f32[1,3,3584,3584]{3,2,1,0:T(8,128)} %shard_map.20._), custom_call_target="tpu_custom_call", output_to_operand_aliasing={{}: (2, {})} | custom-call | flops 3758096384 | bytes 8388608 | tf_op jit(solution)/shard_map/pallas_call | solution.py:55
  130.2 0.0 collective-permute-done.12.refs_0_
  130.2 1.7 collective-permute-start.8
  132.0 0.0 collective-permute-done.13.refs_2_
  132.0 1.6 collective-permute-start.7
  133.5 0.0 collective-permute-done.10.refs_1_.refs_0_
  133.5 1.5 collective-permute-start.4
  135.0 12.8 %shard_map.22.refs_3_ = f32[1,3,3584,3584]{3,2,1,0:T(8,128)} custom-call(bf16[512,1024]{1,0:T(8,128)(2,1)} %collective-permute-done.12.refs_0_, bf16[1536,1024]{1,0:T(8,128)(2,1)} %collective-permute-done.10.refs_1_.refs_0_, bf16[1024,1024]{1,0:T(8,128)(2,1)} %collective-permute-done.13.refs_2_, ...), custom_call_target="tpu_custom_call", output_to_operand_aliasing={{}: (4, {})} | custom-call | flops 7516192768 | bytes 16777216 | tf_op jit(solution)/shard_map/pallas_call | solution.py:55
  147.9 0.0 collective-permute-done.11.refs_1_
  147.9 1.3 collective-permute-start.1
  149.2 12.0 %shard_map.23.refs_3_ = f32[1,3,3584,3584]{3,2,1,0:T(8,128)} custom-call(bf16[1536,1024]{1,0:T(8,128)(2,1)} %collective-permute-done.10.refs_1_.refs_0_, bf16[1024,1024]{1,0:T(8,128)(2,1)} %collective-permute-done.11.refs_1_, bf16[3584,1024]{1,0:T(8,128)(2,1)S(1)} %copy-done, f32[1,3,3584,3584]{3,2,1,0:T(8,128)} %shard_map.22.refs_3_), custom_call_target="tpu_custom_call", output_to_operand_aliasing={{}: (3, {})} | custom-call | flops 7516192768 | bytes 16777216 | tf_op jit(solution)/shard_map/pallas_call | solution.py:55
  161.2 0.0 collective-permute-done.8.refs_1_
  161.2 1.5 collective-permute-start.3
  162.7 0.0 collective-permute-done.6.refs_0_
  162.7 8.6 %shard_map.24.refs_3_ = f32[1,3,3584,3584]{3,2,1,0:T(8,128)} custom-call(bf16[1024,1024]{1,0:T(8,128)(2,1)} %collective-permute-done.6.refs_0_, bf16[640,1024]{1,0:T(8,128)(2,1)} %collective-permute-done.8.refs_1_, bf16[3584,1024]{1,0:T(8,128)(2,1)S(1)} %copy-done, f32[1,3,3584,3584]{3,2,1,0:T(8,128)} %shard_map.23.refs_3_), custom_call_target="tpu_custom_call", output_to_operand_aliasing={{}: (3, {})} | custom-call | flops 4697620480 | bytes 10485760 | tf_op jit(solution)/shard_map/pallas_call | solution.py:55
  171.3 0.0 collective-permute-done.7.refs_1_
  171.3 5.5 %shard_map.25.refs_3_ = f32[1,3,3584,3584]{3,2,1,0:T(8,128)} custom-call(bf16[1024,1024]{1,0:T(8,128)(2,1)} %collective-permute-done.6.refs_0_, bf16[384,1024]{1,0:T(8,128)(2,1)} %collective-permute-done.7.refs_1_, bf16[3584,1024]{1,0:T(8,128)(2,1)S(1)} %copy-done, f32[1,3,3584,3584]{3,2,1,0:T(8,128)} %shard_map.24.refs_3_), custom_call_target="tpu_custom_call", output_to_operand_aliasing={{}: (3, {})} | custom-call | flops 2818572288 | bytes 6291456 | tf_op jit(solution)/shard_map/pallas_call | solution.py:55
  176.7 0.0 collective-permute-done.4.refs_1_
  176.7 0.0 collective-permute-done.1.refs_0_
  176.8 4.2 %shard_map.26.refs_3_ = f32[1,3,3584,3584]{3,2,1,0:T(8,128)} custom-call(bf16[512,1024]{1,0:T(8,128)(2,1)} %collective-permute-done.1.refs_0_, bf16[256,1024]{1,0:T(8,128)(2,1)} %collective-permute-done.4.refs_1_, bf16[3584,1024]{1,0:T(8,128)(2,1)S(1)} %copy-done, f32[1,3,3584,3584]{3,2,1,0:T(8,128)} %shard_map.25.refs_3_), custom_call_target="tpu_custom_call", output_to_operand_aliasing={{}: (3, {})} | custom-call | flops 1879048192 | bytes 4194304 | tf_op jit(solution)/shard_map/pallas_call | solution.py:55
  181.0 0.0 collective-permute-done.3.refs_1_
  181.0 4.2 %shard_map.27 = f32[1,3,3584,3584]{3,2,1,0:T(8,128)} custom-call(bf16[512,1024]{1,0:T(8,128)(2,1)} %collective-permute-done.1.refs_0_, bf16[256,1024]{1,0:T(8,128)(2,1)} %collective-permute-done.3.refs_1_, bf16[3584,1024]{1,0:T(8,128)(2,1)S(1)} %copy-done, f32[1,3,3584,3584]{3,2,1,0:T(8,128)} %shard_map.26.refs_3_), custom_call_target="tpu_custom_call", output_to_operand_aliasing={{}: (3, {})} | custom-call | flops 1879048192 | bytes 4194304 | tf_op jit(solution)/shard_map/pallas_call | solution.py:55
Async XLA Ops:
  0.0 7.4 %copy-start = (bf16[3584,1024]{1,0:T(8,128)(2,1)S(1)}, bf16[3584,1024]{1,0:T(8,128)(2,1)}, u32[]{:S(2)}) copy-start(bf16[3584,1024]{1,0:T(8,128)(2,1)} %refs_2_.9) | copy-start | bytes 22020100
  3.9 37.6 %collective-permute-start.9 = (bf16[1536,1024]{1,0:T(8,128)(2,1)S(1)}, bf16[1536,1024]{1,0:T(8,128)(2,1)}, u32[]{:S(2)}, u32[]{:S(2)}) collective-permute-start(bf16[1536,1024]{1,0:T(8,128)(2,1)S(1)} %slice.37), channel_id=1, source_target_pairs={{1,0},{2,1},{3,2},{0,3},{5,4},{6,5},{7,6},{4,7}} | collective-permute-start | bytes 9437192 | tf_op jit(solution)/shard_map/ppermute | solution.py:179
  6.7 67.8 %collective-permute-start.2 = (bf16[512,1024]{1,0:T(8,128)(2,1)S(1)}, bf16[512,1024]{1,0:T(8,128)(2,1)}, u32[]{:S(2)}, u32[]{:S(2)}) collective-permute-start(bf16[512,1024]{1,0:T(8,128)(2,1)S(1)} %slice.30), channel_id=1, source_target_pairs={{1,0},{2,1},{3,2},{0,3},{5,4},{6,5},{7,6},{4,7}} | collective-permute-start | bytes 3145736 | tf_op jit(solution)/shard_map/ppermute | solution.py:179
  8.9 100.6 %collective-permute-start.5 = (bf16[1024,1024]{1,0:T(8,128)(2,1)}, bf16[1024,1024]{1,0:T(8,128)(2,1)}, u32[]{:S(2)}, u32[]{:S(2)}) collective-permute-start(bf16[1024,1024]{1,0:T(8,128)(2,1)} %slice.34), channel_id=1, source_target_pairs={{1,0},{2,1},{3,2},{0,3},{5,4},{6,5},{7,6},{4,7}} | collective-permute-start | bytes 6291464 | tf_op jit(solution)/shard_map/ppermute | solution.py:179
  10.0 98.2 %collective-permute-start = (bf16[512,1024]{1,0:T(8,128)(2,1)}, bf16[512,1024]{1,0:T(8,128)(2,1)}, u32[]{:S(2)}, u32[]{:S(2)}) collective-permute-start(bf16[512,1024]{1,0:T(8,128)(2,1)} %slice.31), channel_id=1, source_target_pairs={{1,0},{2,1},{3,2},{0,3},{5,4},{6,5},{7,6},{4,7}} | collective-permute-start | bytes 3145736 | tf_op jit(solution)/shard_map/ppermute | solution.py:179
  41.5 92.1 %collective-permute-start.10 = (bf16[1536,1024]{1,0:T(8,128)(2,1)}, bf16[1536,1024]{1,0:T(8,128)(2,1)}, u32[]{:S(2)}, u32[]{:S(2)}) collective-permute-start(bf16[1536,1024]{1,0:T(8,128)(2,1)} %collective-permute-done.9.part_ref), channel_id=1, source_target_pairs={{1,0},{5,4}} | collective-permute-start | bytes 9437192 | tf_op jit(solution)/shard_map/ppermute | solution.py:179
  79.1 52.9 %collective-permute-start.13 = (bf16[1024,1024]{1,0:T(8,128)(2,1)}, bf16[1024,1024]{1,0:T(8,128)(2,1)}, u32[]{:S(2)}, u32[]{:S(2)}) collective-permute-start(bf16[1024,1024]{1,0:T(8,128)(2,1)} %get-tuple-element.11), channel_id=1, source_target_pairs={{3,1},{7,5}} | collective-permute-start | bytes 6291464 | tf_op jit(solution)/shard_map/ppermute | solution.py:179
  81.0 66.8 %collective-permute-start.11 = (bf16[1024,1024]{1,0:T(8,128)(2,1)}, bf16[1024,1024]{1,0:T(8,128)(2,1)}, u32[]{:S(2)}, u32[]{:S(2)}) collective-permute-start(bf16[1024,1024]{1,0:T(8,128)(2,1)} %get-tuple-element.12), channel_id=1, source_target_pairs={{3,1},{7,5}} | collective-permute-start | bytes 6291464 | tf_op jit(solution)/shard_map/ppermute | solution.py:179
  108.2 22.1 %collective-permute-start.12 = (bf16[512,1024]{1,0:T(8,128)(2,1)}, bf16[512,1024]{1,0:T(8,128)(2,1)}, u32[]{:S(2)}, u32[]{:S(2)}) collective-permute-start(bf16[512,1024]{1,0:T(8,128)(2,1)} %collective-permute-done.2.part_ref), channel_id=1, source_target_pairs={{1,0},{5,4}} | collective-permute-start | bytes 3145736 | tf_op jit(solution)/shard_map/ppermute | solution.py:179
  109.5 53.2 %collective-permute-start.6 = (bf16[1024,1024]{1,0:T(8,128)(2,1)}, bf16[1024,1024]{1,0:T(8,128)(2,1)}, u32[]{:S(2)}, u32[]{:S(2)}) collective-permute-start(bf16[1024,1024]{1,0:T(8,128)(2,1)} %collective-permute-done.5.part_ref), channel_id=1, source_target_pairs={{1,0},{5,4}} | collective-permute-start | bytes 6291464 | tf_op jit(solution)/shard_map/ppermute | solution.py:179
  130.2 30.9 %collective-permute-start.8 = (bf16[640,1024]{1,0:T(8,128)(2,1)}, bf16[640,1024]{1,0:T(8,128)(2,1)}, u32[]{:S(2)}, u32[]{:S(2)}) collective-permute-start(bf16[640,1024]{1,0:T(8,128)(2,1)} %slice.36), channel_id=1, source_target_pairs={{3,1},{7,5}} | collective-permute-start | bytes 3932168 | tf_op jit(solution)/shard_map/ppermute | solution.py:179
  132.0 39.3 %collective-permute-start.7 = (bf16[384,1024]{1,0:T(8,128)(2,1)}, bf16[384,1024]{1,0:T(8,128)(2,1)}, u32[]{:S(2)}, u32[]{:S(2)}) collective-permute-start(bf16[384,1024]{1,0:T(8,128)(2,1)} %slice.35), channel_id=1, source_target_pairs={{3,1},{7,5}} | collective-permute-start | bytes 2359304 | tf_op jit(solution)/shard_map/ppermute | solution.py:179
  133.5 43.2 %collective-permute-start.4 = (bf16[256,1024]{1,0:T(8,128)(2,1)}, bf16[256,1024]{1,0:T(8,128)(2,1)}, u32[]{:S(2)}, u32[]{:S(2)}) collective-permute-start(bf16[256,1024]{1,0:T(8,128)(2,1)} %get-tuple-element.13), channel_id=1, source_target_pairs={{3,1},{7,5}} | collective-permute-start | bytes 1572872 | tf_op jit(solution)/shard_map/ppermute | solution.py:179
  147.9 28.9 %collective-permute-start.1 = (bf16[512,1024]{1,0:T(8,128)(2,1)}, bf16[512,1024]{1,0:T(8,128)(2,1)}, u32[]{:S(2)}, u32[]{:S(2)}) collective-permute-start(bf16[512,1024]{1,0:T(8,128)(2,1)} %collective-permute-done.part_ref), channel_id=1, source_target_pairs={{1,0},{5,4}} | collective-permute-start | bytes 3145736 | tf_op jit(solution)/shard_map/ppermute | solution.py:179
  161.2 19.8 %collective-permute-start.3 = (bf16[256,1024]{1,0:T(8,128)(2,1)}, bf16[256,1024]{1,0:T(8,128)(2,1)}, u32[]{:S(2)}, u32[]{:S(2)}) collective-permute-start(bf16[256,1024]{1,0:T(8,128)(2,1)} %get-tuple-element.14), channel_id=1, source_target_pairs={{3,1},{7,5}} | collective-permute-start | bytes 1572872 | tf_op jit(solution)/shard_map/ppermute | solution.py:179

commit v4 on v3

--- a/solution.py
+++ b/solution.py
@@ -11,7 +11,7 @@
 NEXT = [(1, 0), (2, 1), (3, 2), (0, 3)]
 FAR = [(3, 1)]
 PASS = [(1, 0)]
-PARTS = [(0, 512), (512, 1536), (2048, 1024), (3072, 512)]
+PARTS = [(0, 256), (256, 1792), (2048, 1024), (3072, 512)]
 FARS = [(0, 1024), (1024, 1024), (2048, 640), (2688, 384), (3072, 256), (3328, 256)]
 DEPTH = 3
 FEW = 384
@@ -66,6 +66,22 @@
     )(*args)
 
 
+def bring(a):
+    def kernel(a_ref, own_ref, sem):
+        load(a_ref, own_ref, sem)
+
+    return pl.pallas_call(
+        kernel,
+        in_specs=[pl.BlockSpec(memory_space=pl.ANY)],
+        out_specs=pl.BlockSpec(memory_space=pltpu.VMEM),
+        out_shape=pltpu.VMEM(a.shape, a.dtype),
+        scratch_shapes=[pltpu.SemaphoreType.DMA],
+        cost_estimate=pl.CostEstimate(flops=0, bytes_accessed=4 * a.size, transcendentals=0),
+        compiler_params=pltpu.CompilerParams(vmem_limit_bytes=51 << 20),
+        name="bring",
+    )(a)
+
+
 def diag(own):
     rows, depth = own.shape
     wide = rows // WIDE
@@ -83,7 +99,8 @@
 
 def slot1(first, size, part, own, out):
     rows, depth = own.shape
-    tall = size // WIDE
+    wide = WIDE if size % WIDE == 0 else WIDE // 2
+    tall = size // wide
 
     def kernel(part_ref, own_ref, _, out_ref, sem, load_sem, held, buf):
         p = lax.axis_index("row")
@@ -100,9 +117,9 @@
         @pl.when(p == 3)
         def _():
             stream(
-                rows // HIGH * tall, buf, sem,
-                lambda s: dot_t(tiles(own_ref, s // tall, HIGH), tiles(held, lax.rem(s, tall), WIDE)),
-                lambda s: out_ref.at[0, 1, pl.ds(s // tall * HIGH, HIGH), pl.ds(first + lax.rem(s, tall) * WIDE, WIDE)],
+                rows // HIGH * tall, buf.at[:, :, :wide], sem,
+                lambda s: dot_t(tiles(own_ref, s // tall, HIGH), tiles(held, lax.rem(s, tall), wide)),
+                lambda s: out_ref.at[0, 1, pl.ds(s // tall * HIGH, HIGH), pl.ds(first + lax.rem(s, tall) * wide, wide)],
             )
 
     scratch = [pltpu.VMEM((size, depth), jnp.bfloat16), pltpu.VMEM((DEPTH, HIGH, WIDE), jnp.float32)]
@@ -183,17 +200,17 @@
 
     def local(a):
         head = rows_of(a, PARTS[0])
-        rest, head = lax.optimization_barrier((a, head))
         parts = [send(head, NEXT)]
-        parts += [send(rows_of(rest, PARTS[k]), NEXT) for k in range(1, len(PARTS))]
-        out = diag(a)
+        own = bring(a)
+        parts += [send(rows_of(own, PARTS[k]), NEXT) for k in range(1, len(PARTS))]
+        out = diag(own)
         passed = [send(part, PASS) for part in parts]
-        later, _ = lax.optimization_barrier((a, parts[0]))
+        later, _ = lax.optimization_barrier((own, parts[0]))
         far = [send(rows_of(later, chunk), FAR) for chunk in FARS]
         for k, chunk in enumerate(PARTS):
-            out = slot1(*chunk, parts[k], a, out)
+            out = slot1(*chunk, parts[k], own, out)
         for j, chunk in enumerate(FARS):
-            out = slot2(*chunk, passed, far[j], a, out)
+            out = slot2(*chunk, passed, far[j], own, out)
         return out
 
     return jax.shard_map(

time: 188 us -> 193 us (1.027)
  waiting for transfers between devices: 31.2 us -> 36 us
  Pallas kernels: 122 us -> 125 us
  local copies, waits for them, and re-layouts: 12.2 us -> 9.67 us
    ppermute x14, waiting for transfers between devices: 31.2 us -> 36 us  [send(): return lax.ppermute(a, 'row', pairs)]
    pallas_call x0 -> x1, Pallas kernels: none -> 3.09 us  [bring(): pl.pallas_call(kernel, in_specs=[pl.BlockSpec(memory_space=pl.ANY)], out_...]
    slice x8, local copies, waits for them, and re-layouts: 12.2 us -> 9.67 us  [rows_of(): return a[chunk[0]:chunk[0] + chunk[1]]]
  transfers between devices with their start and end apart: 14 -> 14, of which waited for: 1 -> 1; matrix products, arithmetic and copies ran while one was open for 4% -> 5% of each run, Pallas kernels for 64% -> 62%
where the time goes in v4:
time: 193 us; the launch traced here: 191 us
  Pallas kernels  125 us (65%)
  waiting for transfers between devices  36 us (19%)
  starting transfers between devices  19 us (10%)
  local copies, waits for them, and re-layouts  9.67 us (5%)
    pallas_call x11, Pallas kernels, call(): pl.pallas_call(kernel, in_specs=[pl.BlockSpec(memory_space=space) for _,...  122 us
    ppermute x14, waiting for transfers between devices, send(): return lax.ppermute(a, 'row', pairs)  36 us
    ppermute x14, starting transfers between devices, send(): return lax.ppermute(a, 'row', pairs)  19 us
    slice x8, local copies, waits for them, and re-layouts, rows_of(): return a[chunk[0]:chunk[0] + chunk[1]]  9.67 us
  transfers between devices with their start and end apart: 14, of which 1 were waited for; matrix products, arithmetic and copies ran while one was open for 5% of the time, Pallas kernels for 62%

profile of v4, /device:TPU:0, one launch (start us, length us, event | category | flops | bytes accessed | tf_op | source)
XLA Modules:
  0.0 190.6 jit_solution(13761551818655542515)
XLA Ops:
  0.0 3.1 %bring.1.own_ref.refs_3_.refs_2_ = bf16[3584,1024]{1,0:T(8,128)(2,1)S(1)} custom-call(bf16[3584,1024]{1,0:T(8,128)(2,1)} %a_ref.1), custom_call_target="tpu_custom_call" | custom-call | bytes 14680064 | tf_op jit(solution)/shard_map/bring/pallas_call | solution.py:73
  3.1 0.4 slice.42
  3.5 2.8 %collective-permute-start.9 = (bf16[1792,1024]{1,0:T(8,128)(2,1)S(1)}, bf16[1792,1024]{1,0:T(8,128)(2,1)}, u32[]{:S(2)}, u32[]{:S(2)}) collective-permute-start(bf16[1792,1024]{1,0:T(8,128)(2,1)S(1)} %slice.42), channel_id=1, source_target_pairs={{1,0},{2,1},{3,2},{0,3},{5,4},{6,5},{7,6},{4,7}} | collective-permute-start | bytes 11010056 | tf_op jit(solution)/shard_map/ppermute | solution.py:196
  6.3 1.1 slice.31
  7.3 0.7 collective-permute-start.2
  8.0 1.5 slice.41
  9.5 0.0 collective-permute-start.5
  9.5 1.1 slice.40
  10.6 0.0 collective-permute-start
  10.6 36.0 %collective-permute-done.9.part_ref = bf16[1792,1024]{1,0:T(8,128)(2,1)} collective-permute-done((bf16[1792,1024]{1,0:T(8,128)(2,1)S(1)}, bf16[1792,1024]{1,0:T(8,128)(2,1)}, u32[]{:S(2)}, u32[]{:S(2)}) %collective-permute-start.9) | collective-permute-done | bytes 3670048 | tf_op jit(solution)/shard_map/ppermute | solution.py:196
  46.7 1.3 collective-permute-start.10
  47.9 31.7 %shard_map.17._ = f32[1,3,3584,3584]{3,2,1,0:T(8,128)} custom-call(bf16[3584,1024]{1,0:T(8,128)(2,1)S(1)} %bring.1.own_ref.refs_3_.refs_2_), custom_call_target="tpu_custom_call" | custom-call | flops 26306674688 | bytes 58720256 | tf_op jit(solution)/shard_map/pallas_call | solution.py:55
  79.7 0.0 collective-permute-done.2.part_ref
  79.7 1.2 slice.36
  80.8 0.9 slice.35
  81.8 2.4 %fusion = (bf16[1024,1024]{1,0:T(8,128)(2,1)}, bf16[1024,1024]{1,0:T(8,128)(2,1)}) fusion(bf16[3584,1024]{1,0:T(8,128)(2,1)S(1)} %bring.1.own_ref.refs_3_.refs_2_), kind=kLoop, calls=%fused_computation | loop fusion | bytes 8388608 | tf_op jit(solution)/shard_map/slice | solution.py:199
  84.2 2.0 %collective-permute-start.13 = (bf16[1024,1024]{1,0:T(8,128)(2,1)}, bf16[1024,1024]{1,0:T(8,128)(2,1)}, u32[]{:S(2)}, u32[]{:S(2)}) collective-permute-start(bf16[1024,1024]{1,0:T(8,128)(2,1)} %get-tuple-element.7), channel_id=1, source_target_pairs={{3,1},{7,5}} | collective-permute-start | bytes 6291464 | tf_op jit(solution)/shard_map/ppermute | solution.py:196
  86.2 2.1 %collective-permute-start.11 = (bf16[1024,1024]{1,0:T(8,128)(2,1)}, bf16[1024,1024]{1,0:T(8,128)(2,1)}, u32[]{:S(2)}, u32[]{:S(2)}) collective-permute-start(bf16[1024,1024]{1,0:T(8,128)(2,1)} %get-tuple-element.8), channel_id=1, source_target_pairs={{3,1},{7,5}} | collective-permute-start | bytes 6291464 | tf_op jit(solution)/shard_map/ppermute | solution.py:196
  88.3 5.2 %shard_map.18._ = f32[1,3,3584,3584]{3,2,1,0:T(8,128)} custom-call(bf16[256,1024]{1,0:T(8,128)(2,1)} %collective-permute-done.2.part_ref, bf16[3584,1024]{1,0:T(8,128)(2,1)S(1)} %bring.1.own_ref.refs_3_.refs_2_, f32[1,3,3584,3584]{3,2,1,0:T(8,128)} %shard_map.17._), custom_call_target="tpu_custom_call", output_to_operand_aliasing={{}: (2, {})} | custom-call | flops 1879048192 | bytes 4194304 | tf_op jit(solution)/shard_map/pallas_call | solution.py:55
  93.5 1.1 fusion.1
  94.6 18.7 %shard_map.19._ = f32[1,3,3584,3584]{3,2,1,0:T(8,128)} custom-call(bf16[1792,1024]{1,0:T(8,128)(2,1)} %collective-permute-done.9.part_ref, bf16[3584,1024]{1,0:T(8,128)(2,1)S(1)} %bring.1.own_ref.refs_3_.refs_2_, f32[1,3,3584,3584]{3,2,1,0:T(8,128)} %shard_map.18._), custom_call_target="tpu_custom_call", output_to_operand_aliasing={{}: (2, {})} | custom-call | flops 13153337344 | bytes 29360128 | tf_op jit(solution)/shard_map/pallas_call | solution.py:55
  113.3 0.0 collective-permute-done.part_ref
  113.3 1.3 collective-permute-start.12
  114.6 0.0 collective-permute-done.5.part_ref
  114.6 1.3 collective-permute-start.6
  115.9 12.0 %shard_map.20._ = f32[1,3,3584,3584]{3,2,1,0:T(8,128)} custom-call(bf16[1024,1024]{1,0:T(8,128)(2,1)} %collective-permute-done.5.part_ref, bf16[3584,1024]{1,0:T(8,128)(2,1)S(1)} %bring.1.own_ref.refs_3_.refs_2_, f32[1,3,3584,3584]{3,2,1,0:T(8,128)} %shard_map.19._), custom_call_target="tpu_custom_call", output_to_operand_aliasing={{}: (2, {})} | custom-call | flops 7516192768 | bytes 16777216 | tf_op jit(solution)/shard_map/pallas_call | solution.py:55
  127.9 7.5 %shard_map.21.refs_4_ = f32[1,3,3584,3584]{3,2,1,0:T(8,128)} custom-call(bf16[512,1024]{1,0:T(8,128)(2,1)} %collective-permute-done.part_ref, bf16[3584,1024]{1,0:T(8,128)(2,1)S(1)} %bring.1.own_ref.refs_3_.refs_2_, f32[1,3,3584,3584]{3,2,1,0:T(8,128)} %shard_map.20._), custom_call_target="tpu_custom_call", output_to_operand_aliasing={{}: (2, {})} | custom-call | flops 3758096384 | bytes 8388608 | tf_op jit(solution)/shard_map/pallas_call | solution.py:55
  135.4 0.0 collective-permute-done.12.refs_0_
  135.4 1.8 collective-permute-start.8
  137.2 0.0 collective-permute-done.13.refs_2_
  137.2 1.6 collective-permute-start.7
  138.8 0.0 collective-permute-done.10.refs_1_.refs_0_
  138.8 1.4 collective-permute-start.4
  140.2 12.8 %shard_map.22.refs_3_ = f32[1,3,3584,3584]{3,2,1,0:T(8,128)} custom-call(bf16[256,1024]{1,0:T(8,128)(2,1)} %collective-permute-done.12.refs_0_, bf16[1792,1024]{1,0:T(8,128)(2,1)} %collective-permute-done.10.refs_1_.refs_0_, bf16[1024,1024]{1,0:T(8,128)(2,1)} %collective-permute-done.13.refs_2_, ...), custom_call_target="tpu_custom_call", output_to_operand_aliasing={{}: (4, {})} | custom-call | flops 7516192768 | bytes 16777216 | tf_op jit(solution)/shard_map/pallas_call | solution.py:55
  153.1 0.0 collective-permute-done.11.refs_1_
  153.1 1.3 collective-permute-start.1
  154.4 12.0 %shard_map.23.refs_3_ = f32[1,3,3584,3584]{3,2,1,0:T(8,128)} custom-call(bf16[1792,1024]{1,0:T(8,128)(2,1)} %collective-permute-done.10.refs_1_.refs_0_, bf16[1024,1024]{1,0:T(8,128)(2,1)} %collective-permute-done.11.refs_1_, bf16[3584,1024]{1,0:T(8,128)(2,1)S(1)} %bring.1.own_ref.refs_3_.refs_2_, ...), custom_call_target="tpu_custom_call", output_to_operand_aliasing={{}: (3, {})} | custom-call | flops 7516192768 | bytes 16777216 | tf_op jit(solution)/shard_map/pallas_call | solution.py:55
  166.4 0.0 collective-permute-done.8.refs_1_
  166.4 1.5 collective-permute-start.3
  167.9 0.0 collective-permute-done.6.refs_0_
  167.9 8.6 %shard_map.24.refs_3_ = f32[1,3,3584,3584]{3,2,1,0:T(8,128)} custom-call(bf16[1024,1024]{1,0:T(8,128)(2,1)} %collective-permute-done.6.refs_0_, bf16[640,1024]{1,0:T(8,128)(2,1)} %collective-permute-done.8.refs_1_, bf16[3584,1024]{1,0:T(8,128)(2,1)S(1)} %bring.1.own_ref.refs_3_.refs_2_, ...), custom_call_target="tpu_custom_call", output_to_operand_aliasing={{}: (3, {})} | custom-call | flops 4697620480 | bytes 10485760 | tf_op jit(solution)/shard_map/pallas_call | solution.py:55
  176.5 0.0 collective-permute-done.7.refs_1_
  176.5 5.5 %shard_map.25.refs_3_ = f32[1,3,3584,3584]{3,2,1,0:T(8,128)} custom-call(bf16[1024,1024]{1,0:T(8,128)(2,1)} %collective-permute-done.6.refs_0_, bf16[384,1024]{1,0:T(8,128)(2,1)} %collective-permute-done.7.refs_1_, bf16[3584,1024]{1,0:T(8,128)(2,1)S(1)} %bring.1.own_ref.refs_3_.refs_2_, ...), custom_call_target="tpu_custom_call", output_to_operand_aliasing={{}: (3, {})} | custom-call | flops 2818572288 | bytes 6291456 | tf_op jit(solution)/shard_map/pallas_call | solution.py:55
  182.0 0.0 collective-permute-done.4.refs_1_
  182.0 0.0 collective-permute-done.1.refs_0_
  182.0 4.2 %shard_map.26.refs_3_ = f32[1,3,3584,3584]{3,2,1,0:T(8,128)} custom-call(bf16[512,1024]{1,0:T(8,128)(2,1)} %collective-permute-done.1.refs_0_, bf16[256,1024]{1,0:T(8,128)(2,1)} %collective-permute-done.4.refs_1_, bf16[3584,1024]{1,0:T(8,128)(2,1)S(1)} %bring.1.own_ref.refs_3_.refs_2_, ...), custom_call_target="tpu_custom_call", output_to_operand_aliasing={{}: (3, {})} | custom-call | flops 1879048192 | bytes 4194304 | tf_op jit(solution)/shard_map/pallas_call | solution.py:55
  186.2 0.0 collective-permute-done.3.refs_1_
  186.2 4.2 %shard_map.27 = f32[1,3,3584,3584]{3,2,1,0:T(8,128)} custom-call(bf16[512,1024]{1,0:T(8,128)(2,1)} %collective-permute-done.1.refs_0_, bf16[256,1024]{1,0:T(8,128)(2,1)} %collective-permute-done.3.refs_1_, bf16[3584,1024]{1,0:T(8,128)(2,1)S(1)} %bring.1.own_ref.refs_3_.refs_2_, f32[1,3,3584,3584]{3,2,1,0:T(8,128)} %shard_map.26.refs_3_), custom_call_target="tpu_custom_call", output_to_operand_aliasing={{}: (3, {})} | custom-call | flops 1879048192 | bytes 4194304 | tf_op jit(solution)/shard_map/pallas_call | solution.py:55
Async XLA Ops:
  3.5 43.2 %collective-permute-start.9 = (bf16[1792,1024]{1,0:T(8,128)(2,1)S(1)}, bf16[1792,1024]{1,0:T(8,128)(2,1)}, u32[]{:S(2)}, u32[]{:S(2)}) collective-permute-start(bf16[1792,1024]{1,0:T(8,128)(2,1)S(1)} %slice.42), channel_id=1, source_target_pairs={{1,0},{2,1},{3,2},{0,3},{5,4},{6,5},{7,6},{4,7}} | collective-permute-start | bytes 11010056 | tf_op jit(solution)/shard_map/ppermute | solution.py:196
  7.3 72.3 %collective-permute-start.2 = (bf16[256,1024]{1,0:T(8,128)(2,1)S(1)}, bf16[256,1024]{1,0:T(8,128)(2,1)}, u32[]{:S(2)}, u32[]{:S(2)}) collective-permute-start(bf16[256,1024]{1,0:T(8,128)(2,1)S(1)} %slice.31), channel_id=1, source_target_pairs={{1,0},{2,1},{3,2},{0,3},{5,4},{6,5},{7,6},{4,7}} | collective-permute-start | bytes 1572872 | tf_op jit(solution)/shard_map/ppermute | solution.py:196
  9.5 105.1 %collective-permute-start.5 = (bf16[1024,1024]{1,0:T(8,128)(2,1)}, bf16[1024,1024]{1,0:T(8,128)(2,1)}, u32[]{:S(2)}, u32[]{:S(2)}) collective-permute-start(bf16[1024,1024]{1,0:T(8,128)(2,1)} %slice.41), channel_id=1, source_target_pairs={{1,0},{2,1},{3,2},{0,3},{5,4},{6,5},{7,6},{4,7}} | collective-permute-start | bytes 6291464 | tf_op jit(solution)/shard_map/ppermute | solution.py:196
  10.6 102.7 %collective-permute-start = (bf16[512,1024]{1,0:T(8,128)(2,1)}, bf16[512,1024]{1,0:T(8,128)(2,1)}, u32[]{:S(2)}, u32[]{:S(2)}) collective-permute-start(bf16[512,1024]{1,0:T(8,128)(2,1)} %slice.40), channel_id=1, source_target_pairs={{1,0},{2,1},{3,2},{0,3},{5,4},{6,5},{7,6},{4,7}} | collective-permute-start | bytes 3145736 | tf_op jit(solution)/shard_map/ppermute | solution.py:196
  46.7 92.1 %collective-permute-start.10 = (bf16[1792,1024]{1,0:T(8,128)(2,1)}, bf16[1792,1024]{1,0:T(8,128)(2,1)}, u32[]{:S(2)}, u32[]{:S(2)}) collective-permute-start(bf16[1792,1024]{1,0:T(8,128)(2,1)} %collective-permute-done.9.part_ref), channel_id=1, source_target_pairs={{1,0},{5,4}} | collective-permute-start | bytes 11010056 | tf_op jit(solution)/shard_map/ppermute | solution.py:196
  84.2 53.0 %collective-permute-start.13 = (bf16[1024,1024]{1,0:T(8,128)(2,1)}, bf16[1024,1024]{1,0:T(8,128)(2,1)}, u32[]{:S(2)}, u32[]{:S(2)}) collective-permute-start(bf16[1024,1024]{1,0:T(8,128)(2,1)} %get-tuple-element.7), channel_id=1, source_target_pairs={{3,1},{7,5}} | collective-permute-start | bytes 6291464 | tf_op jit(solution)/shard_map/ppermute | solution.py:196
  86.2 66.9 %collective-permute-start.11 = (bf16[1024,1024]{1,0:T(8,128)(2,1)}, bf16[1024,1024]{1,0:T(8,128)(2,1)}, u32[]{:S(2)}, u32[]{:S(2)}) collective-permute-start(bf16[1024,1024]{1,0:T(8,128)(2,1)} %get-tuple-element.8), channel_id=1, source_target_pairs={{3,1},{7,5}} | collective-permute-start | bytes 6291464 | tf_op jit(solution)/shard_map/ppermute | solution.py:196
  113.3 22.1 %collective-permute-start.12 = (bf16[256,1024]{1,0:T(8,128)(2,1)}, bf16[256,1024]{1,0:T(8,128)(2,1)}, u32[]{:S(2)}, u32[]{:S(2)}) collective-permute-start(bf16[256,1024]{1,0:T(8,128)(2,1)} %collective-permute-done.2.part_ref), channel_id=1, source_target_pairs={{1,0},{5,4}} | collective-permute-start | bytes 1572872 | tf_op jit(solution)/shard_map/ppermute | solution.py:196
  114.6 53.3 %collective-permute-start.6 = (bf16[1024,1024]{1,0:T(8,128)(2,1)}, bf16[1024,1024]{1,0:T(8,128)(2,1)}, u32[]{:S(2)}, u32[]{:S(2)}) collective-permute-start(bf16[1024,1024]{1,0:T(8,128)(2,1)} %collective-permute-done.5.part_ref), channel_id=1, source_target_pairs={{1,0},{5,4}} | collective-permute-start | bytes 6291464 | tf_op jit(solution)/shard_map/ppermute | solution.py:196
  135.4 31.0 %collective-permute-start.8 = (bf16[640,1024]{1,0:T(8,128)(2,1)}, bf16[640,1024]{1,0:T(8,128)(2,1)}, u32[]{:S(2)}, u32[]{:S(2)}) collective-permute-start(bf16[640,1024]{1,0:T(8,128)(2,1)} %slice.36), channel_id=1, source_target_pairs={{3,1},{7,5}} | collective-permute-start | bytes 3932168 | tf_op jit(solution)/shard_map/ppermute | solution.py:196
  137.2 39.3 %collective-permute-start.7 = (bf16[384,1024]{1,0:T(8,128)(2,1)}, bf16[384,1024]{1,0:T(8,128)(2,1)}, u32[]{:S(2)}, u32[]{:S(2)}) collective-permute-start(bf16[384,1024]{1,0:T(8,128)(2,1)} %slice.35), channel_id=1, source_target_pairs={{3,1},{7,5}} | collective-permute-start | bytes 2359304 | tf_op jit(solution)/shard_map/ppermute | solution.py:196
  138.8 43.2 %collective-permute-start.4 = (bf16[256,1024]{1,0:T(8,128)(2,1)}, bf16[256,1024]{1,0:T(8,128)(2,1)}, u32[]{:S(2)}, u32[]{:S(2)}) collective-permute-start(bf16[256,1024]{1,0:T(8,128)(2,1)} %get-tuple-element.9), channel_id=1, source_target_pairs={{3,1},{7,5}} | collective-permute-start | bytes 1572872 | tf_op jit(solution)/shard_map/ppermute | solution.py:196
  153.1 28.9 %collective-permute-start.1 = (bf16[512,1024]{1,0:T(8,128)(2,1)}, bf16[512,1024]{1,0:T(8,128)(2,1)}, u32[]{:S(2)}, u32[]{:S(2)}) collective-permute-start(bf16[512,1024]{1,0:T(8,128)(2,1)} %collective-permute-done.part_ref), channel_id=1, source_target_pairs={{1,0},{5,4}} | collective-permute-start | bytes 3145736 | tf_op jit(solution)/shard_map/ppermute | solution.py:196
  166.4 19.8 %collective-permute-start.3 = (bf16[256,1024]{1,0:T(8,128)(2,1)}, bf16[256,1024]{1,0:T(8,128)(2,1)}, u32[]{:S(2)}, u32[]{:S(2)}) collective-permute-start(bf16[256,1024]{1,0:T(8,128)(2,1)} %get-tuple-element.10), channel_id=1, source_target_pairs={{3,1},{7,5}} | collective-permute-start | bytes 1572872 | tf_op jit(solution)/shard_map/ppermute | solution.py:196

commit v5 on v4

--- a/solution.py
+++ b/solution.py
@@ -12,10 +12,11 @@
 FAR = [(3, 1)]
 PASS = [(1, 0)]
 PARTS = [(0, 256), (256, 1792), (2048, 1024), (3072, 512)]
-FARS = [(0, 1024), (1024, 1024), (2048, 640), (2688, 384), (3072, 256), (3328, 256)]
+FARS = [(0, 1024), (1024, 848), (1872, 640), (2512, 416), (2928, 272), (3200, 208), (3408, 176)]
+TURN_AFTER = 0
 DEPTH = 3
-FEW = 384
-PIECES = [(0, 1536), (1536, 1536), (3072, 512)]
+FEW = 448
+PIECES = [(0, 2560), (2560, 1024)]
 
 
 def dot_t(x, y):
@@ -82,6 +83,28 @@
     )(a)
 
 
+def turn(own, out):
+    rows, depth = own.shape
+
+    def kernel(own_ref, _, turned_ref, out_ref):
+        @pl.when(lax.axis_index("row") < 2)
+        def _():
+            @pl.loop(0, rows // WIDE)
+            def _(s):
+                turned_ref[:, pl.ds(pl.multiple_of(s * WIDE, WIDE), WIDE)] = tiles(own_ref, s, WIDE).T
+
+    return pl.pallas_call(
+        kernel,
+        in_specs=[pl.BlockSpec(memory_space=pltpu.VMEM), pl.BlockSpec(memory_space=pl.ANY)],
+        out_specs=[pl.BlockSpec(memory_space=pltpu.VMEM), pl.BlockSpec(memory_space=pl.ANY)],
+        out_shape=[pltpu.VMEM((depth, rows), own.dtype), jax.ShapeDtypeStruct(out.shape, out.dtype)],
+        input_output_aliases={1: 1},
+        cost_estimate=pl.CostEstimate(flops=0, bytes_accessed=4 * own.size, transcendentals=0),
+        compiler_params=pltpu.CompilerParams(vmem_limit_bytes=32 << 20),
+        name="turn",
+    )(own, out)
+
+
 def diag(own):
     rows, depth = own.shape
     wide = rows // WIDE
@@ -127,7 +150,7 @@
 
 
 def slot2(first, size, passed, far, own, out):
-    rows, depth = own.shape
+    rows, depth = own.shape if size > FEW else own.shape[::-1]
     near = []
     for (start, count), part in zip(PARTS, passed):
         low, end = max(first, start), min(first + size, start + count)
@@ -173,7 +196,7 @@
             def _():
                 copies = []
                 for k, (start, wide) in enumerate(PIECES):
-                    buf[k, :, :wide] = dot_t(held[...], own_ref[start:start + wide, :])
+                    buf[k, :, :wide] = jnp.dot(held[...], own_ref[:, start:start + wide], preferred_element_type=jnp.float32)
                     copies.append(pltpu.make_async_copy(buf.at[k, :, :wide], place(start, wide), sem.at[k]))
                     copies[-1].start()
                 for copy in copies:
@@ -210,7 +233,9 @@
         for k, chunk in enumerate(PARTS):
             out = slot1(*chunk, parts[k], own, out)
         for j, chunk in enumerate(FARS):
-            out = slot2(*chunk, passed, far[j], own, out)
+            out = slot2(*chunk, passed, far[j], own if chunk[1] > FEW else turned, out)
+            if j == TURN_AFTER:
+                turned, out = turn(own, out)
         return out
 
     return jax.shard_map(

time: 193 us -> 200 us (1.036)
  Pallas kernels: 125 us -> 130 us
    pallas_call x11 -> x12, Pallas kernels: 122 us -> 125 us  [call(): pl.pallas_call(kernel, in_specs=[pl.BlockSpec(memory_space=space) for _,...]
    pallas_call x0 -> x1, Pallas kernels: none -> 2.29 us  [turn(): pl.pallas_call(kernel, in_specs=[pl.BlockSpec(memory_space=pltpu.VMEM), p...]
    slice x8 -> x11, local copies, waits for them, and re-layouts: 9.67 us -> 11.5 us  [rows_of(): return a[chunk[0]:chunk[0] + chunk[1]]]
    ppermute x14 -> x15, starting transfers between devices: 19 us -> 20.2 us  [send(): return lax.ppermute(a, 'row', pairs)]
    ppermute x14 -> x15, waiting for transfers between devices: 36 us -> 36.1 us  [send(): return lax.ppermute(a, 'row', pairs)]
  transfers between devices with their start and end apart: 14 -> 15, of which waited for: 1 -> 1; matrix products, arithmetic and copies ran while one was open for 5% -> 6% of each run, Pallas kernels for 62% -> 62%
where the time goes in v5:
time: 200 us; the launch traced here: 198 us
  Pallas kernels  130 us (65%)
  waiting for transfers between devices  36.1 us (18%)
  starting transfers between devices  20.2 us (10%)
  local copies, waits for them, and re-layouts  11.5 us (6%)
    pallas_call x12, Pallas kernels, call(): pl.pallas_call(kernel, in_specs=[pl.BlockSpec(memory_space=space) for _,...  125 us
    ppermute x15, waiting for transfers between devices, send(): return lax.ppermute(a, 'row', pairs)  36.1 us
    ppermute x15, starting transfers between devices, send(): return lax.ppermute(a, 'row', pairs)  20.2 us
    slice x11, local copies, waits for them, and re-layouts, rows_of(): return a[chunk[0]:chunk[0] + chunk[1]]  11.5 us
  transfers between devices with their start and end apart: 15, of which 1 were waited for; matrix products, arithmetic and copies ran while one was open for 6% of the time, Pallas kernels for 62%

profile of v5, /device:TPU:0, one launch (start us, length us, event | category | flops | bytes accessed | tf_op | source)
XLA Modules:
  0.0 198.4 jit_solution(10867886752033969775)
XLA Ops:
  0.0 3.1 %bring.1.own_ref.refs_3_.refs_2_ = bf16[3584,1024]{1,0:T(8,128)(2,1)S(1)} custom-call(bf16[3584,1024]{1,0:T(8,128)(2,1)} %a_ref.1), custom_call_target="tpu_custom_call" | custom-call | bytes 14680064 | tf_op jit(solution)/shard_map/bring/pallas_call | solution.py:74
  3.1 0.4 slice.45
  3.5 2.8 %collective-permute-start.5 = (bf16[1792,1024]{1,0:T(8,128)(2,1)S(1)}, bf16[1792,1024]{1,0:T(8,128)(2,1)}, u32[]{:S(2)}, u32[]{:S(2)}) collective-permute-start(bf16[1792,1024]{1,0:T(8,128)(2,1)S(1)} %slice.45), channel_id=1, source_target_pairs={{1,0},{2,1},{3,2},{0,3},{5,4},{6,5},{7,6},{4,7}} | collective-permute-start | bytes 11010056 | tf_op jit(solution)/shard_map/ppermute | solution.py:219
  6.3 1.1 slice.34
  7.3 0.7 collective-permute-start.2
  8.0 1.5 slice.46
  9.5 0.0 collective-permute-start.8
  9.5 1.1 slice.44
  10.6 0.0 collective-permute-start
  10.6 36.1 %collective-permute-done.5.part_ref = bf16[1792,1024]{1,0:T(8,128)(2,1)} collective-permute-done((bf16[1792,1024]{1,0:T(8,128)(2,1)S(1)}, bf16[1792,1024]{1,0:T(8,128)(2,1)}, u32[]{:S(2)}, u32[]{:S(2)}) %collective-permute-start.5) | collective-permute-done | bytes 3670048 | tf_op jit(solution)/shard_map/ppermute | solution.py:219
  46.7 1.3 collective-permute-start.6
  47.9 31.7 %shard_map.17._ = f32[1,3,3584,3584]{3,2,1,0:T(8,128)} custom-call(bf16[3584,1024]{1,0:T(8,128)(2,1)S(1)} %bring.1.own_ref.refs_3_.refs_2_), custom_call_target="tpu_custom_call" | custom-call | flops 26306674688 | bytes 58720256 | tf_op jit(solution)/shard_map/pallas_call | solution.py:56
  79.7 0.0 collective-permute-done.2.part_ref
  79.7 1.6 slice.37
  81.3 1.3 slice.43
  82.6 1.2 slice.42
  83.8 1.0 slice.41
  84.8 0.8 slice.40
  85.6 0.8 slice.39
  86.4 0.8 slice.35
  87.2 2.0 collective-permute-start.7
  89.2 1.9 collective-permute-start.14
  91.1 4.2 %shard_map.18._ = f32[1,3,3584,3584]{3,2,1,0:T(8,128)} custom-call(bf16[256,1024]{1,0:T(8,128)(2,1)S(1)} %collective-permute-done.2.part_ref, bf16[3584,1024]{1,0:T(8,128)(2,1)S(1)} %bring.1.own_ref.refs_3_.refs_2_, f32[1,3,3584,3584]{3,2,1,0:T(8,128)} %shard_map.17._), custom_call_target="tpu_custom_call", output_to_operand_aliasing={{}: (2, {})} | custom-call | flops 1879048192 | bytes 4194304 | tf_op jit(solution)/shard_map/pallas_call | solution.py:56
  95.3 18.7 %shard_map.19._ = f32[1,3,3584,3584]{3,2,1,0:T(8,128)} custom-call(bf16[1792,1024]{1,0:T(8,128)(2,1)} %collective-permute-done.5.part_ref, bf16[3584,1024]{1,0:T(8,128)(2,1)S(1)} %bring.1.own_ref.refs_3_.refs_2_, f32[1,3,3584,3584]{3,2,1,0:T(8,128)} %shard_map.18._), custom_call_target="tpu_custom_call", output_to_operand_aliasing={{}: (2, {})} | custom-call | flops 13153337344 | bytes 29360128 | tf_op jit(solution)/shard_map/pallas_call | solution.py:56
  114.0 0.0 collective-permute-done.part_ref
  114.0 1.3 collective-permute-start.4
  115.3 0.0 collective-permute-done.8.part_ref
  115.3 1.3 collective-permute-start.10
  116.6 12.0 %shard_map.20._ = f32[1,3,3584,3584]{3,2,1,0:T(8,128)} custom-call(bf16[1024,1024]{1,0:T(8,128)(2,1)} %collective-permute-done.8.part_ref, bf16[3584,1024]{1,0:T(8,128)(2,1)S(1)} %bring.1.own_ref.refs_3_.refs_2_, f32[1,3,3584,3584]{3,2,1,0:T(8,128)} %shard_map.19._), custom_call_target="tpu_custom_call", output_to_operand_aliasing={{}: (2, {})} | custom-call | flops 7516192768 | bytes 16777216 | tf_op jit(solution)/shard_map/pallas_call | solution.py:56
  128.6 0.0 collective-permute-done.4.refs_0_
  128.6 1.7 collective-permute-start.13
  130.3 7.5 %shard_map.21.refs_4_ = f32[1,3,3584,3584]{3,2,1,0:T(8,128)} custom-call(bf16[512,1024]{1,0:T(8,128)(2,1)} %collective-permute-done.part_ref, bf16[3584,1024]{1,0:T(8,128)(2,1)S(1)} %bring.1.own_ref.refs_3_.refs_2_, f32[1,3,3584,3584]{3,2,1,0:T(8,128)} %shard_map.20._), custom_call_target="tpu_custom_call", output_to_operand_aliasing={{}: (2, {})} | custom-call | flops 3758096384 | bytes 8388608 | tf_op jit(solution)/shard_map/pallas_call | solution.py:56
  137.8 0.0 collective-permute-done.7.refs_2_
  137.8 1.6 collective-permute-start.12
  139.4 0.0 collective-permute-done.6.refs_1_.refs_0_
  139.4 1.5 collective-permute-start.11
  140.9 11.8 %shard_map.22._ = f32[1,3,3584,3584]{3,2,1,0:T(8,128)} custom-call(bf16[256,1024]{1,0:T(8,128)(2,1)S(1)} %collective-permute-done.4.refs_0_, bf16[1792,1024]{1,0:T(8,128)(2,1)} %collective-permute-done.6.refs_1_.refs_0_, bf16[1024,1024]{1,0:T(8,128)(2,1)} %collective-permute-done.7.refs_2_, ...), custom_call_target="tpu_custom_call", output_to_operand_aliasing={{}: (4, {})} | custom-call | flops 7516192768 | bytes 16777216 | tf_op jit(solution)/shard_map/pallas_call | solution.py:56
  152.7 2.3 %turn.1 = (bf16[1024,3584]{1,0:T(8,128)(2,1)S(1)}, f32[1,3,3584,3584]{3,2,1,0:T(8,128)}) custom-call(bf16[3584,1024]{1,0:T(8,128)(2,1)S(1)} %bring.1.own_ref.refs_3_.refs_2_, f32[1,3,3584,3584]{3,2,1,0:T(8,128)} %shard_map.22._), custom_call_target="tpu_custom_call", output_to_operand_aliasing={{1}: (1, {})} | custom-call | bytes 14680064 | tf_op jit(solution)/shard_map/turn/pallas_call | solution.py:96
  155.0 0.0 collective-permute-done.14.refs_1_
  155.0 1.3 collective-permute-start.1
  156.3 10.4 %shard_map.23.refs_4_ = f32[1,3,3584,3584]{3,2,1,0:T(8,128)} custom-call(bf16[1792,1024]{1,0:T(8,128)(2,1)} %collective-permute-done.6.refs_1_.refs_0_, bf16[848,1024]{1,0:T(8,128)(2,1)} %collective-permute-done.14.refs_1_, bf16[3584,1024]{1,0:T(8,128)(2,1)S(1)} %bring.1.own_ref.refs_3_.refs_2_, ...), custom_call_target="tpu_custom_call", output_to_operand_aliasing={{}: (3, {})} | custom-call | flops 6224347136 | bytes 13893632 | tf_op jit(solution)/shard_map/pallas_call | solution.py:56
  166.8 0.0 collective-permute-done.13.refs_2_
  166.8 1.4 collective-permute-start.9
  168.2 0.0 collective-permute-done.10.refs_1_.refs_0_
  168.2 1.4 collective-permute-start.3
  169.6 9.4 %shard_map.24.refs_3_ = f32[1,3,3584,3584]{3,2,1,0:T(8,128)} custom-call(bf16[1792,1024]{1,0:T(8,128)(2,1)} %collective-permute-done.6.refs_1_.refs_0_, bf16[1024,1024]{1,0:T(8,128)(2,1)} %collective-permute-done.10.refs_1_.refs_0_, bf16[640,1024]{1,0:T(8,128)(2,1)} %collective-permute-done.13.refs_2_, ...), custom_call_target="tpu_custom_call", output_to_operand_aliasing={{}: (4, {})} | custom-call | flops 4697620480 | bytes 10485760 | tf_op jit(solution)/shard_map/pallas_call | solution.py:56
  179.1 0.0 collective-permute-done.12.refs_1_
  179.1 6.2 %shard_map.25.refs_4_ = f32[1,3,3584,3584]{3,2,1,0:T(8,128)} custom-call(bf16[1024,1024]{1,0:T(8,128)(2,1)} %collective-permute-done.10.refs_1_.refs_0_, bf16[416,1024]{1,0:T(8,128)(2,1)} %collective-permute-done.12.refs_1_, bf16[1024,3584]{1,0:T(8,128)(2,1)S(1)} %get-tuple-element.9.refs_2_.refs_3_, ...), custom_call_target="tpu_custom_call", output_to_operand_aliasing={{}: (3, {})} | custom-call | flops 3053453312 | bytes 6815744 | tf_op jit(solution)/shard_map/pallas_call | solution.py:56
  185.2 0.0 collective-permute-done.11.refs_2_
  185.2 0.0 collective-permute-done.1.refs_1_.refs_0_
  185.3 5.5 %shard_map.26.refs_3_ = f32[1,3,3584,3584]{3,2,1,0:T(8,128)} custom-call(bf16[1024,1024]{1,0:T(8,128)(2,1)} %collective-permute-done.10.refs_1_.refs_0_, bf16[512,1024]{1,0:T(8,128)(2,1)} %collective-permute-done.1.refs_1_.refs_0_, bf16[272,1024]{1,0:T(8,128)(2,1)} %collective-permute-done.11.refs_2_, ...), custom_call_target="tpu_custom_call", output_to_operand_aliasing={{}: (4, {})} | custom-call | flops 1996488704 | bytes 4456448 | tf_op jit(solution)/shard_map/pallas_call | solution.py:56
  190.7 0.0 collective-permute-done.9.refs_1_
  190.7 3.9 %shard_map.27.refs_3_ = f32[1,3,3584,3584]{3,2,1,0:T(8,128)} custom-call(bf16[512,1024]{1,0:T(8,128)(2,1)} %collective-permute-done.1.refs_1_.refs_0_, bf16[208,1024]{1,0:T(8,128)(2,1)} %collective-permute-done.9.refs_1_, bf16[1024,3584]{1,0:T(8,128)(2,1)S(1)} %get-tuple-element.9.refs_2_.refs_3_, ...), custom_call_target="tpu_custom_call", output_to_operand_aliasing={{}: (3, {})} | custom-call | flops 1526726656 | bytes 3407872 | tf_op jit(solution)/shard_map/pallas_call | solution.py:56
  194.7 0.0 collective-permute-done.3.refs_1_
  194.7 3.6 %shard_map.28 = f32[1,3,3584,3584]{3,2,1,0:T(8,128)} custom-call(bf16[512,1024]{1,0:T(8,128)(2,1)} %collective-permute-done.1.refs_1_.refs_0_, bf16[176,1024]{1,0:T(8,128)(2,1)} %collective-permute-done.3.refs_1_, bf16[1024,3584]{1,0:T(8,128)(2,1)S(1)} %get-tuple-element.9.refs_2_.refs_3_, ...), custom_call_target="tpu_custom_call", output_to_operand_aliasing={{}: (3, {})} | custom-call | flops 1291845632 | bytes 2883584 | tf_op jit(solution)/shard_map/pallas_call | solution.py:56
Async XLA Ops:
  3.5 43.2 %collective-permute-start.5 = (bf16[1792,1024]{1,0:T(8,128)(2,1)S(1)}, bf16[1792,1024]{1,0:T(8,128)(2,1)}, u32[]{:S(2)}, u32[]{:S(2)}) collective-permute-start(bf16[1792,1024]{1,0:T(8,128)(2,1)S(1)} %slice.45), channel_id=1, source_target_pairs={{1,0},{2,1},{3,2},{0,3},{5,4},{6,5},{7,6},{4,7}} | collective-permute-start | bytes 11010056 | tf_op jit(solution)/shard_map/ppermute | solution.py:219
  7.3 72.3 %collective-permute-start.2 = (bf16[256,1024]{1,0:T(8,128)(2,1)S(1)}, bf16[256,1024]{1,0:T(8,128)(2,1)S(1)}, u32[]{:S(2)}, u32[]{:S(2)}) collective-permute-start(bf16[256,1024]{1,0:T(8,128)(2,1)S(1)} %slice.34), channel_id=1, source_target_pairs={{1,0},{2,1},{3,2},{0,3},{5,4},{6,5},{7,6},{4,7}} | collective-permute-start | bytes 1572872 | tf_op jit(solution)/shard_map/ppermute | solution.py:219
  9.5 105.8 %collective-permute-start.8 = (bf16[1024,1024]{1,0:T(8,128)(2,1)}, bf16[1024,1024]{1,0:T(8,128)(2,1)}, u32[]{:S(2)}, u32[]{:S(2)}) collective-permute-start(bf16[1024,1024]{1,0:T(8,128)(2,1)} %slice.46), channel_id=1, source_target_pairs={{1,0},{2,1},{3,2},{0,3},{5,4},{6,5},{7,6},{4,7}} | collective-permute-start | bytes 6291464 | tf_op jit(solution)/shard_map/ppermute | solution.py:219
  10.6 103.4 %collective-permute-start = (bf16[512,1024]{1,0:T(8,128)(2,1)}, bf16[512,1024]{1,0:T(8,128)(2,1)}, u32[]{:S(2)}, u32[]{:S(2)}) collective-permute-start(bf16[512,1024]{1,0:T(8,128)(2,1)} %slice.44), channel_id=1, source_target_pairs={{1,0},{2,1},{3,2},{0,3},{5,4},{6,5},{7,6},{4,7}} | collective-permute-start | bytes 3145736 | tf_op jit(solution)/shard_map/ppermute | solution.py:219
  46.7 92.7 %collective-permute-start.6 = (bf16[1792,1024]{1,0:T(8,128)(2,1)}, bf16[1792,1024]{1,0:T(8,128)(2,1)}, u32[]{:S(2)}, u32[]{:S(2)}) collective-permute-start(bf16[1792,1024]{1,0:T(8,128)(2,1)} %collective-permute-done.5.part_ref), channel_id=1, source_target_pairs={{1,0},{5,4}} | collective-permute-start | bytes 11010056 | tf_op jit(solution)/shard_map/ppermute | solution.py:219
  87.2 50.6 %collective-permute-start.7 = (bf16[1024,1024]{1,0:T(8,128)(2,1)}, bf16[1024,1024]{1,0:T(8,128)(2,1)}, u32[]{:S(2)}, u32[]{:S(2)}) collective-permute-start(bf16[1024,1024]{1,0:T(8,128)(2,1)} %slice.37), channel_id=1, source_target_pairs={{3,1},{7,5}} | collective-permute-start | bytes 6291464 | tf_op jit(solution)/shard_map/ppermute | solution.py:219
  89.2 65.9 %collective-permute-start.14 = (bf16[848,1024]{1,0:T(8,128)(2,1)}, bf16[848,1024]{1,0:T(8,128)(2,1)}, u32[]{:S(2)}, u32[]{:S(2)}) collective-permute-start(bf16[848,1024]{1,0:T(8,128)(2,1)} %slice.43), channel_id=1, source_target_pairs={{3,1},{7,5}} | collective-permute-start | bytes 5210120 | tf_op jit(solution)/shard_map/ppermute | solution.py:219
  114.0 14.6 %collective-permute-start.4 = (bf16[256,1024]{1,0:T(8,128)(2,1)S(1)}, bf16[256,1024]{1,0:T(8,128)(2,1)S(1)}, u32[]{:S(2)}, u32[]{:S(2)}) collective-permute-start(bf16[256,1024]{1,0:T(8,128)(2,1)S(1)} %collective-permute-done.2.part_ref), channel_id=1, source_target_pairs={{1,0},{5,4}} | collective-permute-start | bytes 1572872 | tf_op jit(solution)/shard_map/ppermute | solution.py:219
  115.3 52.9 %collective-permute-start.10 = (bf16[1024,1024]{1,0:T(8,128)(2,1)}, bf16[1024,1024]{1,0:T(8,128)(2,1)}, u32[]{:S(2)}, u32[]{:S(2)}) collective-permute-start(bf16[1024,1024]{1,0:T(8,128)(2,1)} %collective-permute-done.8.part_ref), channel_id=1, source_target_pairs={{1,0},{5,4}} | collective-permute-start | bytes 6291464 | tf_op jit(solution)/shard_map/ppermute | solution.py:219
  128.6 38.2 %collective-permute-start.13 = (bf16[640,1024]{1,0:T(8,128)(2,1)}, bf16[640,1024]{1,0:T(8,128)(2,1)}, u32[]{:S(2)}, u32[]{:S(2)}) collective-permute-start(bf16[640,1024]{1,0:T(8,128)(2,1)} %slice.42), channel_id=1, source_target_pairs={{3,1},{7,5}} | collective-permute-start | bytes 3932168 | tf_op jit(solution)/shard_map/ppermute | solution.py:219
  137.8 41.3 %collective-permute-start.12 = (bf16[416,1024]{1,0:T(8,128)(2,1)}, bf16[416,1024]{1,0:T(8,128)(2,1)}, u32[]{:S(2)}, u32[]{:S(2)}) collective-permute-start(bf16[416,1024]{1,0:T(8,128)(2,1)} %slice.41), channel_id=1, source_target_pairs={{3,1},{7,5}} | collective-permute-start | bytes 2555912 | tf_op jit(solution)/shard_map/ppermute | solution.py:219
  139.4 45.8 %collective-permute-start.11 = (bf16[272,1024]{1,0:T(8,128)(2,1)}, bf16[272,1024]{1,0:T(8,128)(2,1)}, u32[]{:S(2)}, u32[]{:S(2)}) collective-permute-start(bf16[272,1024]{1,0:T(8,128)(2,1)} %slice.40), channel_id=1, source_target_pairs={{3,1},{7,5}} | collective-permute-start | bytes 1671176 | tf_op jit(solution)/shard_map/ppermute | solution.py:219
  155.0 30.2 %collective-permute-start.1 = (bf16[512,1024]{1,0:T(8,128)(2,1)}, bf16[512,1024]{1,0:T(8,128)(2,1)}, u32[]{:S(2)}, u32[]{:S(2)}) collective-permute-start(bf16[512,1024]{1,0:T(8,128)(2,1)} %collective-permute-done.part_ref), channel_id=1, source_target_pairs={{1,0},{5,4}} | collective-permute-start | bytes 3145736 | tf_op jit(solution)/shard_map/ppermute | solution.py:219
  166.8 24.0 %collective-permute-start.9 = (bf16[208,1024]{1,0:T(8,128)(2,1)}, bf16[208,1024]{1,0:T(8,128)(2,1)}, u32[]{:S(2)}, u32[]{:S(2)}) collective-permute-start(bf16[208,1024]{1,0:T(8,128)(2,1)} %slice.39), channel_id=1, source_target_pairs={{3,1},{7,5}} | collective-permute-start | bytes 1277960 | tf_op jit(solution)/shard_map/ppermute | solution.py:219
  168.2 26.5 %collective-permute-start.3 = (bf16[176,1024]{1,0:T(8,128)(2,1)}, bf16[176,1024]{1,0:T(8,128)(2,1)}, u32[]{:S(2)}, u32[]{:S(2)}) collective-permute-start(bf16[176,1024]{1,0:T(8,128)(2,1)} %slice.35), channel_id=1, source_target_pairs={{3,1},{7,5}} | collective-permute-start | bytes 1081352 | tf_op jit(solution)/shard_map/ppermute | solution.py:219

commit v6 on v5

--- a/solution.py
+++ b/solution.py
@@ -16,7 +16,6 @@
 TURN_AFTER = 0
 DEPTH = 3
 FEW = 448
-PIECES = [(0, 2560), (2560, 1024)]
 
 
 def dot_t(x, y):
@@ -59,7 +58,7 @@
         out_specs=pl.BlockSpec(memory_space=pl.ANY),
         out_shape=jax.ShapeDtypeStruct(out.shape, out.dtype),
         input_output_aliases={} if made else {len(args) - 1: 0},
-        scratch_shapes=[pltpu.SemaphoreType.DMA((DEPTH,)), pltpu.SemaphoreType.DMA, *scratch],
+        scratch_shapes=[pltpu.SemaphoreType.DMA((8,)), pltpu.SemaphoreType.DMA, *scratch],
         cost_estimate=pl.CostEstimate(
             flops=2 * rows * cols * depth, bytes_accessed=4 * rows * cols + 2 * rows * depth, transcendentals=0
         ),
@@ -173,13 +172,6 @@
         def _():
             load(far_ref, held, load_sem)
 
-        def zeros(wide):
-            stream(
-                rows // wide, buf.at[:, :, :wide], sem,
-                lambda s: jnp.zeros((size, wide), jnp.float32),
-                lambda s: place(s * wide, wide),
-            )
-
         if size > FEW:
 
             @pl.when(p < 2)
@@ -195,19 +187,24 @@
             @pl.when(p < 2)
             def _():
                 copies = []
-                for k, (start, wide) in enumerate(PIECES):
-                    buf[k, :, :wide] = jnp.dot(held[...], own_ref[:, start:start + wide], preferred_element_type=jnp.float32)
-                    copies.append(pltpu.make_async_copy(buf.at[k, :, :wide], place(start, wide), sem.at[k]))
+                for k in range(rows // WIDE):
+                    at = slice(k * WIDE, (k + 1) * WIDE)
+                    buf[k] = jnp.dot(held[...], own_ref[:, at], preferred_element_type=jnp.float32)
+                    copies.append(pltpu.make_async_copy(buf.at[k], place(k * WIDE, WIDE), sem.at[k]))
                     copies[-1].start()
                 for copy in copies:
                     copy.wait()
 
         @pl.when(p >= 2)
         def _():
-            zeros(WIDE)
-
-    width = WIDE if size > FEW else PIECES[0][1]
-    scratch = [pltpu.VMEM((size, depth), jnp.bfloat16), pltpu.VMEM((DEPTH, size, width), jnp.float32)]
+            stream(
+                rows // WIDE, buf, sem,
+                lambda s: jnp.zeros((size, WIDE), jnp.float32),
+                lambda s: place(s * WIDE, WIDE),
+            )
+
+    bufs = DEPTH if size > FEW else rows // WIDE
+    scratch = [pltpu.VMEM((size, depth), jnp.bfloat16), pltpu.VMEM((bufs, size, WIDE), jnp.float32)]
     refs = [(part, pl.ANY) for part, *_ in near] + [(far, pl.ANY), (own, pltpu.VMEM)]
     return call(kernel, size, rows, depth, out, refs, scratch)
 

time: 200 us -> 198 us (0.990)
  no operation moved by 1% of the time
where the time goes in v6:
time: 198 us; the launch traced here: 197 us
  Pallas kernels  129 us (65%)
  waiting for transfers between devices  36.1 us (18%)
  starting transfers between devices  20.2 us (10%)
  local copies, waits for them, and re-layouts  11.5 us (6%)
    pallas_call x12, Pallas kernels, call(): pl.pallas_call(kernel, in_specs=[pl.BlockSpec(memory_space=space) for _,...  123 us
    ppermute x15, waiting for transfers between devices, send(): return lax.ppermute(a, 'row', pairs)  36.1 us
    ppermute x15, starting transfers between devices, send(): return lax.ppermute(a, 'row', pairs)  20.2 us
    slice x11, local copies, waits for them, and re-layouts, rows_of(): return a[chunk[0]:chunk[0] + chunk[1]]  11.5 us
  transfers between devices with their start and end apart: 15, of which 1 were waited for; matrix products, arithmetic and copies ran while one was open for 6% of the time, Pallas kernels for 62%

profile of v6, /device:TPU:0, one launch (start us, length us, event | category | flops | bytes accessed | tf_op | source)
XLA Modules:
  0.0 196.9 jit_solution(6020004086363335268)
XLA Ops:
  0.0 3.1 %bring.1.own_ref.refs_3_.refs_2_ = bf16[3584,1024]{1,0:T(8,128)(2,1)S(1)} custom-call(bf16[3584,1024]{1,0:T(8,128)(2,1)} %a_ref.1), custom_call_target="tpu_custom_call" | custom-call | bytes 14680064 | tf_op jit(solution)/shard_map/bring/pallas_call | solution.py:73
  3.1 0.4 slice.45
  3.5 2.8 %collective-permute-start.5 = (bf16[1792,1024]{1,0:T(8,128)(2,1)S(1)}, bf16[1792,1024]{1,0:T(8,128)(2,1)}, u32[]{:S(2)}, u32[]{:S(2)}) collective-permute-start(bf16[1792,1024]{1,0:T(8,128)(2,1)S(1)} %slice.45), channel_id=1, source_target_pairs={{1,0},{2,1},{3,2},{0,3},{5,4},{6,5},{7,6},{4,7}} | collective-permute-start | bytes 11010056 | tf_op jit(solution)/shard_map/ppermute | solution.py:216
  6.3 1.1 slice.34
  7.3 0.7 collective-permute-start.2
  8.0 1.5 slice.46
  9.5 0.0 collective-permute-start.8
  9.5 1.1 slice.44
  10.6 0.0 collective-permute-start
  10.6 36.1 %collective-permute-done.5.part_ref = bf16[1792,1024]{1,0:T(8,128)(2,1)} collective-permute-done((bf16[1792,1024]{1,0:T(8,128)(2,1)S(1)}, bf16[1792,1024]{1,0:T(8,128)(2,1)}, u32[]{:S(2)}, u32[]{:S(2)}) %collective-permute-start.5) | collective-permute-done | bytes 3670048 | tf_op jit(solution)/shard_map/ppermute | solution.py:216
  46.7 1.3 collective-permute-start.6
  47.9 31.8 %shard_map.17._ = f32[1,3,3584,3584]{3,2,1,0:T(8,128)} custom-call(bf16[3584,1024]{1,0:T(8,128)(2,1)S(1)} %bring.1.own_ref.refs_3_.refs_2_), custom_call_target="tpu_custom_call" | custom-call | flops 26306674688 | bytes 58720256 | tf_op jit(solution)/shard_map/pallas_call | solution.py:55
  79.7 0.0 collective-permute-done.2.part_ref
  79.7 1.6 slice.37
  81.3 1.3 slice.43
  82.7 1.2 slice.42
  83.8 1.0 slice.41
  84.8 0.8 slice.40
  85.7 0.8 slice.39
  86.4 0.8 slice.35
  87.3 2.0 collective-permute-start.7
  89.2 1.9 collective-permute-start.14
  91.1 4.2 %shard_map.18._ = f32[1,3,3584,3584]{3,2,1,0:T(8,128)} custom-call(bf16[256,1024]{1,0:T(8,128)(2,1)S(1)} %collective-permute-done.2.part_ref, bf16[3584,1024]{1,0:T(8,128)(2,1)S(1)} %bring.1.own_ref.refs_3_.refs_2_, f32[1,3,3584,3584]{3,2,1,0:T(8,128)} %shard_map.17._), custom_call_target="tpu_custom_call", output_to_operand_aliasing={{}: (2, {})} | custom-call | flops 1879048192 | bytes 4194304 | tf_op jit(solution)/shard_map/pallas_call | solution.py:55
  95.4 18.7 %shard_map.19._ = f32[1,3,3584,3584]{3,2,1,0:T(8,128)} custom-call(bf16[1792,1024]{1,0:T(8,128)(2,1)} %collective-permute-done.5.part_ref, bf16[3584,1024]{1,0:T(8,128)(2,1)S(1)} %bring.1.own_ref.refs_3_.refs_2_, f32[1,3,3584,3584]{3,2,1,0:T(8,128)} %shard_map.18._), custom_call_target="tpu_custom_call", output_to_operand_aliasing={{}: (2, {})} | custom-call | flops 13153337344 | bytes 29360128 | tf_op jit(solution)/shard_map/pallas_call | solution.py:55
  114.1 0.0 collective-permute-done.part_ref
  114.1 1.3 collective-permute-start.4
  115.4 0.0 collective-permute-done.8.part_ref
  115.4 1.3 collective-permute-start.10
  116.7 12.0 %shard_map.20._ = f32[1,3,3584,3584]{3,2,1,0:T(8,128)} custom-call(bf16[1024,1024]{1,0:T(8,128)(2,1)} %collective-permute-done.8.part_ref, bf16[3584,1024]{1,0:T(8,128)(2,1)S(1)} %bring.1.own_ref.refs_3_.refs_2_, f32[1,3,3584,3584]{3,2,1,0:T(8,128)} %shard_map.19._), custom_call_target="tpu_custom_call", output_to_operand_aliasing={{}: (2, {})} | custom-call | flops 7516192768 | bytes 16777216 | tf_op jit(solution)/shard_map/pallas_call | solution.py:55
  128.8 0.0 collective-permute-done.4.refs_0_
  128.8 1.7 collective-permute-start.13
  130.5 7.5 %shard_map.21.refs_4_ = f32[1,3,3584,3584]{3,2,1,0:T(8,128)} custom-call(bf16[512,1024]{1,0:T(8,128)(2,1)} %collective-permute-done.part_ref, bf16[3584,1024]{1,0:T(8,128)(2,1)S(1)} %bring.1.own_ref.refs_3_.refs_2_, f32[1,3,3584,3584]{3,2,1,0:T(8,128)} %shard_map.20._), custom_call_target="tpu_custom_call", output_to_operand_aliasing={{}: (2, {})} | custom-call | flops 3758096384 | bytes 8388608 | tf_op jit(solution)/shard_map/pallas_call | solution.py:55
  138.0 0.0 collective-permute-done.7.refs_2_
  138.0 1.6 collective-permute-start.12
  139.6 0.0 collective-permute-done.6.refs_1_.refs_0_
  139.6 1.5 collective-permute-start.11
  141.1 11.9 %shard_map.22._ = f32[1,3,3584,3584]{3,2,1,0:T(8,128)} custom-call(bf16[256,1024]{1,0:T(8,128)(2,1)S(1)} %collective-permute-done.4.refs_0_, bf16[1792,1024]{1,0:T(8,128)(2,1)} %collective-permute-done.6.refs_1_.refs_0_, bf16[1024,1024]{1,0:T(8,128)(2,1)} %collective-permute-done.7.refs_2_, ...), custom_call_target="tpu_custom_call", output_to_operand_aliasing={{}: (4, {})} | custom-call | flops 7516192768 | bytes 16777216 | tf_op jit(solution)/shard_map/pallas_call | solution.py:55
  153.0 2.3 %turn.1 = (bf16[1024,3584]{1,0:T(8,128)(2,1)S(1)}, f32[1,3,3584,3584]{3,2,1,0:T(8,128)}) custom-call(bf16[3584,1024]{1,0:T(8,128)(2,1)S(1)} %bring.1.own_ref.refs_3_.refs_2_, f32[1,3,3584,3584]{3,2,1,0:T(8,128)} %shard_map.22._), custom_call_target="tpu_custom_call", output_to_operand_aliasing={{1}: (1, {})} | custom-call | bytes 14680064 | tf_op jit(solution)/shard_map/turn/pallas_call | solution.py:95
  155.3 0.0 collective-permute-done.14.refs_1_
  155.3 1.3 collective-permute-start.1
  156.6 10.5 %shard_map.23.refs_4_ = f32[1,3,3584,3584]{3,2,1,0:T(8,128)} custom-call(bf16[1792,1024]{1,0:T(8,128)(2,1)} %collective-permute-done.6.refs_1_.refs_0_, bf16[848,1024]{1,0:T(8,128)(2,1)} %collective-permute-done.14.refs_1_, bf16[3584,1024]{1,0:T(8,128)(2,1)S(1)} %bring.1.own_ref.refs_3_.refs_2_, ...), custom_call_target="tpu_custom_call", output_to_operand_aliasing={{}: (3, {})} | custom-call | flops 6224347136 | bytes 13893632 | tf_op jit(solution)/shard_map/pallas_call | solution.py:55
  167.1 0.0 collective-permute-done.13.refs_2_
  167.1 1.4 collective-permute-start.9
  168.5 0.0 collective-permute-done.10.refs_1_.refs_0_
  168.5 1.4 collective-permute-start.3
  169.9 9.5 %shard_map.24.refs_3_ = f32[1,3,3584,3584]{3,2,1,0:T(8,128)} custom-call(bf16[1792,1024]{1,0:T(8,128)(2,1)} %collective-permute-done.6.refs_1_.refs_0_, bf16[1024,1024]{1,0:T(8,128)(2,1)} %collective-permute-done.10.refs_1_.refs_0_, bf16[640,1024]{1,0:T(8,128)(2,1)} %collective-permute-done.13.refs_2_, ...), custom_call_target="tpu_custom_call", output_to_operand_aliasing={{}: (4, {})} | custom-call | flops 4697620480 | bytes 10485760 | tf_op jit(solution)/shard_map/pallas_call | solution.py:55
  179.4 0.0 collective-permute-done.12.refs_1_
  179.4 5.4 %shard_map.25.refs_4_ = f32[1,3,3584,3584]{3,2,1,0:T(8,128)} custom-call(bf16[1024,1024]{1,0:T(8,128)(2,1)} %collective-permute-done.10.refs_1_.refs_0_, bf16[416,1024]{1,0:T(8,128)(2,1)} %collective-permute-done.12.refs_1_, bf16[1024,3584]{1,0:T(8,128)(2,1)S(1)} %get-tuple-element.9.refs_2_.refs_3_, ...), custom_call_target="tpu_custom_call", output_to_operand_aliasing={{}: (3, {})} | custom-call | flops 3053453312 | bytes 6815744 | tf_op jit(solution)/shard_map/pallas_call | solution.py:55
  184.8 0.0 collective-permute-done.11.refs_2_
  184.8 0.0 collective-permute-done.1.refs_1_.refs_0_
  184.9 5.0 %shard_map.26.refs_3_ = f32[1,3,3584,3584]{3,2,1,0:T(8,128)} custom-call(bf16[1024,1024]{1,0:T(8,128)(2,1)} %collective-permute-done.10.refs_1_.refs_0_, bf16[512,1024]{1,0:T(8,128)(2,1)} %collective-permute-done.1.refs_1_.refs_0_, bf16[272,1024]{1,0:T(8,128)(2,1)} %collective-permute-done.11.refs_2_, ...), custom_call_target="tpu_custom_call", output_to_operand_aliasing={{}: (4, {})} | custom-call | flops 1996488704 | bytes 4456448 | tf_op jit(solution)/shard_map/pallas_call | solution.py:55
  189.9 0.0 collective-permute-done.9.refs_1_
  189.9 3.6 %shard_map.27.refs_3_ = f32[1,3,3584,3584]{3,2,1,0:T(8,128)} custom-call(bf16[512,1024]{1,0:T(8,128)(2,1)} %collective-permute-done.1.refs_1_.refs_0_, bf16[208,1024]{1,0:T(8,128)(2,1)} %collective-permute-done.9.refs_1_, bf16[1024,3584]{1,0:T(8,128)(2,1)S(1)} %get-tuple-element.9.refs_2_.refs_3_, ...), custom_call_target="tpu_custom_call", output_to_operand_aliasing={{}: (3, {})} | custom-call | flops 1526726656 | bytes 3407872 | tf_op jit(solution)/shard_map/pallas_call | solution.py:55
  193.4 0.0 collective-permute-done.3.refs_1_
  193.4 3.3 %shard_map.28 = f32[1,3,3584,3584]{3,2,1,0:T(8,128)} custom-call(bf16[512,1024]{1,0:T(8,128)(2,1)} %collective-permute-done.1.refs_1_.refs_0_, bf16[176,1024]{1,0:T(8,128)(2,1)} %collective-permute-done.3.refs_1_, bf16[1024,3584]{1,0:T(8,128)(2,1)S(1)} %get-tuple-element.9.refs_2_.refs_3_, ...), custom_call_target="tpu_custom_call", output_to_operand_aliasing={{}: (3, {})} | custom-call | flops 1291845632 | bytes 2883584 | tf_op jit(solution)/shard_map/pallas_call | solution.py:55
Async XLA Ops:
  3.5 43.2 %collective-permute-start.5 = (bf16[1792,1024]{1,0:T(8,128)(2,1)S(1)}, bf16[1792,1024]{1,0:T(8,128)(2,1)}, u32[]{:S(2)}, u32[]{:S(2)}) collective-permute-start(bf16[1792,1024]{1,0:T(8,128)(2,1)S(1)} %slice.45), channel_id=1, source_target_pairs={{1,0},{2,1},{3,2},{0,3},{5,4},{6,5},{7,6},{4,7}} | collective-permute-start | bytes 11010056 | tf_op jit(solution)/shard_map/ppermute | solution.py:216
  7.3 72.4 %collective-permute-start.2 = (bf16[256,1024]{1,0:T(8,128)(2,1)S(1)}, bf16[256,1024]{1,0:T(8,128)(2,1)S(1)}, u32[]{:S(2)}, u32[]{:S(2)}) collective-permute-start(bf16[256,1024]{1,0:T(8,128)(2,1)S(1)} %slice.34), channel_id=1, source_target_pairs={{1,0},{2,1},{3,2},{0,3},{5,4},{6,5},{7,6},{4,7}} | collective-permute-start | bytes 1572872 | tf_op jit(solution)/shard_map/ppermute | solution.py:216
  9.5 105.9 %collective-permute-start.8 = (bf16[1024,1024]{1,0:T(8,128)(2,1)}, bf16[1024,1024]{1,0:T(8,128)(2,1)}, u32[]{:S(2)}, u32[]{:S(2)}) collective-permute-start(bf16[1024,1024]{1,0:T(8,128)(2,1)} %slice.46), channel_id=1, source_target_pairs={{1,0},{2,1},{3,2},{0,3},{5,4},{6,5},{7,6},{4,7}} | collective-permute-start | bytes 6291464 | tf_op jit(solution)/shard_map/ppermute | solution.py:216
  10.6 103.5 %collective-permute-start = (bf16[512,1024]{1,0:T(8,128)(2,1)}, bf16[512,1024]{1,0:T(8,128)(2,1)}, u32[]{:S(2)}, u32[]{:S(2)}) collective-permute-start(bf16[512,1024]{1,0:T(8,128)(2,1)} %slice.44), channel_id=1, source_target_pairs={{1,0},{2,1},{3,2},{0,3},{5,4},{6,5},{7,6},{4,7}} | collective-permute-start | bytes 3145736 | tf_op jit(solution)/shard_map/ppermute | solution.py:216
  46.7 93.0 %collective-permute-start.6 = (bf16[1792,1024]{1,0:T(8,128)(2,1)}, bf16[1792,1024]{1,0:T(8,128)(2,1)}, u32[]{:S(2)}, u32[]{:S(2)}) collective-permute-start(bf16[1792,1024]{1,0:T(8,128)(2,1)} %collective-permute-done.5.part_ref), channel_id=1, source_target_pairs={{1,0},{5,4}} | collective-permute-start | bytes 11010056 | tf_op jit(solution)/shard_map/ppermute | solution.py:216
  87.3 50.8 %collective-permute-start.7 = (bf16[1024,1024]{1,0:T(8,128)(2,1)}, bf16[1024,1024]{1,0:T(8,128)(2,1)}, u32[]{:S(2)}, u32[]{:S(2)}) collective-permute-start(bf16[1024,1024]{1,0:T(8,128)(2,1)} %slice.37), channel_id=1, source_target_pairs={{3,1},{7,5}} | collective-permute-start | bytes 6291464 | tf_op jit(solution)/shard_map/ppermute | solution.py:216
  89.2 66.1 %collective-permute-start.14 = (bf16[848,1024]{1,0:T(8,128)(2,1)}, bf16[848,1024]{1,0:T(8,128)(2,1)}, u32[]{:S(2)}, u32[]{:S(2)}) collective-permute-start(bf16[848,1024]{1,0:T(8,128)(2,1)} %slice.43), channel_id=1, source_target_pairs={{3,1},{7,5}} | collective-permute-start | bytes 5210120 | tf_op jit(solution)/shard_map/ppermute | solution.py:216
  114.1 14.6 %collective-permute-start.4 = (bf16[256,1024]{1,0:T(8,128)(2,1)S(1)}, bf16[256,1024]{1,0:T(8,128)(2,1)S(1)}, u32[]{:S(2)}, u32[]{:S(2)}) collective-permute-start(bf16[256,1024]{1,0:T(8,128)(2,1)S(1)} %collective-permute-done.2.part_ref), channel_id=1, source_target_pairs={{1,0},{5,4}} | collective-permute-start | bytes 1572872 | tf_op jit(solution)/shard_map/ppermute | solution.py:216
  115.4 53.1 %collective-permute-start.10 = (bf16[1024,1024]{1,0:T(8,128)(2,1)}, bf16[1024,1024]{1,0:T(8,128)(2,1)}, u32[]{:S(2)}, u32[]{:S(2)}) collective-permute-start(bf16[1024,1024]{1,0:T(8,128)(2,1)} %collective-permute-done.8.part_ref), channel_id=1, source_target_pairs={{1,0},{5,4}} | collective-permute-start | bytes 6291464 | tf_op jit(solution)/shard_map/ppermute | solution.py:216
  128.8 38.3 %collective-permute-start.13 = (bf16[640,1024]{1,0:T(8,128)(2,1)}, bf16[640,1024]{1,0:T(8,128)(2,1)}, u32[]{:S(2)}, u32[]{:S(2)}) collective-permute-start(bf16[640,1024]{1,0:T(8,128)(2,1)} %slice.42), channel_id=1, source_target_pairs={{3,1},{7,5}} | collective-permute-start | bytes 3932168 | tf_op jit(solution)/shard_map/ppermute | solution.py:216
  138.0 41.4 %collective-permute-start.12 = (bf16[416,1024]{1,0:T(8,128)(2,1)}, bf16[416,1024]{1,0:T(8,128)(2,1)}, u32[]{:S(2)}, u32[]{:S(2)}) collective-permute-start(bf16[416,1024]{1,0:T(8,128)(2,1)} %slice.41), channel_id=1, source_target_pairs={{3,1},{7,5}} | collective-permute-start | bytes 2555912 | tf_op jit(solution)/shard_map/ppermute | solution.py:216
  139.6 45.2 %collective-permute-start.11 = (bf16[272,1024]{1,0:T(8,128)(2,1)}, bf16[272,1024]{1,0:T(8,128)(2,1)}, u32[]{:S(2)}, u32[]{:S(2)}) collective-permute-start(bf16[272,1024]{1,0:T(8,128)(2,1)} %slice.40), channel_id=1, source_target_pairs={{3,1},{7,5}} | collective-permute-start | bytes 1671176 | tf_op jit(solution)/shard_map/ppermute | solution.py:216
  155.3 29.5 %collective-permute-start.1 = (bf16[512,1024]{1,0:T(8,128)(2,1)}, bf16[512,1024]{1,0:T(8,128)(2,1)}, u32[]{:S(2)}, u32[]{:S(2)}) collective-permute-start(bf16[512,1024]{1,0:T(8,128)(2,1)} %collective-permute-done.part_ref), channel_id=1, source_target_pairs={{1,0},{5,4}} | collective-permute-start | bytes 3145736 | tf_op jit(solution)/shard_map/ppermute | solution.py:216
  167.1 22.8 %collective-permute-start.9 = (bf16[208,1024]{1,0:T(8,128)(2,1)}, bf16[208,1024]{1,0:T(8,128)(2,1)}, u32[]{:S(2)}, u32[]{:S(2)}) collective-permute-start(bf16[208,1024]{1,0:T(8,128)(2,1)} %slice.39), channel_id=1, source_target_pairs={{3,1},{7,5}} | collective-permute-start | bytes 1277960 | tf_op jit(solution)/shard_map/ppermute | solution.py:216
  168.5 24.9 %collective-permute-start.3 = (bf16[176,1024]{1,0:T(8,128)(2,1)}, bf16[176,1024]{1,0:T(8,128)(2,1)}, u32[]{:S(2)}, u32[]{:S(2)}) collective-permute-start(bf16[176,1024]{1,0:T(8,128)(2,1)} %slice.35), channel_id=1, source_target_pairs={{3,1},{7,5}} | collective-permute-start | bytes 1081352 | tf_op jit(solution)/shard_map/ppermute | solution.py:216

commit v7 on v6

--- a/solution.py
+++ b/solution.py
@@ -12,10 +12,10 @@
 FAR = [(3, 1)]
 PASS = [(1, 0)]
 PARTS = [(0, 256), (256, 1792), (2048, 1024), (3072, 512)]
-FARS = [(0, 1024), (1024, 848), (1872, 640), (2512, 416), (2928, 272), (3200, 208), (3408, 176)]
+FARS = [(0, 816), (816, 768), (1584, 768), (2352, 464), (2816, 272), (3088, 192), (3280, 160), (3440, 144)]
 TURN_AFTER = 0
 DEPTH = 3
-FEW = 448
+FEW = 464
 
 
 def dot_t(x, y):
@@ -66,20 +66,49 @@
     )(*args)
 
 
-def bring(a):
-    def kernel(a_ref, own_ref, sem):
-        load(a_ref, own_ref, sem)
+def bring(a, first, size, grant):
+    def kernel(a_ref, rows_ref, sem):
+        load(a_ref.at[pl.ds(first, size), :], rows_ref, sem)
 
     return pl.pallas_call(
         kernel,
         in_specs=[pl.BlockSpec(memory_space=pl.ANY)],
         out_specs=pl.BlockSpec(memory_space=pltpu.VMEM),
-        out_shape=pltpu.VMEM(a.shape, a.dtype),
+        out_shape=pltpu.VMEM((size, a.shape[1]), a.dtype),
         scratch_shapes=[pltpu.SemaphoreType.DMA],
-        cost_estimate=pl.CostEstimate(flops=0, bytes_accessed=4 * a.size, transcendentals=0),
-        compiler_params=pltpu.CompilerParams(vmem_limit_bytes=51 << 20),
+        cost_estimate=pl.CostEstimate(flops=0, bytes_accessed=4 * size * a.shape[1], transcendentals=0),
+        compiler_params=pltpu.CompilerParams(vmem_limit_bytes=grant),
         name="bring",
     )(a)
+
+
+def cut(own):
+    depth = own.shape[1]
+
+    def kernel(own_ref, *refs):
+        piece_refs, sem = refs[:-1], refs[-1]
+
+        @pl.when(lax.axis_index("row") == FAR[0][0])
+        def _():
+            copies = [
+                pltpu.make_async_copy(own_ref.at[pl.ds(first, size), :], piece_ref, sem.at[k])
+                for k, ((first, size), piece_ref) in enumerate(zip(FARS, piece_refs))
+            ]
+            for copy in copies:
+                copy.start()
+            for copy in copies:
+                copy.wait()
+
+    return pl.pallas_call(
+        kernel,
+        in_specs=[pl.BlockSpec(memory_space=pltpu.VMEM)],
+        out_specs=[pl.BlockSpec(memory_space=pl.ANY)] * len(FARS),
+        out_shape=[jax.ShapeDtypeStruct((size, depth), own.dtype) for _, size in FARS],
+        scratch_shapes=[pltpu.SemaphoreType.DMA((len(FARS),))],
+        cost_estimate=pl.CostEstimate(flops=0, bytes_accessed=4 * own.size, transcendentals=0),
+        compiler_params=pltpu.CompilerParams(vmem_limit_bytes=32 << 20),
+        name="cut",
+    )(own)
 
 
 def turn(own, out):
@@ -219,14 +248,14 @@
         return a[chunk[0]:chunk[0] + chunk[1]]
 
     def local(a):
-        head = rows_of(a, PARTS[0])
+        head = bring(a, *PARTS[0], 58 << 20)
         parts = [send(head, NEXT)]
-        own = bring(a)
+        own = bring(a, 0, a.shape[0], 51 << 20)
         parts += [send(rows_of(own, PARTS[k]), NEXT) for k in range(1, len(PARTS))]
         out = diag(own)
         passed = [send(part, PASS) for part in parts]
-        later, _ = lax.optimization_barrier((own, parts[0]))
-        far = [send(rows_of(later, chunk), FAR) for chunk in FARS]
+        pieces = cut(own)
+        far = [send(piece, FAR) for piece in pieces]
         for k, chunk in enumerate(PARTS):
             out = slot1(*chunk, parts[k], own, out)
         for j, chunk in enumerate(FARS):

time: 198 us -> 216 us (1.091)
  the two profiles are of different devices: /device:TPU:0 before, /device:TPU:1 now
where the time goes in v7:
time: 216 us; the launch traced here: 215 us
  Pallas kernels  132 us (61%)
  waiting for transfers between devices  47.1 us (22%)
  starting transfers between devices  24 us (11%)
  local copies, waits for them, and re-layouts  11.8 us (5%)
    pallas_call x13, Pallas kernels, call(): pl.pallas_call(kernel, in_specs=[pl.BlockSpec(memory_space=space) for _,...  125 us
    ppermute x16, waiting for transfers between devices, send(): return lax.ppermute(a, 'row', pairs)  47.1 us
    ppermute x16, starting transfers between devices, send(): return lax.ppermute(a, 'row', pairs)  24 us
    unnamed x8, local copies, waits for them, and re-layouts  6.03 us
    slice x3, local copies, waits for them, and re-layouts, rows_of(): return a[chunk[0]:chunk[0] + chunk[1]]  5.78 us
  transfers between devices with their start and end apart: 16, of which 1 were waited for; matrix products, arithmetic and copies ran while one was open for 3% of the time, Pallas kernels for 58%

profile of v7, /device:TPU:1, one launch (start us, length us, event | category | flops | bytes accessed | tf_op | source)
XLA Modules:
  0.0 215.0 jit_solution(7628101338020189560)
XLA Ops:
  0.0 3.1 %bring.2.own_ref.refs_3_.refs_2_ = bf16[3584,1024]{1,0:T(8,128)(2,1)S(1)} custom-call(bf16[3584,1024]{1,0:T(8,128)(2,1)} %a_ref.3), custom_call_target="tpu_custom_call" | custom-call | bytes 14680064 | tf_op jit(solution)/shard_map/bring/pallas_call | solution.py:73
  3.1 0.0 copy-start
  3.1 2.9 %copy-done = bf16[3584,1024]{1,0:T(8,128)(2,1)} copy-done((bf16[3584,1024]{1,0:T(8,128)(2,1)}, bf16[3584,1024]{1,0:T(8,128)(2,1)S(1)}, u32[]{:S(2)}) %copy-start) | copy-done | bytes 7340056
  6.0 0.4 slice.13
  6.4 0.0 collective-permute-start.5
  6.5 1.1 bring.3
  7.5 2.4 %collective-permute-start.3 = (bf16[256,1024]{1,0:T(8,128)(2,1)S(1)}, bf16[256,1024]{1,0:T(8,128)(2,1)}, u32[]{:S(2)}, u32[]{:S(2)}) collective-permute-start(bf16[256,1024]{1,0:T(8,128)(2,1)S(1)} %bring.3), channel_id=1, source_target_pairs={{1,0},{2,1},{3,2},{0,3},{5,4},{6,5},{7,6},{4,7}} | collective-permute-start | bytes 1572872 | tf_op jit(solution)/shard_map/ppermute | solution.py:245
  9.9 3.1 %slice.14 = bf16[1024,1024]{1,0:T(8,128)(2,1)} slice(bf16[3584,1024]{1,0:T(8,128)(2,1)} %copy-done), slice={[2048:3072], [0:1024]} | slice | bytes 4194304 | tf_op jit(solution)/shard_map/slice | solution.py:248
  13.0 0.7 collective-permute-start.8
  13.7 2.3 %slice.12 = bf16[512,1024]{1,0:T(8,128)(2,1)} slice(bf16[3584,1024]{1,0:T(8,128)(2,1)} %copy-done), slice={[3072:3584], [0:1024]} | slice | bytes 2097152 | tf_op jit(solution)/shard_map/slice | solution.py:248
  16.0 0.0 collective-permute-start
  16.1 0.0 copy-start.1
  16.1 3.1 %copy-done.1 = bf16[3584,1024]{1,0:T(8,128)(2,1)S(1)} copy-done((bf16[3584,1024]{1,0:T(8,128)(2,1)S(1)}, bf16[3584,1024]{1,0:T(8,128)(2,1)}, u32[]{:S(2)}) %copy-start.1) | copy-done | bytes 7340056
  19.1 0.1 cut.1
  19.2 1.3 collective-permute-start.7
  20.5 47.1 %collective-permute-done.5.part_ref = bf16[1792,1024]{1,0:T(8,128)(2,1)} collective-permute-done((bf16[1792,1024]{1,0:T(8,128)(2,1)S(1)}, bf16[1792,1024]{1,0:T(8,128)(2,1)}, u32[]{:S(2)}, u32[]{:S(2)}) %collective-permute-start.5) | collective-permute-done | bytes 3670048 | tf_op jit(solution)/shard_map/ppermute | solution.py:245
  67.6 3.2 %collective-permute-start.6 = (bf16[1792,1024]{1,0:T(8,128)(2,1)}, bf16[1792,1024]{1,0:T(8,128)(2,1)}, u32[]{:S(2)}, u32[]{:S(2)}) collective-permute-start(bf16[1792,1024]{1,0:T(8,128)(2,1)} %collective-permute-done.5.part_ref), channel_id=1, source_target_pairs={{1,0},{5,4}} | collective-permute-start | bytes 11010056 | tf_op jit(solution)/shard_map/ppermute | solution.py:245
  70.8 31.7 %shard_map.17._ = f32[1,3,3584,3584]{3,2,1,0:T(8,128)} custom-call(bf16[3584,1024]{1,0:T(8,128)(2,1)S(1)} %copy-done.1), custom_call_target="tpu_custom_call" | custom-call | flops 26306674688 | bytes 58720256 | tf_op jit(solution)/shard_map/pallas_call | solution.py:55
  102.6 0.0 collective-permute-done.3.part_ref
  102.6 2.1 collective-permute-start.4
  104.7 5.2 %shard_map.18._ = f32[1,3,3584,3584]{3,2,1,0:T(8,128)} custom-call(bf16[256,1024]{1,0:T(8,128)(2,1)} %collective-permute-done.3.part_ref, bf16[3584,1024]{1,0:T(8,128)(2,1)S(1)} %copy-done.1, f32[1,3,3584,3584]{3,2,1,0:T(8,128)} %shard_map.17._), custom_call_target="tpu_custom_call", output_to_operand_aliasing={{}: (2, {})} | custom-call | flops 1879048192 | bytes 4194304 | tf_op jit(solution)/shard_map/pallas_call | solution.py:55
  109.9 18.7 %shard_map.19._ = f32[1,3,3584,3584]{3,2,1,0:T(8,128)} custom-call(bf16[1792,1024]{1,0:T(8,128)(2,1)} %collective-permute-done.5.part_ref, bf16[3584,1024]{1,0:T(8,128)(2,1)S(1)} %copy-done.1, f32[1,3,3584,3584]{3,2,1,0:T(8,128)} %shard_map.18._), custom_call_target="tpu_custom_call", output_to_operand_aliasing={{}: (2, {})} | custom-call | flops 13153337344 | bytes 29360128 | tf_op jit(solution)/shard_map/pallas_call | solution.py:55
  128.7 0.0 collective-permute-done.part_ref
  128.7 1.3 collective-permute-start.15
  130.0 0.0 collective-permute-done.4.refs_0_
  130.0 1.3 collective-permute-start.14
  131.3 0.0 collective-permute-done.8.part_ref
  131.3 2.6 %collective-permute-start.11 = (bf16[1024,1024]{1,0:T(8,128)(2,1)}, bf16[1024,1024]{1,0:T(8,128)(2,1)}, u32[]{:S(2)}, u32[]{:S(2)}) collective-permute-start(bf16[1024,1024]{1,0:T(8,128)(2,1)} %collective-permute-done.8.part_ref), channel_id=1, source_target_pairs={{1,0},{5,4}} | collective-permute-start | bytes 6291464 | tf_op jit(solution)/shard_map/ppermute | solution.py:245
  133.9 12.0 %shard_map.20._ = f32[1,3,3584,3584]{3,2,1,0:T(8,128)} custom-call(bf16[1024,1024]{1,0:T(8,128)(2,1)} %collective-permute-done.8.part_ref, bf16[3584,1024]{1,0:T(8,128)(2,1)S(1)} %copy-done.1, f32[1,3,3584,3584]{3,2,1,0:T(8,128)} %shard_map.19._), custom_call_target="tpu_custom_call", output_to_operand_aliasing={{}: (2, {})} | custom-call | flops 7516192768 | bytes 16777216 | tf_op jit(solution)/shard_map/pallas_call | solution.py:55
  146.0 7.5 %shard_map.21.refs_4_ = f32[1,3,3584,3584]{3,2,1,0:T(8,128)} custom-call(bf16[512,1024]{1,0:T(8,128)(2,1)} %collective-permute-done.part_ref, bf16[3584,1024]{1,0:T(8,128)(2,1)S(1)} %copy-done.1, f32[1,3,3584,3584]{3,2,1,0:T(8,128)} %shard_map.20._), custom_call_target="tpu_custom_call", output_to_operand_aliasing={{}: (2, {})} | custom-call | flops 3758096384 | bytes 8388608 | tf_op jit(solution)/shard_map/pallas_call | solution.py:55
  153.5 0.0 collective-permute-done.7.refs_2_
  153.5 1.3 collective-permute-start.13
  154.8 0.0 collective-permute-done.6.refs_1_.refs_0_
  154.8 0.0 slice-start
  154.8 0.0 slice-start.1
  154.8 1.6 collective-permute-start.12
  156.4 10.7 %shard_map.22._ = f32[1,3,3584,3584]{3,2,1,0:T(8,128)} custom-call(bf16[256,1024]{1,0:T(8,128)(2,1)} %collective-permute-done.4.refs_0_, bf16[1792,1024]{1,0:T(8,128)(2,1)} %collective-permute-done.6.refs_1_.refs_0_, bf16[816,1024]{1,0:T(8,128)(2,1)} %collective-permute-done.7.refs_2_, ...), custom_call_target="tpu_custom_call", output_to_operand_aliasing={{}: (4, {})} | custom-call | flops 5989466112 | bytes 13369344 | tf_op jit(solution)/shard_map/pallas_call | solution.py:55
  167.1 0.0 slice-done
  167.1 0.0 slice-done.1
  167.2 2.3 %turn.1 = (bf16[1024,3584]{1,0:T(8,128)(2,1)S(1)}, f32[1,3,3584,3584]{3,2,1,0:T(8,128)}) custom-call(bf16[3584,1024]{1,0:T(8,128)(2,1)S(1)} %bitcast.1, f32[1,3,3584,3584]{3,2,1,0:T(8,128)} %shard_map.22._), custom_call_target="tpu_custom_call", output_to_operand_aliasing={{1}: (1, {})} | custom-call | bytes 14680064 | tf_op jit(solution)/shard_map/turn/pallas_call | solution.py:124
  169.5 0.0 collective-permute-done.15.refs_1_
  169.5 2.3 %collective-permute-start.1 = (bf16[512,1024]{1,0:T(8,128)(2,1)}, bf16[512,1024]{1,0:T(8,128)(2,1)}, u32[]{:S(2)}, u32[]{:S(2)}) collective-permute-start(bf16[512,1024]{1,0:T(8,128)(2,1)} %collective-permute-done.part_ref), channel_id=1, source_target_pairs={{1,0},{5,4}} | collective-permute-start | bytes 3145736 | tf_op jit(solution)/shard_map/ppermute | solution.py:245
  171.8 9.8 %shard_map.23.refs_4_ = f32[1,3,3584,3584]{3,2,1,0:T(8,128)} custom-call(bf16[1792,1024]{1,0:T(8,128)(2,1)} %collective-permute-done.6.refs_1_.refs_0_, bf16[768,1024]{1,0:T(8,128)(2,1)} %collective-permute-done.15.refs_1_, bf16[3584,1024]{1,0:T(8,128)(2,1)S(1)} %bitcast.1, ...), custom_call_target="tpu_custom_call", output_to_operand_aliasing={{}: (3, {})} | custom-call | flops 5637144576 | bytes 12582912 | tf_op jit(solution)/shard_map/pallas_call | solution.py:55
  181.5 0.0 collective-permute-done.14.refs_2_
  181.5 1.3 collective-permute-start.10
  182.8 0.0 collective-permute-done.11.refs_1_.refs_0_
  182.9 1.3 collective-permute-start.9
  184.2 9.8 %shard_map.24.refs_3_ = f32[1,3,3584,3584]{3,2,1,0:T(8,128)} custom-call(bf16[1792,1024]{1,0:T(8,128)(2,1)} %collective-permute-done.6.refs_1_.refs_0_, bf16[1024,1024]{1,0:T(8,128)(2,1)} %collective-permute-done.11.refs_1_.refs_0_, bf16[768,1024]{1,0:T(8,128)(2,1)} %collective-permute-done.14.refs_2_, ...), custom_call_target="tpu_custom_call", output_to_operand_aliasing={{}: (4, {})} | custom-call | flops 5637144576 | bytes 12582912 | tf_op jit(solution)/shard_map/pallas_call | solution.py:55
  193.9 0.0 collective-permute-done.13.refs_1_
  193.9 1.3 collective-permute-start.2
  195.2 5.8 %shard_map.25.refs_4_ = f32[1,3,3584,3584]{3,2,1,0:T(8,128)} custom-call(bf16[1024,1024]{1,0:T(8,128)(2,1)} %collective-permute-done.11.refs_1_.refs_0_, bf16[464,1024]{1,0:T(8,128)(2,1)} %collective-permute-done.13.refs_1_, bf16[1024,3584]{1,0:T(8,128)(2,1)S(1)} %get-tuple-element.17.refs_2_.refs_3_, ...), custom_call_target="tpu_custom_call", output_to_operand_aliasing={{}: (3, {})} | custom-call | flops 3405774848 | bytes 7602176 | tf_op jit(solution)/shard_map/pallas_call | solution.py:55
  201.1 0.0 collective-permute-done.12.refs_2_
  201.1 0.0 collective-permute-done.1.refs_1_.refs_0_
  201.1 4.1 %shard_map.26.refs_3_ = f32[1,3,3584,3584]{3,2,1,0:T(8,128)} custom-call(bf16[1024,1024]{1,0:T(8,128)(2,1)} %collective-permute-done.11.refs_1_.refs_0_, bf16[512,1024]{1,0:T(8,128)(2,1)} %collective-permute-done.1.refs_1_.refs_0_, bf16[272,1024]{1,0:T(8,128)(2,1)} %collective-permute-done.12.refs_2_, ...), custom_call_target="tpu_custom_call", output_to_operand_aliasing={{}: (4, {})} | custom-call | flops 1996488704 | bytes 4456448 | tf_op jit(solution)/shard_map/pallas_call | solution.py:55
  205.2 0.0 collective-permute-done.10.refs_1_
  205.3 3.4 %shard_map.27.refs_3_ = f32[1,3,3584,3584]{3,2,1,0:T(8,128)} custom-call(bf16[512,1024]{1,0:T(8,128)(2,1)} %collective-permute-done.1.refs_1_.refs_0_, bf16[192,1024]{1,0:T(8,128)(2,1)} %collective-permute-done.10.refs_1_, bf16[1024,3584]{1,0:T(8,128)(2,1)S(1)} %get-tuple-element.17.refs_2_.refs_3_, ...), custom_call_target="tpu_custom_call", output_to_operand_aliasing={{}: (3, {})} | custom-call | flops 1409286144 | bytes 3145728 | tf_op jit(solution)/shard_map/pallas_call | solution.py:55
  208.7 0.0 collective-permute-done.9.refs_1_
  208.7 3.2 %shard_map.28.refs_3_ = f32[1,3,3584,3584]{3,2,1,0:T(8,128)} custom-call(bf16[512,1024]{1,0:T(8,128)(2,1)} %collective-permute-done.1.refs_1_.refs_0_, bf16[160,1024]{1,0:T(8,128)(2,1)} %collective-permute-done.9.refs_1_, bf16[1024,3584]{1,0:T(8,128)(2,1)S(1)} %get-tuple-element.17.refs_2_.refs_3_, ...), custom_call_target="tpu_custom_call", output_to_operand_aliasing={{}: (3, {})} | custom-call | flops 1174405120 | bytes 2621440 | tf_op jit(solution)/shard_map/pallas_call | solution.py:55
  211.9 0.0 collective-permute-done.2.refs_1_
  211.9 3.0 %shard_map.29 = f32[1,3,3584,3584]{3,2,1,0:T(8,128)} custom-call(bf16[512,1024]{1,0:T(8,128)(2,1)} %collective-permute-done.1.refs_1_.refs_0_, bf16[144,1024]{1,0:T(8,128)(2,1)} %collective-permute-done.2.refs_1_, bf16[1024,3584]{1,0:T(8,128)(2,1)S(1)} %get-tuple-element.17.refs_2_.refs_3_, ...), custom_call_target="tpu_custom_call", output_to_operand_aliasing={{}: (3, {})} | custom-call | flops 1056964608 | bytes 2359296 | tf_op jit(solution)/shard_map/pallas_call | solution.py:55
  (1 shorter events, 0.0 us)
Async XLA Ops:
  3.1 2.9 %copy-start = (bf16[3584,1024]{1,0:T(8,128)(2,1)}, bf16[3584,1024]{1,0:T(8,128)(2,1)S(1)}, u32[]{:S(2)}) copy-start(bf16[3584,1024]{1,0:T(8,128)(2,1)S(1)} %bring.2.own_ref.refs_3_.refs_2_) | copy-start | bytes 22020100
  6.4 61.2 %collective-permute-start.5 = (bf16[1792,1024]{1,0:T(8,128)(2,1)S(1)}, bf16[1792,1024]{1,0:T(8,128)(2,1)}, u32[]{:S(2)}, u32[]{:S(2)}) collective-permute-start(bf16[1792,1024]{1,0:T(8,128)(2,1)S(1)} %slice.13), channel_id=1, source_target_pairs={{1,0},{2,1},{3,2},{0,3},{5,4},{6,5},{7,6},{4,7}} | collective-permute-start | bytes 11010056 | tf_op jit(solution)/shard_map/ppermute | solution.py:245
  7.5 95.0 %collective-permute-start.3 = (bf16[256,1024]{1,0:T(8,128)(2,1)S(1)}, bf16[256,1024]{1,0:T(8,128)(2,1)}, u32[]{:S(2)}, u32[]{:S(2)}) collective-permute-start(bf16[256,1024]{1,0:T(8,128)(2,1)S(1)} %bring.3), channel_id=1, source_target_pairs={{1,0},{2,1},{3,2},{0,3},{5,4},{6,5},{7,6},{4,7}} | collective-permute-start | bytes 1572872 | tf_op jit(solution)/shard_map/ppermute | solution.py:245
  13.0 118.3 %collective-permute-start.8 = (bf16[1024,1024]{1,0:T(8,128)(2,1)}, bf16[1024,1024]{1,0:T(8,128)(2,1)}, u32[]{:S(2)}, u32[]{:S(2)}) collective-permute-start(bf16[1024,1024]{1,0:T(8,128)(2,1)} %slice.14), channel_id=1, source_target_pairs={{1,0},{2,1},{3,2},{0,3},{5,4},{6,5},{7,6},{4,7}} | collective-permute-start | bytes 6291464 | tf_op jit(solution)/shard_map/ppermute | solution.py:245
  16.0 112.6 %collective-permute-start = (bf16[512,1024]{1,0:T(8,128)(2,1)}, bf16[512,1024]{1,0:T(8,128)(2,1)}, u32[]{:S(2)}, u32[]{:S(2)}) collective-permute-start(bf16[512,1024]{1,0:T(8,128)(2,1)} %slice.12), channel_id=1, source_target_pairs={{1,0},{2,1},{3,2},{0,3},{5,4},{6,5},{7,6},{4,7}} | collective-permute-start | bytes 3145736 | tf_op jit(solution)/shard_map/ppermute | solution.py:245
  16.1 3.1 %copy-start.1 = (bf16[3584,1024]{1,0:T(8,128)(2,1)S(1)}, bf16[3584,1024]{1,0:T(8,128)(2,1)}, u32[]{:S(2)}) copy-start(bf16[3584,1024]{1,0:T(8,128)(2,1)} %copy-done) | copy-start | bytes 22020100
  19.2 134.3 %collective-permute-start.7 = (bf16[816,1024]{1,0:T(8,128)(2,1)}, bf16[816,1024]{1,0:T(8,128)(2,1)}, u32[]{:S(2)}, u32[]{:S(2)}) collective-permute-start(bf16[816,1024]{1,0:T(8,128)(2,1)} %get-tuple-element.16), channel_id=1, source_target_pairs={{3,1},{7,5}} | collective-permute-start | bytes 5013512 | tf_op jit(solution)/shard_map/ppermute | solution.py:245
  67.6 87.2 %collective-permute-start.6 = (bf16[1792,1024]{1,0:T(8,128)(2,1)}, bf16[1792,1024]{1,0:T(8,128)(2,1)}, u32[]{:S(2)}, u32[]{:S(2)}) collective-permute-start(bf16[1792,1024]{1,0:T(8,128)(2,1)} %collective-permute-done.5.part_ref), channel_id=1, source_target_pairs={{1,0},{5,4}} | collective-permute-start | bytes 11010056 | tf_op jit(solution)/shard_map/ppermute | solution.py:245
  102.6 27.4 %collective-permute-start.4 = (bf16[256,1024]{1,0:T(8,128)(2,1)}, bf16[256,1024]{1,0:T(8,128)(2,1)}, u32[]{:S(2)}, u32[]{:S(2)}) collective-permute-start(bf16[256,1024]{1,0:T(8,128)(2,1)} %collective-permute-done.3.part_ref), channel_id=1, source_target_pairs={{1,0},{5,4}} | collective-permute-start | bytes 1572872 | tf_op jit(solution)/shard_map/ppermute | solution.py:245
  128.7 40.8 %collective-permute-start.15 = (bf16[768,1024]{1,0:T(8,128)(2,1)}, bf16[768,1024]{1,0:T(8,128)(2,1)}, u32[]{:S(2)}, u32[]{:S(2)}) collective-permute-start(bf16[768,1024]{1,0:T(8,128)(2,1)} %get-tuple-element.23), channel_id=1, source_target_pairs={{3,1},{7,5}} | collective-permute-start | bytes 4718600 | tf_op jit(solution)/shard_map/ppermute | solution.py:245
  130.0 51.5 %collective-permute-start.14 = (bf16[768,1024]{1,0:T(8,128)(2,1)}, bf16[768,1024]{1,0:T(8,128)(2,1)}, u32[]{:S(2)}, u32[]{:S(2)}) collective-permute-start(bf16[768,1024]{1,0:T(8,128)(2,1)} %get-tuple-element.22), channel_id=1, source_target_pairs={{3,1},{7,5}} | collective-permute-start | bytes 4718600 | tf_op jit(solution)/shard_map/ppermute | solution.py:245
  131.3 51.5 %collective-permute-start.11 = (bf16[1024,1024]{1,0:T(8,128)(2,1)}, bf16[1024,1024]{1,0:T(8,128)(2,1)}, u32[]{:S(2)}, u32[]{:S(2)}) collective-permute-start(bf16[1024,1024]{1,0:T(8,128)(2,1)} %collective-permute-done.8.part_ref), channel_id=1, source_target_pairs={{1,0},{5,4}} | collective-permute-start | bytes 6291464 | tf_op jit(solution)/shard_map/ppermute | solution.py:245
  153.5 40.4 %collective-permute-start.13 = (bf16[464,1024]{1,0:T(8,128)(2,1)}, bf16[464,1024]{1,0:T(8,128)(2,1)}, u32[]{:S(2)}, u32[]{:S(2)}) collective-permute-start(bf16[464,1024]{1,0:T(8,128)(2,1)} %get-tuple-element.21), channel_id=1, source_target_pairs={{3,1},{7,5}} | collective-permute-start | bytes 2850824 | tf_op jit(solution)/shard_map/ppermute | solution.py:245
  154.8 12.3 %slice-start = ((s8[7340032]{0:T(1024)(128)(4,1)}), s8[4194304]{0:T(1024)(128)(4,1)S(1)}, s32[]{:S(2)}) async-start(s8[7340032]{0:T(1024)(128)(4,1)} %bitcast), calls=%async_computation | async-start | bytes 8388608
  154.8 12.3 %slice-start.1 = ((s8[7340032]{0:T(1024)(128)(4,1)}), s8[3145728]{0:T(1024)(128)(4,1)S(1)}, s32[]{:S(2)}) async-start(s8[7340032]{0:T(1024)(128)(4,1)} %bitcast), calls=%async_computation.1 | async-start | bytes 6291456
  154.8 46.2 %collective-permute-start.12 = (bf16[272,1024]{1,0:T(8,128)(2,1)}, bf16[272,1024]{1,0:T(8,128)(2,1)}, u32[]{:S(2)}, u32[]{:S(2)}) collective-permute-start(bf16[272,1024]{1,0:T(8,128)(2,1)} %get-tuple-element.20), channel_id=1, source_target_pairs={{3,1},{7,5}} | collective-permute-start | bytes 1671176 | tf_op jit(solution)/shard_map/ppermute | solution.py:245
  169.5 31.6 %collective-permute-start.1 = (bf16[512,1024]{1,0:T(8,128)(2,1)}, bf16[512,1024]{1,0:T(8,128)(2,1)}, u32[]{:S(2)}, u32[]{:S(2)}) collective-permute-start(bf16[512,1024]{1,0:T(8,128)(2,1)} %collective-permute-done.part_ref), channel_id=1, source_target_pairs={{1,0},{5,4}} | collective-permute-start | bytes 3145736 | tf_op jit(solution)/shard_map/ppermute | solution.py:245
  181.5 23.7 %collective-permute-start.10 = (bf16[192,1024]{1,0:T(8,128)(2,1)}, bf16[192,1024]{1,0:T(8,128)(2,1)}, u32[]{:S(2)}, u32[]{:S(2)}) collective-permute-start(bf16[192,1024]{1,0:T(8,128)(2,1)} %get-tuple-element.19), channel_id=1, source_target_pairs={{3,1},{7,5}} | collective-permute-start | bytes 1179656 | tf_op jit(solution)/shard_map/ppermute | solution.py:245
  182.9 25.8 %collective-permute-start.9 = (bf16[160,1024]{1,0:T(8,128)(2,1)}, bf16[160,1024]{1,0:T(8,128)(2,1)}, u32[]{:S(2)}, u32[]{:S(2)}) collective-permute-start(bf16[160,1024]{1,0:T(8,128)(2,1)} %get-tuple-element.18), channel_id=1, source_target_pairs={{3,1},{7,5}} | collective-permute-start | bytes 983048 | tf_op jit(solution)/shard_map/ppermute | solution.py:245
  193.9 17.9 %collective-permute-start.2 = (bf16[144,1024]{1,0:T(8,128)(2,1)}, bf16[144,1024]{1,0:T(8,128)(2,1)}, u32[]{:S(2)}, u32[]{:S(2)}) collective-permute-start(bf16[144,1024]{1,0:T(8,128)(2,1)} %get-tuple-element.15), channel_id=1, source_target_pairs={{3,1},{7,5}} | collective-permute-start | bytes 884744 | tf_op jit(solution)/shard_map/ppermute | solution.py:245

commit v8 on v7

--- a/solution.py
+++ b/solution.py
@@ -11,7 +11,8 @@
 NEXT = [(1, 0), (2, 1), (3, 2), (0, 3)]
 FAR = [(3, 1)]
 PASS = [(1, 0)]
-PARTS = [(0, 256), (256, 1792), (2048, 1024), (3072, 512)]
+PARTS = [(0, 96), (96, 1952), (2048, 1024), (3072, 512)]
+GROUPS = [[0, 1], [2], [3]]
 FARS = [(0, 816), (816, 768), (1584, 768), (2352, 464), (2816, 272), (3088, 192), (3280, 160), (3440, 144)]
 TURN_AFTER = 0
 DEPTH = 3
@@ -148,14 +149,17 @@
     return call(kernel, rows, rows, depth, out, [(own, pltpu.VMEM)], [pltpu.VMEM((DEPTH, HIGH, WIDE), jnp.float32)])
 
 
-def slot1(first, size, part, own, out):
+def slot1(group, parts, own, out):
     rows, depth = own.shape
-    wide = WIDE if size % WIDE == 0 else WIDE // 2
-    tall = size // wide
-
-    def kernel(part_ref, own_ref, _, out_ref, sem, load_sem, held, buf):
+    first = PARTS[group[0]][0]
+    size = sum(PARTS[k][1] for k in group)
+    tall = size // WIDE
+
+    def kernel(*refs):
+        part_refs, (own_ref, _, out_ref, sem, load_sem, held, buf) = refs[:len(group)], refs[len(group):]
         p = lax.axis_index("row")
-        load(part_ref, held, load_sem)
+        for k, part_ref in zip(group, part_refs):
+            load(part_ref, held.at[pl.ds(PARTS[k][0] - first, PARTS[k][1]), :], load_sem)
 
         @pl.when(p < 3)
         def _():
@@ -168,13 +172,14 @@
         @pl.when(p == 3)
         def _():
             stream(
-                rows // HIGH * tall, buf.at[:, :, :wide], sem,
-                lambda s: dot_t(tiles(own_ref, s // tall, HIGH), tiles(held, lax.rem(s, tall), wide)),
-                lambda s: out_ref.at[0, 1, pl.ds(s // tall * HIGH, HIGH), pl.ds(first + lax.rem(s, tall) * wide, wide)],
+                rows // HIGH * tall, buf.at[:, :HIGH], sem,
+                lambda s: dot_t(tiles(own_ref, s // tall, HIGH), tiles(held, lax.rem(s, tall), WIDE)),
+                lambda s: out_ref.at[0, 1, pl.ds(s // tall * HIGH, HIGH), pl.ds(first + lax.rem(s, tall) * WIDE, WIDE)],
             )
 
-    scratch = [pltpu.VMEM((size, depth), jnp.bfloat16), pltpu.VMEM((DEPTH, HIGH, WIDE), jnp.float32)]
-    return call(kernel, size, rows, depth, out, [(part, pl.ANY), (own, pltpu.VMEM)], scratch)
+    scratch = [pltpu.VMEM((size, depth), jnp.bfloat16), pltpu.VMEM((DEPTH, max(size, HIGH), WIDE), jnp.float32)]
+    refs = [(part, pl.ANY) for part in parts] + [(own, pltpu.VMEM)]
+    return call(kernel, size, rows, depth, out, refs, scratch)
 
 
 def slot2(first, size, passed, far, own, out):
@@ -199,7 +204,15 @@
 
         @pl.when(p == 1)
         def _():
-            load(far_ref, held, load_sem)
+            half = size // 32 * 16
+            copies = [
+                pltpu.make_async_copy(far_ref.at[at, :], held.at[at, :], load_sem)
+                for at in (pl.ds(0, half), pl.ds(half, size - half))
+            ]
+            for copy in copies:
+                copy.start()
+            for copy in copies:
+                copy.wait()
 
         if size > FEW:
 
@@ -250,14 +263,16 @@
     def local(a):
         head = bring(a, *PARTS[0], 58 << 20)
         parts = [send(head, NEXT)]
+        second = bring(a, *PARTS[1], 55 << 20)
+        parts += [send(second, NEXT)]
         own = bring(a, 0, a.shape[0], 51 << 20)
-        parts += [send(rows_of(own, PARTS[k]), NEXT) for k in range(1, len(PARTS))]
+        parts += [send(rows_of(own, PARTS[k]), NEXT) for k in range(2, len(PARTS))]
         out = diag(own)
         passed = [send(part, PASS) for part in parts]
         pieces = cut(own)
         far = [send(piece, FAR) for piece in pieces]
-        for k, chunk in enumerate(PARTS):
-            out = slot1(*chunk, parts[k], own, out)
+        for group in GROUPS:
+            out = slot1(group, [parts[k] for k in group], own, out)
         for j, chunk in enumerate(FARS):
             out = slot2(*chunk, passed, far[j], own if chunk[1] > FEW else turned, out)
             if j == TURN_AFTER:

time: 216 us -> 211 us (0.977)
  local copies, waits for them, and re-layouts: 11.8 us -> 0.24 us
  waiting for transfers between devices: 47.1 us -> 55.8 us
    ppermute x16, waiting for transfers between devices: 47.1 us -> 55.8 us  [send(): return lax.ppermute(a, 'row', pairs)]
    unnamed x8 -> x0, local copies, waits for them, and re-layouts: 6.03 us -> none
    slice x3 -> x2, local copies, waits for them, and re-layouts: 5.78 us -> 0.24 us  [rows_of(): return a[chunk[0]:chunk[0] + chunk[1]]]
    pallas_call x13 -> x12, Pallas kernels: 125 us -> 122 us  [call(): pl.pallas_call(kernel, in_specs=[pl.BlockSpec(memory_space=space) for _,...]
    pallas_call x2 -> x3, Pallas kernels: 4.14 us -> 6.17 us  [bring(): pl.pallas_call(kernel, in_specs=[pl.BlockSpec(memory_space=pl.ANY)], out_...]
  transfers between devices with their start and end apart: 16 -> 16, of which waited for: 1 -> 1; matrix products, arithmetic and copies ran while one was open for 3% -> 0% of each run, Pallas kernels for 58% -> 60%
where the time goes in v8:
time: 211 us; the launch traced here: 210 us
  Pallas kernels  130 us (62%)
  waiting for transfers between devices  55.8 us (26%)
  starting transfers between devices  22.9 us (11%)
    pallas_call x12, Pallas kernels, call(): pl.pallas_call(kernel, in_specs=[pl.BlockSpec(memory_space=space) for _,...  122 us
    ppermute x16, waiting for transfers between devices, send(): return lax.ppermute(a, 'row', pairs)  55.8 us
    ppermute x16, starting transfers between devices, send(): return lax.ppermute(a, 'row', pairs)  22.9 us
    pallas_call x3, Pallas kernels, bring(): pl.pallas_call(kernel, in_specs=[pl.BlockSpec(memory_space=pl.ANY)], out_...  6.17 us
  transfers between devices with their start and end apart: 16, of which 1 were waited for; matrix products, arithmetic and copies ran while one was open for 0% of the time, Pallas kernels for 60%

profile of v8, /device:TPU:1, one launch (start us, length us, event | category | flops | bytes accessed | tf_op | source)
XLA Modules:
  0.0 209.7 jit_solution(13408057357437321672)
XLA Ops:
  0.0 2.1 %bring.5 = bf16[1952,1024]{1,0:T(8,128)(2,1)S(1)} custom-call(bf16[3584,1024]{1,0:T(8,128)(2,1)} %a_ref.5), custom_call_target="tpu_custom_call" | custom-call | bytes 7995392 | tf_op jit(solution)/shard_map/bring/pallas_call | solution.py:74
  2.1 0.0 collective-permute-start.5
  2.2 0.9 bring.4
  3.1 2.4 %collective-permute-start.3 = (bf16[96,1024]{1,0:T(8,128)(2,1)S(1)}, bf16[96,1024]{1,0:T(8,128)(2,1)S(1)}, u32[]{:S(2)}, u32[]{:S(2)}) collective-permute-start(bf16[96,1024]{1,0:T(8,128)(2,1)S(1)} %bring.4), channel_id=1, source_target_pairs={{1,0},{2,1},{3,2},{0,3},{5,4},{6,5},{7,6},{4,7}} | collective-permute-start | bytes 589832 | tf_op jit(solution)/shard_map/ppermute | solution.py:258
  5.6 3.1 %bring.3.own_ref.refs_2_.refs_1_.refs_3_ = bf16[3584,1024]{1,0:T(8,128)(2,1)S(1)} custom-call(bf16[3584,1024]{1,0:T(8,128)(2,1)} %a_ref.5), custom_call_target="tpu_custom_call" | custom-call | bytes 14680064 | tf_op jit(solution)/shard_map/bring/pallas_call | solution.py:74
  8.7 0.2 slice.9
  8.8 0.7 collective-permute-start.8
  9.5 0.1 slice.8
  9.6 0.0 collective-permute-start
  9.7 0.1 cut.1
  9.8 1.3 collective-permute-start.7
  11.1 55.8 %collective-permute-done.5.refs_1_ = bf16[1952,1024]{1,0:T(8,128)(2,1)} collective-permute-done((bf16[1952,1024]{1,0:T(8,128)(2,1)S(1)}, bf16[1952,1024]{1,0:T(8,128)(2,1)}, u32[]{:S(2)}, u32[]{:S(2)}) %collective-permute-start.5) | collective-permute-done | bytes 3997728 | tf_op jit(solution)/shard_map/ppermute | solution.py:258
  66.9 3.2 %collective-permute-start.6 = (bf16[1952,1024]{1,0:T(8,128)(2,1)}, bf16[1952,1024]{1,0:T(8,128)(2,1)}, u32[]{:S(2)}, u32[]{:S(2)}) collective-permute-start(bf16[1952,1024]{1,0:T(8,128)(2,1)} %collective-permute-done.5.refs_1_), channel_id=1, source_target_pairs={{1,0},{5,4}} | collective-permute-start | bytes 11993096 | tf_op jit(solution)/shard_map/ppermute | solution.py:258
  70.0 31.8 %shard_map.17.refs_3_ = f32[1,3,3584,3584]{3,2,1,0:T(8,128)} custom-call(bf16[3584,1024]{1,0:T(8,128)(2,1)S(1)} %bring.3.own_ref.refs_2_.refs_1_.refs_3_), custom_call_target="tpu_custom_call" | custom-call | flops 26306674688 | bytes 58720256 | tf_op jit(solution)/shard_map/pallas_call | solution.py:56
  101.8 0.0 collective-permute-done.3.refs_0_
  101.8 1.3 collective-permute-start.4
  103.1 21.2 %shard_map.18.refs_2_ = f32[1,3,3584,3584]{3,2,1,0:T(8,128)} custom-call(bf16[96,1024]{1,0:T(8,128)(2,1)S(1)} %collective-permute-done.3.refs_0_, bf16[1952,1024]{1,0:T(8,128)(2,1)} %collective-permute-done.5.refs_1_, bf16[3584,1024]{1,0:T(8,128)(2,1)S(1)} %bring.3.own_ref.refs_2_.refs_1_.refs_3_, ...), custom_call_target="tpu_custom_call", output_to_operand_aliasing={{}: (3, {})} | custom-call | flops 15032385536 | bytes 33554432 | tf_op jit(solution)/shard_map/pallas_call | solution.py:56
  124.4 0.0 collective-permute-done.4.refs_0_
  124.4 1.3 collective-permute-start.15
  125.7 0.0 collective-permute-done.refs_0_
  125.7 1.3 collective-permute-start.14
  127.0 0.0 collective-permute-done.8.refs_0_
  127.0 2.6 %collective-permute-start.11 = (bf16[1024,1024]{1,0:T(8,128)(2,1)}, bf16[1024,1024]{1,0:T(8,128)(2,1)}, u32[]{:S(2)}, u32[]{:S(2)}) collective-permute-start(bf16[1024,1024]{1,0:T(8,128)(2,1)} %collective-permute-done.8.refs_0_), channel_id=1, source_target_pairs={{1,0},{5,4}} | collective-permute-start | bytes 6291464 | tf_op jit(solution)/shard_map/ppermute | solution.py:258
  129.6 12.0 %shard_map.19.refs_2_ = f32[1,3,3584,3584]{3,2,1,0:T(8,128)} custom-call(bf16[1024,1024]{1,0:T(8,128)(2,1)} %collective-permute-done.8.refs_0_, bf16[3584,1024]{1,0:T(8,128)(2,1)S(1)} %bring.3.own_ref.refs_2_.refs_1_.refs_3_, f32[1,3,3584,3584]{3,2,1,0:T(8,128)} %shard_map.18.refs_2_), custom_call_target="tpu_custom_call", output_to_operand_aliasing={{}: (2, {})} | custom-call | flops 7516192768 | bytes 16777216 | tf_op jit(solution)/shard_map/pallas_call | solution.py:56
  141.6 7.5 %shard_map.20.refs_4_ = f32[1,3,3584,3584]{3,2,1,0:T(8,128)} custom-call(bf16[512,1024]{1,0:T(8,128)(2,1)} %collective-permute-done.refs_0_, bf16[3584,1024]{1,0:T(8,128)(2,1)S(1)} %bring.3.own_ref.refs_2_.refs_1_.refs_3_, f32[1,3,3584,3584]{3,2,1,0:T(8,128)} %shard_map.19.refs_2_), custom_call_target="tpu_custom_call", output_to_operand_aliasing={{}: (2, {})} | custom-call | flops 3758096384 | bytes 8388608 | tf_op jit(solution)/shard_map/pallas_call | solution.py:56
  149.1 0.0 collective-permute-done.7.refs_2_
  149.1 1.3 collective-permute-start.13
  150.4 0.0 collective-permute-done.6.refs_1_.refs_0_
  150.5 1.3 collective-permute-start.12
  151.8 10.1 %shard_map.21._ = f32[1,3,3584,3584]{3,2,1,0:T(8,128)} custom-call(bf16[96,1024]{1,0:T(8,128)(2,1)S(1)} %collective-permute-done.4.refs_0_, bf16[1952,1024]{1,0:T(8,128)(2,1)} %collective-permute-done.6.refs_1_.refs_0_, bf16[816,1024]{1,0:T(8,128)(2,1)} %collective-permute-done.7.refs_2_, ...), custom_call_target="tpu_custom_call", output_to_operand_aliasing={{}: (4, {})} | custom-call | flops 5989466112 | bytes 13369344 | tf_op jit(solution)/shard_map/pallas_call | solution.py:56
  161.9 2.3 %turn.1 = (bf16[1024,3584]{1,0:T(8,128)(2,1)S(1)}, f32[1,3,3584,3584]{3,2,1,0:T(8,128)}) custom-call(bf16[3584,1024]{1,0:T(8,128)(2,1)S(1)} %bring.3.own_ref.refs_2_.refs_1_.refs_3_, f32[1,3,3584,3584]{3,2,1,0:T(8,128)} %shard_map.21._), custom_call_target="tpu_custom_call", output_to_operand_aliasing={{1}: (1, {})} | custom-call | bytes 14680064 | tf_op jit(solution)/shard_map/turn/pallas_call | solution.py:125
  164.2 0.0 collective-permute-done.15.refs_1_
  164.2 2.3 %collective-permute-start.1 = (bf16[512,1024]{1,0:T(8,128)(2,1)}, bf16[512,1024]{1,0:T(8,128)(2,1)}, u32[]{:S(2)}, u32[]{:S(2)}) collective-permute-start(bf16[512,1024]{1,0:T(8,128)(2,1)} %collective-permute-done.refs_0_), channel_id=1, source_target_pairs={{1,0},{5,4}} | collective-permute-start | bytes 3145736 | tf_op jit(solution)/shard_map/ppermute | solution.py:258
  166.5 9.7 %shard_map.22.refs_4_ = f32[1,3,3584,3584]{3,2,1,0:T(8,128)} custom-call(bf16[1952,1024]{1,0:T(8,128)(2,1)} %collective-permute-done.6.refs_1_.refs_0_, bf16[768,1024]{1,0:T(8,128)(2,1)} %collective-permute-done.15.refs_1_, bf16[3584,1024]{1,0:T(8,128)(2,1)S(1)} %bring.3.own_ref.refs_2_.refs_1_.refs_3_, ...), custom_call_target="tpu_custom_call", output_to_operand_aliasing={{}: (3, {})} | custom-call | flops 5637144576 | bytes 12582912 | tf_op jit(solution)/shard_map/pallas_call | solution.py:56
  176.2 0.0 collective-permute-done.14.refs_2_
  176.2 1.3 collective-permute-start.10
  177.5 0.0 collective-permute-done.11.refs_1_.refs_0_
  177.5 1.3 collective-permute-start.9
  178.8 9.7 %shard_map.23.refs_3_ = f32[1,3,3584,3584]{3,2,1,0:T(8,128)} custom-call(bf16[1952,1024]{1,0:T(8,128)(2,1)} %collective-permute-done.6.refs_1_.refs_0_, bf16[1024,1024]{1,0:T(8,128)(2,1)} %collective-permute-done.11.refs_1_.refs_0_, bf16[768,1024]{1,0:T(8,128)(2,1)} %collective-permute-done.14.refs_2_, ...), custom_call_target="tpu_custom_call", output_to_operand_aliasing={{}: (4, {})} | custom-call | flops 5637144576 | bytes 12582912 | tf_op jit(solution)/shard_map/pallas_call | solution.py:56
  188.6 0.0 collective-permute-done.13.refs_1_
  188.6 1.3 collective-permute-start.2
  189.9 5.8 %shard_map.24.refs_4_ = f32[1,3,3584,3584]{3,2,1,0:T(8,128)} custom-call(bf16[1024,1024]{1,0:T(8,128)(2,1)} %collective-permute-done.11.refs_1_.refs_0_, bf16[464,1024]{1,0:T(8,128)(2,1)} %collective-permute-done.13.refs_1_, bf16[1024,3584]{1,0:T(8,128)(2,1)S(1)} %get-tuple-element.17.refs_2_.refs_3_, ...), custom_call_target="tpu_custom_call", output_to_operand_aliasing={{}: (3, {})} | custom-call | flops 3405774848 | bytes 7602176 | tf_op jit(solution)/shard_map/pallas_call | solution.py:56
  195.7 0.0 collective-permute-done.12.refs_2_
  195.7 0.0 collective-permute-done.1.refs_1_.refs_0_
  195.7 4.1 %shard_map.25.refs_3_ = f32[1,3,3584,3584]{3,2,1,0:T(8,128)} custom-call(bf16[1024,1024]{1,0:T(8,128)(2,1)} %collective-permute-done.11.refs_1_.refs_0_, bf16[512,1024]{1,0:T(8,128)(2,1)} %collective-permute-done.1.refs_1_.refs_0_, bf16[272,1024]{1,0:T(8,128)(2,1)} %collective-permute-done.12.refs_2_, ...), custom_call_target="tpu_custom_call", output_to_operand_aliasing={{}: (4, {})} | custom-call | flops 1996488704 | bytes 4456448 | tf_op jit(solution)/shard_map/pallas_call | solution.py:56
  199.8 0.0 collective-permute-done.10.refs_1_
  199.8 3.5 %shard_map.26.refs_3_ = f32[1,3,3584,3584]{3,2,1,0:T(8,128)} custom-call(bf16[512,1024]{1,0:T(8,128)(2,1)} %collective-permute-done.1.refs_1_.refs_0_, bf16[192,1024]{1,0:T(8,128)(2,1)} %collective-permute-done.10.refs_1_, bf16[1024,3584]{1,0:T(8,128)(2,1)S(1)} %get-tuple-element.17.refs_2_.refs_3_, ...), custom_call_target="tpu_custom_call", output_to_operand_aliasing={{}: (3, {})} | custom-call | flops 1409286144 | bytes 3145728 | tf_op jit(solution)/shard_map/pallas_call | solution.py:56
  203.3 0.0 collective-permute-done.9.refs_1_
  203.3 3.2 %shard_map.27.refs_3_ = f32[1,3,3584,3584]{3,2,1,0:T(8,128)} custom-call(bf16[512,1024]{1,0:T(8,128)(2,1)} %collective-permute-done.1.refs_1_.refs_0_, bf16[160,1024]{1,0:T(8,128)(2,1)} %collective-permute-done.9.refs_1_, bf16[1024,3584]{1,0:T(8,128)(2,1)S(1)} %get-tuple-element.17.refs_2_.refs_3_, ...), custom_call_target="tpu_custom_call", output_to_operand_aliasing={{}: (3, {})} | custom-call | flops 1174405120 | bytes 2621440 | tf_op jit(solution)/shard_map/pallas_call | solution.py:56
  206.5 0.0 collective-permute-done.2.refs_1_
  206.5 3.0 %shard_map.28 = f32[1,3,3584,3584]{3,2,1,0:T(8,128)} custom-call(bf16[512,1024]{1,0:T(8,128)(2,1)} %collective-permute-done.1.refs_1_.refs_0_, bf16[144,1024]{1,0:T(8,128)(2,1)} %collective-permute-done.2.refs_1_, bf16[1024,3584]{1,0:T(8,128)(2,1)S(1)} %get-tuple-element.17.refs_2_.refs_3_, ...), custom_call_target="tpu_custom_call", output_to_operand_aliasing={{}: (3, {})} | custom-call | flops 1056964608 | bytes 2359296 | tf_op jit(solution)/shard_map/pallas_call | solution.py:56
Async XLA Ops:
  2.1 64.7 %collective-permute-start.5 = (bf16[1952,1024]{1,0:T(8,128)(2,1)S(1)}, bf16[1952,1024]{1,0:T(8,128)(2,1)}, u32[]{:S(2)}, u32[]{:S(2)}) collective-permute-start(bf16[1952,1024]{1,0:T(8,128)(2,1)S(1)} %bring.5), channel_id=1, source_target_pairs={{1,0},{2,1},{3,2},{0,3},{5,4},{6,5},{7,6},{4,7}} | collective-permute-start | bytes 11993096 | tf_op jit(solution)/shard_map/ppermute | solution.py:258
  3.1 98.7 %collective-permute-start.3 = (bf16[96,1024]{1,0:T(8,128)(2,1)S(1)}, bf16[96,1024]{1,0:T(8,128)(2,1)S(1)}, u32[]{:S(2)}, u32[]{:S(2)}) collective-permute-start(bf16[96,1024]{1,0:T(8,128)(2,1)S(1)} %bring.4), channel_id=1, source_target_pairs={{1,0},{2,1},{3,2},{0,3},{5,4},{6,5},{7,6},{4,7}} | collective-permute-start | bytes 589832 | tf_op jit(solution)/shard_map/ppermute | solution.py:258
  8.8 118.1 %collective-permute-start.8 = (bf16[1024,1024]{1,0:T(8,128)(2,1)S(1)}, bf16[1024,1024]{1,0:T(8,128)(2,1)}, u32[]{:S(2)}, u32[]{:S(2)}) collective-permute-start(bf16[1024,1024]{1,0:T(8,128)(2,1)S(1)} %slice.9), channel_id=1, source_target_pairs={{1,0},{2,1},{3,2},{0,3},{5,4},{6,5},{7,6},{4,7}} | collective-permute-start | bytes 6291464 | tf_op jit(solution)/shard_map/ppermute | solution.py:258
  9.6 116.1 %collective-permute-start = (bf16[512,1024]{1,0:T(8,128)(2,1)S(1)}, bf16[512,1024]{1,0:T(8,128)(2,1)}, u32[]{:S(2)}, u32[]{:S(2)}) collective-permute-start(bf16[512,1024]{1,0:T(8,128)(2,1)S(1)} %slice.8), channel_id=1, source_target_pairs={{1,0},{2,1},{3,2},{0,3},{5,4},{6,5},{7,6},{4,7}} | collective-permute-start | bytes 3145736 | tf_op jit(solution)/shard_map/ppermute | solution.py:258
  9.8 139.4 %collective-permute-start.7 = (bf16[816,1024]{1,0:T(8,128)(2,1)}, bf16[816,1024]{1,0:T(8,128)(2,1)}, u32[]{:S(2)}, u32[]{:S(2)}) collective-permute-start(bf16[816,1024]{1,0:T(8,128)(2,1)} %get-tuple-element.16), channel_id=1, source_target_pairs={{3,1},{7,5}} | collective-permute-start | bytes 5013512 | tf_op jit(solution)/shard_map/ppermute | solution.py:258
  66.9 83.6 %collective-permute-start.6 = (bf16[1952,1024]{1,0:T(8,128)(2,1)}, bf16[1952,1024]{1,0:T(8,128)(2,1)}, u32[]{:S(2)}, u32[]{:S(2)}) collective-permute-start(bf16[1952,1024]{1,0:T(8,128)(2,1)} %collective-permute-done.5.refs_1_), channel_id=1, source_target_pairs={{1,0},{5,4}} | collective-permute-start | bytes 11993096 | tf_op jit(solution)/shard_map/ppermute | solution.py:258
  101.8 22.5 %collective-permute-start.4 = (bf16[96,1024]{1,0:T(8,128)(2,1)S(1)}, bf16[96,1024]{1,0:T(8,128)(2,1)S(1)}, u32[]{:S(2)}, u32[]{:S(2)}) collective-permute-start(bf16[96,1024]{1,0:T(8,128)(2,1)S(1)} %collective-permute-done.3.refs_0_), channel_id=1, source_target_pairs={{1,0},{5,4}} | collective-permute-start | bytes 589832 | tf_op jit(solution)/shard_map/ppermute | solution.py:258
  124.4 39.8 %collective-permute-start.15 = (bf16[768,1024]{1,0:T(8,128)(2,1)}, bf16[768,1024]{1,0:T(8,128)(2,1)}, u32[]{:S(2)}, u32[]{:S(2)}) collective-permute-start(bf16[768,1024]{1,0:T(8,128)(2,1)} %get-tuple-element.23), channel_id=1, source_target_pairs={{3,1},{7,5}} | collective-permute-start | bytes 4718600 | tf_op jit(solution)/shard_map/ppermute | solution.py:258
  125.7 50.5 %collective-permute-start.14 = (bf16[768,1024]{1,0:T(8,128)(2,1)}, bf16[768,1024]{1,0:T(8,128)(2,1)}, u32[]{:S(2)}, u32[]{:S(2)}) collective-permute-start(bf16[768,1024]{1,0:T(8,128)(2,1)} %get-tuple-element.22), channel_id=1, source_target_pairs={{3,1},{7,5}} | collective-permute-start | bytes 4718600 | tf_op jit(solution)/shard_map/ppermute | solution.py:258
  127.0 50.5 %collective-permute-start.11 = (bf16[1024,1024]{1,0:T(8,128)(2,1)}, bf16[1024,1024]{1,0:T(8,128)(2,1)}, u32[]{:S(2)}, u32[]{:S(2)}) collective-permute-start(bf16[1024,1024]{1,0:T(8,128)(2,1)} %collective-permute-done.8.refs_0_), channel_id=1, source_target_pairs={{1,0},{5,4}} | collective-permute-start | bytes 6291464 | tf_op jit(solution)/shard_map/ppermute | solution.py:258
  149.1 39.4 %collective-permute-start.13 = (bf16[464,1024]{1,0:T(8,128)(2,1)}, bf16[464,1024]{1,0:T(8,128)(2,1)}, u32[]{:S(2)}, u32[]{:S(2)}) collective-permute-start(bf16[464,1024]{1,0:T(8,128)(2,1)} %get-tuple-element.21), channel_id=1, source_target_pairs={{3,1},{7,5}} | collective-permute-start | bytes 2850824 | tf_op jit(solution)/shard_map/ppermute | solution.py:258
  150.5 45.2 %collective-permute-start.12 = (bf16[272,1024]{1,0:T(8,128)(2,1)}, bf16[272,1024]{1,0:T(8,128)(2,1)}, u32[]{:S(2)}, u32[]{:S(2)}) collective-permute-start(bf16[272,1024]{1,0:T(8,128)(2,1)} %get-tuple-element.20), channel_id=1, source_target_pairs={{3,1},{7,5}} | collective-permute-start | bytes 1671176 | tf_op jit(solution)/shard_map/ppermute | solution.py:258
  164.2 31.5 %collective-permute-start.1 = (bf16[512,1024]{1,0:T(8,128)(2,1)}, bf16[512,1024]{1,0:T(8,128)(2,1)}, u32[]{:S(2)}, u32[]{:S(2)}) collective-permute-start(bf16[512,1024]{1,0:T(8,128)(2,1)} %collective-permute-done.refs_0_), channel_id=1, source_target_pairs={{1,0},{5,4}} | collective-permute-start | bytes 3145736 | tf_op jit(solution)/shard_map/ppermute | solution.py:258
  176.2 23.6 %collective-permute-start.10 = (bf16[192,1024]{1,0:T(8,128)(2,1)}, bf16[192,1024]{1,0:T(8,128)(2,1)}, u32[]{:S(2)}, u32[]{:S(2)}) collective-permute-start(bf16[192,1024]{1,0:T(8,128)(2,1)} %get-tuple-element.19), channel_id=1, source_target_pairs={{3,1},{7,5}} | collective-permute-start | bytes 1179656 | tf_op jit(solution)/shard_map/ppermute | solution.py:258
  177.5 25.8 %collective-permute-start.9 = (bf16[160,1024]{1,0:T(8,128)(2,1)}, bf16[160,1024]{1,0:T(8,128)(2,1)}, u32[]{:S(2)}, u32[]{:S(2)}) collective-permute-start(bf16[160,1024]{1,0:T(8,128)(2,1)} %get-tuple-element.18), channel_id=1, source_target_pairs={{3,1},{7,5}} | collective-permute-start | bytes 983048 | tf_op jit(solution)/shard_map/ppermute | solution.py:258
  188.6 17.9 %collective-permute-start.2 = (bf16[144,1024]{1,0:T(8,128)(2,1)}, bf16[144,1024]{1,0:T(8,128)(2,1)}, u32[]{:S(2)}, u32[]{:S(2)}) collective-permute-start(bf16[144,1024]{1,0:T(8,128)(2,1)} %get-tuple-element.15), channel_id=1, source_target_pairs={{3,1},{7,5}} | collective-permute-start | bytes 884744 | tf_op jit(solution)/shard_map/ppermute | solution.py:258

commit v9 on v8

--- a/solution.py
+++ b/solution.py
@@ -9,12 +9,13 @@
 WIDE = 512
 HIGH = 1792
 NEXT = [(1, 0), (2, 1), (3, 2), (0, 3)]
-FAR = [(3, 1)]
+FAR = [(3, 1), (1, 0), (0, 2), (2, 3)]
 PASS = [(1, 0)]
-PARTS = [(0, 96), (96, 1952), (2048, 1024), (3072, 512)]
+PARTS = [(0, 192), (192, 1856), (2048, 1024), (3072, 512)]
 GROUPS = [[0, 1], [2], [3]]
 FARS = [(0, 816), (816, 768), (1584, 768), (2352, 464), (2816, 272), (3088, 192), (3280, 160), (3440, 144)]
-TURN_AFTER = 0
+HEAD = PARTS[0][1]
+SENDS = [(HEAD, FARS[0][1] - HEAD)] + FARS[1:]
 DEPTH = 3
 FEW = 464
 
@@ -48,6 +49,17 @@
     copy = pltpu.make_async_copy(src, dst, sem)
     copy.start()
     copy.wait()
+
+
+def fill(held, refs, starts, counts, sem):
+    copies, at = [], 0
+    for ref, start, count in zip(refs, starts, counts):
+        copies.append(pltpu.make_async_copy(ref.at[pl.ds(start, count), :], held.at[pl.ds(at, count), :], sem))
+        at += count
+    for copy in copies:
+        copy.start()
+    for copy in copies:
+        copy.wait()
 
 
 def call(kernel, rows, cols, depth, out, refs, scratch):
@@ -93,7 +105,7 @@
         def _():
             copies = [
                 pltpu.make_async_copy(own_ref.at[pl.ds(first, size), :], piece_ref, sem.at[k])
-                for k, ((first, size), piece_ref) in enumerate(zip(FARS, piece_refs))
+                for k, ((first, size), piece_ref) in enumerate(zip(SENDS, piece_refs))
             ]
             for copy in copies:
                 copy.start()
@@ -103,9 +115,9 @@
     return pl.pallas_call(
         kernel,
         in_specs=[pl.BlockSpec(memory_space=pltpu.VMEM)],
-        out_specs=[pl.BlockSpec(memory_space=pl.ANY)] * len(FARS),
-        out_shape=[jax.ShapeDtypeStruct((size, depth), own.dtype) for _, size in FARS],
-        scratch_shapes=[pltpu.SemaphoreType.DMA((len(FARS),))],
+        out_specs=[pl.BlockSpec(memory_space=pl.ANY)] * len(SENDS),
+        out_shape=[jax.ShapeDtypeStruct((size, depth), own.dtype) for _, size in SENDS],
+        scratch_shapes=[pltpu.SemaphoreType.DMA((len(SENDS),))],
         cost_estimate=pl.CostEstimate(flops=0, bytes_accessed=4 * own.size, transcendentals=0),
         compiler_params=pltpu.CompilerParams(vmem_limit_bytes=32 << 20),
         name="cut",
@@ -158,8 +170,7 @@
     def kernel(*refs):
         part_refs, (own_ref, _, out_ref, sem, load_sem, held, buf) = refs[:len(group)], refs[len(group):]
         p = lax.axis_index("row")
-        for k, part_ref in zip(group, part_refs):
-            load(part_ref, held.at[pl.ds(PARTS[k][0] - first, PARTS[k][1]), :], load_sem)
+        fill(held, part_refs, [0] * len(group), [PARTS[k][1] for k in group], load_sem)
 
         @pl.when(p < 3)
         def _():
@@ -188,10 +199,11 @@
     for (start, count), part in zip(PARTS, passed):
         low, end = max(first, start), min(first + size, start + count)
         if low < end:
-            near.append((part, low - start, low - first, end - low))
+            near.append((part, low - start, end - low))
 
     def kernel(*refs):
-        near_refs, (far_ref, own_ref, _, out_ref, sem, load_sem, held, buf) = refs[:len(near)], refs[len(near):]
+        near_refs, far_refs = refs[:len(near)], refs[len(near):len(near) + len(far)]
+        own_ref, _, out_ref, sem, load_sem, held, buf = refs[len(near) + len(far):]
         p = lax.axis_index("row")
 
         def place(start, wide):
@@ -199,20 +211,13 @@
 
         @pl.when(p == 0)
         def _():
-            for ref, (_, src, dst, count) in zip(near_refs, near):
-                load(ref.at[pl.ds(src, count), :], held.at[pl.ds(dst, count), :], load_sem)
+            fill(held, near_refs, [src for _, src, _ in near], [count for _, _, count in near], load_sem)
 
         @pl.when(p == 1)
         def _():
-            half = size // 32 * 16
-            copies = [
-                pltpu.make_async_copy(far_ref.at[at, :], held.at[at, :], load_sem)
-                for at in (pl.ds(0, half), pl.ds(half, size - half))
-            ]
-            for copy in copies:
-                copy.start()
-            for copy in copies:
-                copy.wait()
+            if len(far) > 1:
+                held[:HEAD, :] = far_refs[0][...]
+            load(far_refs[-1], held.at[pl.ds(size - far[-1].shape[0], far[-1].shape[0]), :], load_sem)
 
         if size > FEW:
 
@@ -247,7 +252,7 @@
 
     bufs = DEPTH if size > FEW else rows // WIDE
     scratch = [pltpu.VMEM((size, depth), jnp.bfloat16), pltpu.VMEM((bufs, size, WIDE), jnp.float32)]
-    refs = [(part, pl.ANY) for part, *_ in near] + [(far, pl.ANY), (own, pltpu.VMEM)]
+    refs = [(part, pl.ANY) for part, *_ in near] + [(part, pltpu.VMEM) for part in far[:-1]] + [(far[-1], pl.ANY), (own, pltpu.VMEM)]
     return call(kernel, size, rows, depth, out, refs, scratch)
 
 
@@ -262,21 +267,20 @@
 
     def local(a):
         head = bring(a, *PARTS[0], 58 << 20)
+        far_head = send(head, FAR)
         parts = [send(head, NEXT)]
-        second = bring(a, *PARTS[1], 55 << 20)
-        parts += [send(second, NEXT)]
         own = bring(a, 0, a.shape[0], 51 << 20)
-        parts += [send(rows_of(own, PARTS[k]), NEXT) for k in range(2, len(PARTS))]
+        parts += [send(rows_of(own, PARTS[k]), NEXT) for k in range(1, len(PARTS))]
         out = diag(own)
         passed = [send(part, PASS) for part in parts]
         pieces = cut(own)
-        far = [send(piece, FAR) for piece in pieces]
+        far = [[send(piece, FAR)] for piece in pieces]
+        far[0].insert(0, far_head)
+        turned, out = turn(own, out)
         for group in GROUPS:
             out = slot1(group, [parts[k] for k in group], own, out)
         for j, chunk in enumerate(FARS):
             out = slot2(*chunk, passed, far[j], own if chunk[1] > FEW else turned, out)
-            if j == TURN_AFTER:
-                turned, out = turn(own, out)
         return out
 
     return jax.shard_map(

time: 211 us -> 202 us (0.957)
  the two profiles are of different devices: /device:TPU:1 before, /device:TPU:0 now
where the time goes in v9:
time: 202 us; the launch traced here: 199 us
  Pallas kernels  128 us (63%)
  waiting for transfers between devices  33.8 us (17%)
  starting transfers between devices  19.4 us (10%)
  local copies, waits for them, and re-layouts  17.7 us (9%)
    pallas_call x12, Pallas kernels, call(): pl.pallas_call(kernel, in_specs=[pl.BlockSpec(memory_space=space) for _,...  122 us
    ppermute x17, waiting for transfers between devices, send(): return lax.ppermute(a, 'row', pairs)  33.8 us
    ppermute x17, starting transfers between devices, send(): return lax.ppermute(a, 'row', pairs)  19.4 us
    unnamed x10, local copies, waits for them, and re-layouts  9.98 us
    slice x3, local copies, waits for them, and re-layouts, rows_of(): return a[chunk[0]:chunk[0] + chunk[1]]  7.71 us
    pallas_call x2, Pallas kernels, bring(): pl.pallas_call(kernel, in_specs=[pl.BlockSpec(memory_space=pl.ANY)], out_...  4.09 us
  transfers between devices with their start and end apart: 17, of which 1 were waited for; matrix products, arithmetic and copies ran while one was open for 3% of the time, Pallas kernels for 61%

profile of v9, /device:TPU:0, one launch (start us, length us, event | category | flops | bytes accessed | tf_op | source)
XLA Modules:
  0.0 199.5 jit_solution(16692323279308558673)
XLA Ops:
  0.0 3.1 %bring.2.own_ref.refs_2_.refs_1_.refs_4_.refs_3_ = bf16[3584,1024]{1,0:T(8,128)(2,1)S(1)} custom-call(bf16[3584,1024]{1,0:T(8,128)(2,1)} %a_ref.3), custom_call_target="tpu_custom_call" | custom-call | bytes 14680064 | tf_op jit(solution)/shard_map/bring/pallas_call | solution.py:86
  3.1 0.0 copy-start
  3.1 2.9 %copy-done = bf16[3584,1024]{1,0:T(8,128)(2,1)} copy-done((bf16[3584,1024]{1,0:T(8,128)(2,1)}, bf16[3584,1024]{1,0:T(8,128)(2,1)S(1)}, u32[]{:S(2)}) %copy-start) | copy-done | bytes 7340056
  6.0 2.3 %slice.14 = bf16[1856,1024]{1,0:T(8,128)(2,1)} slice(bf16[3584,1024]{1,0:T(8,128)(2,1)S(1)} %bring.2.own_ref.refs_2_.refs_1_.refs_4_.refs_3_), slice={[192:2048], [0:1024]} | slice | bytes 7602176 | tf_op jit(solution)/shard_map/slice | solution.py:266
  8.3 2.7 %collective-permute-start.9 = (bf16[1856,1024]{1,0:T(8,128)(2,1)}, bf16[1856,1024]{1,0:T(8,128)(2,1)}, u32[]{:S(2)}, u32[]{:S(2)}) collective-permute-start(bf16[1856,1024]{1,0:T(8,128)(2,1)} %slice.14), channel_id=1, source_target_pairs={{1,0},{2,1},{3,2},{0,3},{5,4},{6,5},{7,6},{4,7}} | collective-permute-start | bytes 11403272 | tf_op jit(solution)/shard_map/ppermute | solution.py:263
  11.1 1.0 bring.3
  12.1 0.7 collective-permute-start.13
  12.8 0.0 collective-permute-start.15
  12.8 3.1 %slice.13 = bf16[1024,1024]{1,0:T(8,128)(2,1)} slice(bf16[3584,1024]{1,0:T(8,128)(2,1)} %copy-done), slice={[2048:3072], [0:1024]} | slice | bytes 4194304 | tf_op jit(solution)/shard_map/slice | solution.py:266
  15.9 1.2 collective-permute-start.5
  17.1 2.3 %slice.12 = bf16[512,1024]{1,0:T(8,128)(2,1)} slice(bf16[3584,1024]{1,0:T(8,128)(2,1)} %copy-done), slice={[3072:3584], [0:1024]} | slice | bytes 2097152 | tf_op jit(solution)/shard_map/slice | solution.py:266
  19.4 0.0 collective-permute-start
  19.4 33.8 %collective-permute-done.9.refs_1_ = bf16[1856,1024]{1,0:T(8,128)(2,1)} collective-permute-done((bf16[1856,1024]{1,0:T(8,128)(2,1)}, bf16[1856,1024]{1,0:T(8,128)(2,1)}, u32[]{:S(2)}, u32[]{:S(2)}) %collective-permute-start.9) | collective-permute-done | bytes 3801120 | tf_op jit(solution)/shard_map/ppermute | solution.py:263
  53.2 1.3 collective-permute-start.10
  54.5 0.0 copy-start.1
  54.5 3.1 %copy-done.1 = bf16[3584,1024]{1,0:T(8,128)(2,1)S(1)} copy-done((bf16[3584,1024]{1,0:T(8,128)(2,1)S(1)}, bf16[3584,1024]{1,0:T(8,128)(2,1)}, u32[]{:S(2)}) %copy-start.1) | copy-done | bytes 7340056
  57.6 31.7 %shard_map.17._ = f32[1,3,3584,3584]{3,2,1,0:T(8,128)} custom-call(bf16[3584,1024]{1,0:T(8,128)(2,1)S(1)} %copy-done.1), custom_call_target="tpu_custom_call" | custom-call | flops 26306674688 | bytes 58720256 | tf_op jit(solution)/shard_map/pallas_call | solution.py:68
  89.3 0.0 copy-start.2
  89.3 0.1 cut.1
  89.4 3.0 %copy-done.2 = bf16[3584,1024]{1,0:T(8,128)(2,1)S(1)} copy-done((bf16[3584,1024]{1,0:T(8,128)(2,1)S(1)}, bf16[3584,1024]{1,0:T(8,128)(2,1)}, u32[]{:S(2)}) %copy-start.2) | copy-done | bytes 7340056
  92.4 2.3 %turn.1 = (bf16[1024,3584]{1,0:T(8,128)(2,1)S(1)}, f32[1,3,3584,3584]{3,2,1,0:T(8,128)}) custom-call(bf16[3584,1024]{1,0:T(8,128)(2,1)S(1)} %copy-done.2, f32[1,3,3584,3584]{3,2,1,0:T(8,128)} %shard_map.17._), custom_call_target="tpu_custom_call", output_to_operand_aliasing={{1}: (1, {})} | custom-call | bytes 14680064 | tf_op jit(solution)/shard_map/turn/pallas_call | solution.py:137
  94.7 0.0 collective-permute-done.13.refs_0_
  94.7 3.8 %collective-permute-start.16 = (bf16[624,1024]{1,0:T(8,128)(2,1)}, bf16[624,1024]{1,0:T(8,128)(2,1)}, u32[]{:S(2)}, u32[]{:S(2)}) collective-permute-start(bf16[624,1024]{1,0:T(8,128)(2,1)} %get-tuple-element.23), channel_id=1, source_target_pairs={{3,1},{1,0},{0,2},{2,3},{7,5},{5,4},{4,6},{6,7}} | collective-permute-start | bytes 3833864 | tf_op jit(solution)/shard_map/ppermute | solution.py:263
  98.5 0.0 collective-permute-done.15.refs_2_
  98.5 1.3 collective-permute-start.14
  99.8 21.1 %shard_map.18.refs_2_ = f32[1,3,3584,3584]{3,2,1,0:T(8,128)} custom-call(bf16[192,1024]{1,0:T(8,128)(2,1)S(1)} %collective-permute-done.13.refs_0_, bf16[1856,1024]{1,0:T(8,128)(2,1)} %collective-permute-done.9.refs_1_, bf16[3584,1024]{1,0:T(8,128)(2,1)S(1)} %copy-done.2, f32[1,3,3584,3584]{3,2,1,0:T(8,128)} %get-tuple-element.24.refs_3_), custom_call_target="tpu_custom_call", output_to_operand_aliasing={{}: (3, {})} | custom-call | flops 15032385536 | bytes 33554432 | tf_op jit(solution)/shard_map/pallas_call | solution.py:68
  120.9 0.0 collective-permute-done.14.refs_0_
  120.9 0.0 copy-start.3
  120.9 0.0 collective-permute-start.12
  120.9 0.0 collective-permute-done.refs_0_
  121.0 4.3 %collective-permute-start.11 = (bf16[768,1024]{1,0:T(8,128)(2,1)}, bf16[768,1024]{1,0:T(8,128)(2,1)}, u32[]{:S(2)}, u32[]{:S(2)}) collective-permute-start(bf16[768,1024]{1,0:T(8,128)(2,1)} %get-tuple-element.21), channel_id=1, source_target_pairs={{3,1},{1,0},{0,2},{2,3},{7,5},{5,4},{4,6},{6,7}} | collective-permute-start | bytes 4718600 | tf_op jit(solution)/shard_map/ppermute | solution.py:263
  125.3 0.0 collective-permute-done.5.refs_0_
  125.3 1.3 collective-permute-start.6
  126.6 12.0 %shard_map.19.refs_2_ = f32[1,3,3584,3584]{3,2,1,0:T(8,128)} custom-call(bf16[1024,1024]{1,0:T(8,128)(2,1)} %collective-permute-done.5.refs_0_, bf16[3584,1024]{1,0:T(8,128)(2,1)S(1)} %copy-done.2, f32[1,3,3584,3584]{3,2,1,0:T(8,128)} %shard_map.18.refs_2_), custom_call_target="tpu_custom_call", output_to_operand_aliasing={{}: (2, {})} | custom-call | flops 7516192768 | bytes 16777216 | tf_op jit(solution)/shard_map/pallas_call | solution.py:68
  138.6 0.0 copy-done.3
  138.6 7.5 %shard_map.20.refs_5_ = f32[1,3,3584,3584]{3,2,1,0:T(8,128)} custom-call(bf16[512,1024]{1,0:T(8,128)(2,1)} %collective-permute-done.refs_0_, bf16[3584,1024]{1,0:T(8,128)(2,1)S(1)} %copy-done.2, f32[1,3,3584,3584]{3,2,1,0:T(8,128)} %shard_map.19.refs_2_), custom_call_target="tpu_custom_call", output_to_operand_aliasing={{}: (2, {})} | custom-call | flops 3758096384 | bytes 8388608 | tf_op jit(solution)/shard_map/pallas_call | solution.py:68
  146.1 0.0 collective-permute-done.16.refs_3_
  146.1 1.4 collective-permute-start.8
  147.5 0.0 collective-permute-done.10.refs_1_.refs_0_
  147.5 0.0 collective-permute-start.7
  147.6 0.0 copy-start.4
  147.6 1.0 copy-done.4
  148.6 10.2 %shard_map.21.refs_3_ = f32[1,3,3584,3584]{3,2,1,0:T(8,128)} custom-call(bf16[192,1024]{1,0:T(8,128)(2,1)S(1)} %copy-done.4, bf16[1856,1024]{1,0:T(8,128)(2,1)} %collective-permute-done.10.refs_1_.refs_0_, bf16[192,1024]{1,0:T(8,128)(2,1)S(1)} %collective-permute-done.15.refs_2_, ...), custom_call_target="tpu_custom_call", output_to_operand_aliasing={{}: (5, {})} | custom-call | flops 5989466112 | bytes 13369344 | tf_op jit(solution)/shard_map/pallas_call | solution.py:68
  158.8 0.0 collective-permute-done.12.refs_1_
  158.8 1.3 collective-permute-start.1
  160.1 9.8 %shard_map.22.refs_4_ = f32[1,3,3584,3584]{3,2,1,0:T(8,128)} custom-call(bf16[1856,1024]{1,0:T(8,128)(2,1)} %collective-permute-done.10.refs_1_.refs_0_, bf16[768,1024]{1,0:T(8,128)(2,1)} %collective-permute-done.12.refs_1_, bf16[3584,1024]{1,0:T(8,128)(2,1)S(1)} %copy-done.2, f32[1,3,3584,3584]{3,2,1,0:T(8,128)} %shard_map.21.refs_3_), custom_call_target="tpu_custom_call", output_to_operand_aliasing={{}: (3, {})} | custom-call | flops 5637144576 | bytes 12582912 | tf_op jit(solution)/shard_map/pallas_call | solution.py:68
  169.9 0.0 collective-permute-done.11.refs_2_
  169.9 0.0 collective-permute-start.4
  169.9 0.0 collective-permute-done.6.refs_1_.refs_0_
  169.9 0.0 collective-permute-start.3
  169.9 9.7 %shard_map.23.refs_3_ = f32[1,3,3584,3584]{3,2,1,0:T(8,128)} custom-call(bf16[1856,1024]{1,0:T(8,128)(2,1)} %collective-permute-done.10.refs_1_.refs_0_, bf16[1024,1024]{1,0:T(8,128)(2,1)} %collective-permute-done.6.refs_1_.refs_0_, bf16[768,1024]{1,0:T(8,128)(2,1)} %collective-permute-done.11.refs_2_, ...), custom_call_target="tpu_custom_call", output_to_operand_aliasing={{}: (4, {})} | custom-call | flops 5637144576 | bytes 12582912 | tf_op jit(solution)/shard_map/pallas_call | solution.py:68
  179.7 0.0 collective-permute-done.8.refs_1_
  179.7 0.0 collective-permute-start.2
  179.7 5.8 %shard_map.24.refs_4_ = f32[1,3,3584,3584]{3,2,1,0:T(8,128)} custom-call(bf16[1024,1024]{1,0:T(8,128)(2,1)} %collective-permute-done.6.refs_1_.refs_0_, bf16[464,1024]{1,0:T(8,128)(2,1)} %collective-permute-done.8.refs_1_, bf16[1024,3584]{1,0:T(8,128)(2,1)S(1)} %get-tuple-element.16.refs_2_.refs_3_, ...), custom_call_target="tpu_custom_call", output_to_operand_aliasing={{}: (3, {})} | custom-call | flops 3405774848 | bytes 7602176 | tf_op jit(solution)/shard_map/pallas_call | solution.py:68
  185.5 0.0 collective-permute-done.7.refs_2_
  185.5 0.0 collective-permute-done.1.refs_1_.refs_0_
  185.6 4.1 %shard_map.25.refs_3_ = f32[1,3,3584,3584]{3,2,1,0:T(8,128)} custom-call(bf16[1024,1024]{1,0:T(8,128)(2,1)} %collective-permute-done.6.refs_1_.refs_0_, bf16[512,1024]{1,0:T(8,128)(2,1)} %collective-permute-done.1.refs_1_.refs_0_, bf16[272,1024]{1,0:T(8,128)(2,1)} %collective-permute-done.7.refs_2_, ...), custom_call_target="tpu_custom_call", output_to_operand_aliasing={{}: (4, {})} | custom-call | flops 1996488704 | bytes 4456448 | tf_op jit(solution)/shard_map/pallas_call | solution.py:68
  189.7 0.0 collective-permute-done.4.refs_1_
  189.7 3.4 %shard_map.26.refs_3_ = f32[1,3,3584,3584]{3,2,1,0:T(8,128)} custom-call(bf16[512,1024]{1,0:T(8,128)(2,1)} %collective-permute-done.1.refs_1_.refs_0_, bf16[192,1024]{1,0:T(8,128)(2,1)} %collective-permute-done.4.refs_1_, bf16[1024,3584]{1,0:T(8,128)(2,1)S(1)} %get-tuple-element.16.refs_2_.refs_3_, ...), custom_call_target="tpu_custom_call", output_to_operand_aliasing={{}: (3, {})} | custom-call | flops 1409286144 | bytes 3145728 | tf_op jit(solution)/shard_map/pallas_call | solution.py:68
  193.1 0.0 collective-permute-done.3.refs_1_
  193.1 3.1 %shard_map.27.refs_3_ = f32[1,3,3584,3584]{3,2,1,0:T(8,128)} custom-call(bf16[512,1024]{1,0:T(8,128)(2,1)} %collective-permute-done.1.refs_1_.refs_0_, bf16[160,1024]{1,0:T(8,128)(2,1)} %collective-permute-done.3.refs_1_, bf16[1024,3584]{1,0:T(8,128)(2,1)S(1)} %get-tuple-element.16.refs_2_.refs_3_, ...), custom_call_target="tpu_custom_call", output_to_operand_aliasing={{}: (3, {})} | custom-call | flops 1174405120 | bytes 2621440 | tf_op jit(solution)/shard_map/pallas_call | solution.py:68
  196.3 0.0 collective-permute-done.2.refs_1_
  196.3 3.0 %shard_map.28 = f32[1,3,3584,3584]{3,2,1,0:T(8,128)} custom-call(bf16[512,1024]{1,0:T(8,128)(2,1)} %collective-permute-done.1.refs_1_.refs_0_, bf16[144,1024]{1,0:T(8,128)(2,1)} %collective-permute-done.2.refs_1_, bf16[1024,3584]{1,0:T(8,128)(2,1)S(1)} %get-tuple-element.16.refs_2_.refs_3_, ...), custom_call_target="tpu_custom_call", output_to_operand_aliasing={{}: (3, {})} | custom-call | flops 1056964608 | bytes 2359296 | tf_op jit(solution)/shard_map/pallas_call | solution.py:68
Async XLA Ops:
  3.1 2.9 %copy-start = (bf16[3584,1024]{1,0:T(8,128)(2,1)}, bf16[3584,1024]{1,0:T(8,128)(2,1)S(1)}, u32[]{:S(2)}) copy-start(bf16[3584,1024]{1,0:T(8,128)(2,1)S(1)} %bring.2.own_ref.refs_2_.refs_1_.refs_4_.refs_3_) | copy-start | bytes 22020100
  8.3 44.9 %collective-permute-start.9 = (bf16[1856,1024]{1,0:T(8,128)(2,1)}, bf16[1856,1024]{1,0:T(8,128)(2,1)}, u32[]{:S(2)}, u32[]{:S(2)}) collective-permute-start(bf16[1856,1024]{1,0:T(8,128)(2,1)} %slice.14), channel_id=1, source_target_pairs={{1,0},{2,1},{3,2},{0,3},{5,4},{6,5},{7,6},{4,7}} | collective-permute-start | bytes 11403272 | tf_op jit(solution)/shard_map/ppermute | solution.py:263
  12.1 82.6 %collective-permute-start.13 = (bf16[192,1024]{1,0:T(8,128)(2,1)S(1)}, bf16[192,1024]{1,0:T(8,128)(2,1)S(1)}, u32[]{:S(2)}, u32[]{:S(2)}) collective-permute-start(bf16[192,1024]{1,0:T(8,128)(2,1)S(1)} %bring.3), channel_id=1, source_target_pairs={{1,0},{2,1},{3,2},{0,3},{5,4},{6,5},{7,6},{4,7}} | collective-permute-start | bytes 1179656 | tf_op jit(solution)/shard_map/ppermute | solution.py:263
  12.8 85.7 %collective-permute-start.15 = (bf16[192,1024]{1,0:T(8,128)(2,1)S(1)}, bf16[192,1024]{1,0:T(8,128)(2,1)S(1)}, u32[]{:S(2)}, u32[]{:S(2)}) collective-permute-start(bf16[192,1024]{1,0:T(8,128)(2,1)S(1)} %bring.3), channel_id=1, source_target_pairs={{3,1},{1,0},{0,2},{2,3},{7,5},{5,4},{4,6},{6,7}} | collective-permute-start | bytes 1179656 | tf_op jit(solution)/shard_map/ppermute | solution.py:263
  15.9 109.4 %collective-permute-start.5 = (bf16[1024,1024]{1,0:T(8,128)(2,1)}, bf16[1024,1024]{1,0:T(8,128)(2,1)}, u32[]{:S(2)}, u32[]{:S(2)}) collective-permute-start(bf16[1024,1024]{1,0:T(8,128)(2,1)} %slice.13), channel_id=1, source_target_pairs={{1,0},{2,1},{3,2},{0,3},{5,4},{6,5},{7,6},{4,7}} | collective-permute-start | bytes 6291464 | tf_op jit(solution)/shard_map/ppermute | solution.py:263
  19.4 101.5 %collective-permute-start = (bf16[512,1024]{1,0:T(8,128)(2,1)}, bf16[512,1024]{1,0:T(8,128)(2,1)}, u32[]{:S(2)}, u32[]{:S(2)}) collective-permute-start(bf16[512,1024]{1,0:T(8,128)(2,1)} %slice.12), channel_id=1, source_target_pairs={{1,0},{2,1},{3,2},{0,3},{5,4},{6,5},{7,6},{4,7}} | collective-permute-start | bytes 3145736 | tf_op jit(solution)/shard_map/ppermute | solution.py:263
  53.2 94.3 %collective-permute-start.10 = (bf16[1856,1024]{1,0:T(8,128)(2,1)}, bf16[1856,1024]{1,0:T(8,128)(2,1)}, u32[]{:S(2)}, u32[]{:S(2)}) collective-permute-start(bf16[1856,1024]{1,0:T(8,128)(2,1)} %collective-permute-done.9.refs_1_), channel_id=1, source_target_pairs={{1,0},{5,4}} | collective-permute-start | bytes 11403272 | tf_op jit(solution)/shard_map/ppermute | solution.py:263
  54.5 3.1 %copy-start.1 = (bf16[3584,1024]{1,0:T(8,128)(2,1)S(1)}, bf16[3584,1024]{1,0:T(8,128)(2,1)}, u32[]{:S(2)}) copy-start(bf16[3584,1024]{1,0:T(8,128)(2,1)} %copy-done) | copy-start | bytes 22020100
  89.3 3.1 %copy-start.2 = (bf16[3584,1024]{1,0:T(8,128)(2,1)S(1)}, bf16[3584,1024]{1,0:T(8,128)(2,1)}, u32[]{:S(2)}) copy-start(bf16[3584,1024]{1,0:T(8,128)(2,1)} %copy-done) | copy-start | bytes 22020100
  94.7 51.5 %collective-permute-start.16 = (bf16[624,1024]{1,0:T(8,128)(2,1)}, bf16[624,1024]{1,0:T(8,128)(2,1)}, u32[]{:S(2)}, u32[]{:S(2)}) collective-permute-start(bf16[624,1024]{1,0:T(8,128)(2,1)} %get-tuple-element.23), channel_id=1, source_target_pairs={{3,1},{1,0},{0,2},{2,3},{7,5},{5,4},{4,6},{6,7}} | collective-permute-start | bytes 3833864 | tf_op jit(solution)/shard_map/ppermute | solution.py:263
  98.5 22.4 %collective-permute-start.14 = (bf16[192,1024]{1,0:T(8,128)(2,1)S(1)}, bf16[192,1024]{1,0:T(8,128)(2,1)S(1)}, u32[]{:S(2)}, u32[]{:S(2)}) collective-permute-start(bf16[192,1024]{1,0:T(8,128)(2,1)S(1)} %collective-permute-done.13.refs_0_), channel_id=1, source_target_pairs={{1,0},{5,4}} | collective-permute-start | bytes 1179656 | tf_op jit(solution)/shard_map/ppermute | solution.py:263
  120.9 17.7 %copy-start.3 = (bf16[192,1024]{1,0:T(8,128)(2,1)}, bf16[192,1024]{1,0:T(8,128)(2,1)S(1)}, u32[]{:S(2)}) copy-start(bf16[192,1024]{1,0:T(8,128)(2,1)S(1)} %collective-permute-done.14.refs_0_) | copy-start | bytes 1179652
  120.9 37.9 %collective-permute-start.12 = (bf16[768,1024]{1,0:T(8,128)(2,1)}, bf16[768,1024]{1,0:T(8,128)(2,1)}, u32[]{:S(2)}, u32[]{:S(2)}) collective-permute-start(bf16[768,1024]{1,0:T(8,128)(2,1)} %get-tuple-element.22), channel_id=1, source_target_pairs={{3,1},{1,0},{0,2},{2,3},{7,5},{5,4},{4,6},{6,7}} | collective-permute-start | bytes 4718600 | tf_op jit(solution)/shard_map/ppermute | solution.py:263
  121.0 48.9 %collective-permute-start.11 = (bf16[768,1024]{1,0:T(8,128)(2,1)}, bf16[768,1024]{1,0:T(8,128)(2,1)}, u32[]{:S(2)}, u32[]{:S(2)}) collective-permute-start(bf16[768,1024]{1,0:T(8,128)(2,1)} %get-tuple-element.21), channel_id=1, source_target_pairs={{3,1},{1,0},{0,2},{2,3},{7,5},{5,4},{4,6},{6,7}} | collective-permute-start | bytes 4718600 | tf_op jit(solution)/shard_map/ppermute | solution.py:263
  125.3 44.6 %collective-permute-start.6 = (bf16[1024,1024]{1,0:T(8,128)(2,1)}, bf16[1024,1024]{1,0:T(8,128)(2,1)}, u32[]{:S(2)}, u32[]{:S(2)}) collective-permute-start(bf16[1024,1024]{1,0:T(8,128)(2,1)} %collective-permute-done.5.refs_0_), channel_id=1, source_target_pairs={{1,0},{5,4}} | collective-permute-start | bytes 6291464 | tf_op jit(solution)/shard_map/ppermute | solution.py:263
  146.1 33.5 %collective-permute-start.8 = (bf16[464,1024]{1,0:T(8,128)(2,1)}, bf16[464,1024]{1,0:T(8,128)(2,1)}, u32[]{:S(2)}, u32[]{:S(2)}) collective-permute-start(bf16[464,1024]{1,0:T(8,128)(2,1)} %get-tuple-element.20), channel_id=1, source_target_pairs={{3,1},{1,0},{0,2},{2,3},{7,5},{5,4},{4,6},{6,7}} | collective-permute-start | bytes 2850824 | tf_op jit(solution)/shard_map/ppermute | solution.py:263
  147.5 38.0 %collective-permute-start.7 = (bf16[272,1024]{1,0:T(8,128)(2,1)}, bf16[272,1024]{1,0:T(8,128)(2,1)}, u32[]{:S(2)}, u32[]{:S(2)}) collective-permute-start(bf16[272,1024]{1,0:T(8,128)(2,1)} %get-tuple-element.19), channel_id=1, source_target_pairs={{3,1},{1,0},{0,2},{2,3},{7,5},{5,4},{4,6},{6,7}} | collective-permute-start | bytes 1671176 | tf_op jit(solution)/shard_map/ppermute | solution.py:263
  147.6 1.0 copy-start.4
  158.8 26.8 %collective-permute-start.1 = (bf16[512,1024]{1,0:T(8,128)(2,1)}, bf16[512,1024]{1,0:T(8,128)(2,1)}, u32[]{:S(2)}, u32[]{:S(2)}) collective-permute-start(bf16[512,1024]{1,0:T(8,128)(2,1)} %collective-permute-done.refs_0_), channel_id=1, source_target_pairs={{1,0},{5,4}} | collective-permute-start | bytes 3145736 | tf_op jit(solution)/shard_map/ppermute | solution.py:263
  169.9 19.8 %collective-permute-start.4 = (bf16[192,1024]{1,0:T(8,128)(2,1)}, bf16[192,1024]{1,0:T(8,128)(2,1)}, u32[]{:S(2)}, u32[]{:S(2)}) collective-permute-start(bf16[192,1024]{1,0:T(8,128)(2,1)} %get-tuple-element.18), channel_id=1, source_target_pairs={{3,1},{1,0},{0,2},{2,3},{7,5},{5,4},{4,6},{6,7}} | collective-permute-start | bytes 1179656 | tf_op jit(solution)/shard_map/ppermute | solution.py:263
  169.9 23.2 %collective-permute-start.3 = (bf16[160,1024]{1,0:T(8,128)(2,1)}, bf16[160,1024]{1,0:T(8,128)(2,1)}, u32[]{:S(2)}, u32[]{:S(2)}) collective-permute-start(bf16[160,1024]{1,0:T(8,128)(2,1)} %get-tuple-element.17), channel_id=1, source_target_pairs={{3,1},{1,0},{0,2},{2,3},{7,5},{5,4},{4,6},{6,7}} | collective-permute-start | bytes 983048 | tf_op jit(solution)/shard_map/ppermute | solution.py:263
  179.7 16.6 %collective-permute-start.2 = (bf16[144,1024]{1,0:T(8,128)(2,1)}, bf16[144,1024]{1,0:T(8,128)(2,1)}, u32[]{:S(2)}, u32[]{:S(2)}) collective-permute-start(bf16[144,1024]{1,0:T(8,128)(2,1)} %get-tuple-element.15), channel_id=1, source_target_pairs={{3,1},{1,0},{0,2},{2,3},{7,5},{5,4},{4,6},{6,7}} | collective-permute-start | bytes 884744 | tf_op jit(solution)/shard_map/ppermute | solution.py:263

commit v10 on v9

--- a/solution.py
+++ b/solution.py
@@ -9,7 +9,8 @@
 WIDE = 512
 HIGH = 1792
 NEXT = [(1, 0), (2, 1), (3, 2), (0, 3)]
-FAR = [(3, 1), (1, 0), (0, 2), (2, 3)]
+FAR = [(3, 1)]
+FAR_HEAD = [(3, 1), (1, 0), (0, 2), (2, 3)]
 PASS = [(1, 0)]
 PARTS = [(0, 192), (192, 1856), (2048, 1024), (3072, 512)]
 GROUPS = [[0, 1], [2], [3]]
@@ -267,7 +268,7 @@
 
     def local(a):
         head = bring(a, *PARTS[0], 58 << 20)
-        far_head = send(head, FAR)
+        far_head = send(head, FAR_HEAD)
         parts = [send(head, NEXT)]
         own = bring(a, 0, a.shape[0], 51 << 20)
         parts += [send(rows_of(own, PARTS[k]), NEXT) for k in range(1, len(PARTS))]

time: 202 us -> 210 us (1.040)
  the two profiles are of different devices: /device:TPU:0 before, /device:TPU:1 now
where the time goes in v10:
time: 210 us; the launch traced here: 209 us
  Pallas kernels  128 us (61%)
  waiting for transfers between devices  38.4 us (18%)
  starting transfers between devices  24.1 us (11%)
  local copies, waits for them, and re-layouts  17.7 us (8%)
    pallas_call x12, Pallas kernels, call(): pl.pallas_call(kernel, in_specs=[pl.BlockSpec(memory_space=space) for _,...  121 us
    ppermute x17, waiting for transfers between devices, send(): return lax.ppermute(a, 'row', pairs)  38.4 us
    ppermute x17, starting transfers between devices, send(): return lax.ppermute(a, 'row', pairs)  24.1 us
    unnamed x10, local copies, waits for them, and re-layouts  9.98 us
    slice x3, local copies, waits for them, and re-layouts, rows_of(): return a[chunk[0]:chunk[0] + chunk[1]]  7.71 us
  transfers between devices with their start and end apart: 17, of which 1 were waited for; matrix products, arithmetic and copies ran while one was open for 3% of the time, Pallas kernels for 58%

profile of v10, /device:TPU:1, one launch (start us, length us, event | category | flops | bytes accessed | tf_op | source)
XLA Modules:
  0.0 208.7 jit_solution(17097101212529294391)
XLA Ops:
  0.0 3.1 %bring.2.own_ref.refs_2_.refs_1_.refs_4_.refs_3_ = bf16[3584,1024]{1,0:T(8,128)(2,1)S(1)} custom-call(bf16[3584,1024]{1,0:T(8,128)(2,1)} %a_ref.3), custom_call_target="tpu_custom_call" | custom-call | bytes 14680064 | tf_op jit(solution)/shard_map/bring/pallas_call | solution.py:87
  3.1 0.0 copy-start
  3.1 2.9 %copy-done = bf16[3584,1024]{1,0:T(8,128)(2,1)} copy-done((bf16[3584,1024]{1,0:T(8,128)(2,1)}, bf16[3584,1024]{1,0:T(8,128)(2,1)S(1)}, u32[]{:S(2)}) %copy-start) | copy-done | bytes 7340056
  6.0 2.3 %slice.14 = bf16[1856,1024]{1,0:T(8,128)(2,1)} slice(bf16[3584,1024]{1,0:T(8,128)(2,1)S(1)} %bring.2.own_ref.refs_2_.refs_1_.refs_4_.refs_3_), slice={[192:2048], [0:1024]} | slice | bytes 7602176 | tf_op jit(solution)/shard_map/slice | solution.py:267
  8.3 0.0 collective-permute-start.9
  8.3 1.0 bring.3
  9.3 2.4 %collective-permute-start.13 = (bf16[192,1024]{1,0:T(8,128)(2,1)S(1)}, bf16[192,1024]{1,0:T(8,128)(2,1)S(1)}, u32[]{:S(2)}, u32[]{:S(2)}) collective-permute-start(bf16[192,1024]{1,0:T(8,128)(2,1)S(1)} %bring.3), channel_id=1, source_target_pairs={{1,0},{2,1},{3,2},{0,3},{5,4},{6,5},{7,6},{4,7}} | collective-permute-start | bytes 1179656 | tf_op jit(solution)/shard_map/ppermute | solution.py:264
  11.8 0.7 collective-permute-start.15
  12.4 3.1 %slice.13 = bf16[1024,1024]{1,0:T(8,128)(2,1)} slice(bf16[3584,1024]{1,0:T(8,128)(2,1)} %copy-done), slice={[2048:3072], [0:1024]} | slice | bytes 4194304 | tf_op jit(solution)/shard_map/slice | solution.py:267
  15.6 0.0 collective-permute-start.5
  15.6 2.3 %slice.12 = bf16[512,1024]{1,0:T(8,128)(2,1)} slice(bf16[3584,1024]{1,0:T(8,128)(2,1)} %copy-done), slice={[3072:3584], [0:1024]} | slice | bytes 2097152 | tf_op jit(solution)/shard_map/slice | solution.py:267
  17.9 1.2 collective-permute-start
  19.1 38.3 %collective-permute-done.9.refs_1_ = bf16[1856,1024]{1,0:T(8,128)(2,1)} collective-permute-done((bf16[1856,1024]{1,0:T(8,128)(2,1)}, bf16[1856,1024]{1,0:T(8,128)(2,1)}, u32[]{:S(2)}, u32[]{:S(2)}) %collective-permute-start.9) | collective-permute-done | bytes 3801120 | tf_op jit(solution)/shard_map/ppermute | solution.py:264
  57.4 3.3 %collective-permute-start.10 = (bf16[1856,1024]{1,0:T(8,128)(2,1)}, bf16[1856,1024]{1,0:T(8,128)(2,1)}, u32[]{:S(2)}, u32[]{:S(2)}) collective-permute-start(bf16[1856,1024]{1,0:T(8,128)(2,1)} %collective-permute-done.9.refs_1_), channel_id=1, source_target_pairs={{1,0},{5,4}} | collective-permute-start | bytes 11403272 | tf_op jit(solution)/shard_map/ppermute | solution.py:264
  60.7 0.0 copy-start.1
  60.7 3.1 %copy-done.1 = bf16[3584,1024]{1,0:T(8,128)(2,1)S(1)} copy-done((bf16[3584,1024]{1,0:T(8,128)(2,1)S(1)}, bf16[3584,1024]{1,0:T(8,128)(2,1)}, u32[]{:S(2)}) %copy-start.1) | copy-done | bytes 7340056
  63.7 31.7 %shard_map.17._ = f32[1,3,3584,3584]{3,2,1,0:T(8,128)} custom-call(bf16[3584,1024]{1,0:T(8,128)(2,1)S(1)} %copy-done.1), custom_call_target="tpu_custom_call" | custom-call | flops 26306674688 | bytes 58720256 | tf_op jit(solution)/shard_map/pallas_call | solution.py:69
  95.5 0.0 copy-start.2
  95.5 0.1 cut.1
  95.6 3.0 %copy-done.2 = bf16[3584,1024]{1,0:T(8,128)(2,1)S(1)} copy-done((bf16[3584,1024]{1,0:T(8,128)(2,1)S(1)}, bf16[3584,1024]{1,0:T(8,128)(2,1)}, u32[]{:S(2)}) %copy-start.2) | copy-done | bytes 7340056
  98.6 2.3 %turn.1 = (bf16[1024,3584]{1,0:T(8,128)(2,1)S(1)}, f32[1,3,3584,3584]{3,2,1,0:T(8,128)}) custom-call(bf16[3584,1024]{1,0:T(8,128)(2,1)S(1)} %copy-done.2, f32[1,3,3584,3584]{3,2,1,0:T(8,128)} %shard_map.17._), custom_call_target="tpu_custom_call", output_to_operand_aliasing={{1}: (1, {})} | custom-call | bytes 14680064 | tf_op jit(solution)/shard_map/turn/pallas_call | solution.py:138
  100.8 0.0 collective-permute-done.13.refs_0_
  100.9 1.3 collective-permute-start.16
  102.2 0.0 collective-permute-done.15.refs_2_
  102.2 1.3 collective-permute-start.14
  103.5 21.1 %shard_map.18.refs_2_ = f32[1,3,3584,3584]{3,2,1,0:T(8,128)} custom-call(bf16[192,1024]{1,0:T(8,128)(2,1)S(1)} %collective-permute-done.13.refs_0_, bf16[1856,1024]{1,0:T(8,128)(2,1)} %collective-permute-done.9.refs_1_, bf16[3584,1024]{1,0:T(8,128)(2,1)S(1)} %copy-done.2, f32[1,3,3584,3584]{3,2,1,0:T(8,128)} %get-tuple-element.24.refs_3_), custom_call_target="tpu_custom_call", output_to_operand_aliasing={{}: (3, {})} | custom-call | flops 15032385536 | bytes 33554432 | tf_op jit(solution)/shard_map/pallas_call | solution.py:69
  124.6 0.0 collective-permute-done.14.refs_0_
  124.6 0.0 copy-start.3
  124.6 1.3 collective-permute-start.12
  125.9 0.0 collective-permute-done.refs_0_
  125.9 1.3 collective-permute-start.11
  127.2 0.0 collective-permute-done.5.refs_0_
  127.2 2.6 %collective-permute-start.6 = (bf16[1024,1024]{1,0:T(8,128)(2,1)}, bf16[1024,1024]{1,0:T(8,128)(2,1)}, u32[]{:S(2)}, u32[]{:S(2)}) collective-permute-start(bf16[1024,1024]{1,0:T(8,128)(2,1)} %collective-permute-done.5.refs_0_), channel_id=1, source_target_pairs={{1,0},{5,4}} | collective-permute-start | bytes 6291464 | tf_op jit(solution)/shard_map/ppermute | solution.py:264
  129.9 12.0 %shard_map.19.refs_2_ = f32[1,3,3584,3584]{3,2,1,0:T(8,128)} custom-call(bf16[1024,1024]{1,0:T(8,128)(2,1)} %collective-permute-done.5.refs_0_, bf16[3584,1024]{1,0:T(8,128)(2,1)S(1)} %copy-done.2, f32[1,3,3584,3584]{3,2,1,0:T(8,128)} %shard_map.18.refs_2_), custom_call_target="tpu_custom_call", output_to_operand_aliasing={{}: (2, {})} | custom-call | flops 7516192768 | bytes 16777216 | tf_op jit(solution)/shard_map/pallas_call | solution.py:69
  141.9 0.0 copy-done.3
  141.9 7.5 %shard_map.20.refs_5_ = f32[1,3,3584,3584]{3,2,1,0:T(8,128)} custom-call(bf16[512,1024]{1,0:T(8,128)(2,1)} %collective-permute-done.refs_0_, bf16[3584,1024]{1,0:T(8,128)(2,1)S(1)} %copy-done.2, f32[1,3,3584,3584]{3,2,1,0:T(8,128)} %shard_map.19.refs_2_), custom_call_target="tpu_custom_call", output_to_operand_aliasing={{}: (2, {})} | custom-call | flops 3758096384 | bytes 8388608 | tf_op jit(solution)/shard_map/pallas_call | solution.py:69
  149.4 0.0 collective-permute-done.16.refs_3_
  149.4 1.3 collective-permute-start.8
  150.7 0.0 collective-permute-done.10.refs_1_.refs_0_
  150.7 1.3 collective-permute-start.7
  152.0 0.0 copy-start.4
  152.0 1.0 copy-done.4
  153.0 10.0 %shard_map.21.refs_3_ = f32[1,3,3584,3584]{3,2,1,0:T(8,128)} custom-call(bf16[192,1024]{1,0:T(8,128)(2,1)S(1)} %copy-done.4, bf16[1856,1024]{1,0:T(8,128)(2,1)} %collective-permute-done.10.refs_1_.refs_0_, bf16[192,1024]{1,0:T(8,128)(2,1)S(1)} %collective-permute-done.15.refs_2_, ...), custom_call_target="tpu_custom_call", output_to_operand_aliasing={{}: (5, {})} | custom-call | flops 5989466112 | bytes 13369344 | tf_op jit(solution)/shard_map/pallas_call | solution.py:69
  163.1 0.0 collective-permute-done.12.refs_1_
  163.1 2.3 %collective-permute-start.1 = (bf16[512,1024]{1,0:T(8,128)(2,1)}, bf16[512,1024]{1,0:T(8,128)(2,1)}, u32[]{:S(2)}, u32[]{:S(2)}) collective-permute-start(bf16[512,1024]{1,0:T(8,128)(2,1)} %collective-permute-done.refs_0_), channel_id=1, source_target_pairs={{1,0},{5,4}} | collective-permute-start | bytes 3145736 | tf_op jit(solution)/shard_map/ppermute | solution.py:264
  165.4 9.8 %shard_map.22.refs_4_ = f32[1,3,3584,3584]{3,2,1,0:T(8,128)} custom-call(bf16[1856,1024]{1,0:T(8,128)(2,1)} %collective-permute-done.10.refs_1_.refs_0_, bf16[768,1024]{1,0:T(8,128)(2,1)} %collective-permute-done.12.refs_1_, bf16[3584,1024]{1,0:T(8,128)(2,1)S(1)} %copy-done.2, f32[1,3,3584,3584]{3,2,1,0:T(8,128)} %shard_map.21.refs_3_), custom_call_target="tpu_custom_call", output_to_operand_aliasing={{}: (3, {})} | custom-call | flops 5637144576 | bytes 12582912 | tf_op jit(solution)/shard_map/pallas_call | solution.py:69
  175.2 0.0 collective-permute-done.11.refs_2_
  175.2 1.3 collective-permute-start.4
  176.5 0.0 collective-permute-done.6.refs_1_.refs_0_
  176.5 1.3 collective-permute-start.3
  177.8 9.8 %shard_map.23.refs_3_ = f32[1,3,3584,3584]{3,2,1,0:T(8,128)} custom-call(bf16[1856,1024]{1,0:T(8,128)(2,1)} %collective-permute-done.10.refs_1_.refs_0_, bf16[1024,1024]{1,0:T(8,128)(2,1)} %collective-permute-done.6.refs_1_.refs_0_, bf16[768,1024]{1,0:T(8,128)(2,1)} %collective-permute-done.11.refs_2_, ...), custom_call_target="tpu_custom_call", output_to_operand_aliasing={{}: (4, {})} | custom-call | flops 5637144576 | bytes 12582912 | tf_op jit(solution)/shard_map/pallas_call | solution.py:69
  187.6 0.0 collective-permute-done.8.refs_1_
  187.6 1.3 collective-permute-start.2
  188.9 5.8 %shard_map.24.refs_4_ = f32[1,3,3584,3584]{3,2,1,0:T(8,128)} custom-call(bf16[1024,1024]{1,0:T(8,128)(2,1)} %collective-permute-done.6.refs_1_.refs_0_, bf16[464,1024]{1,0:T(8,128)(2,1)} %collective-permute-done.8.refs_1_, bf16[1024,3584]{1,0:T(8,128)(2,1)S(1)} %get-tuple-element.16.refs_2_.refs_3_, ...), custom_call_target="tpu_custom_call", output_to_operand_aliasing={{}: (3, {})} | custom-call | flops 3405774848 | bytes 7602176 | tf_op jit(solution)/shard_map/pallas_call | solution.py:69
  194.7 0.0 collective-permute-done.7.refs_2_
  194.7 0.0 collective-permute-done.1.refs_1_.refs_0_
  194.7 4.1 %shard_map.25.refs_3_ = f32[1,3,3584,3584]{3,2,1,0:T(8,128)} custom-call(bf16[1024,1024]{1,0:T(8,128)(2,1)} %collective-permute-done.6.refs_1_.refs_0_, bf16[512,1024]{1,0:T(8,128)(2,1)} %collective-permute-done.1.refs_1_.refs_0_, bf16[272,1024]{1,0:T(8,128)(2,1)} %collective-permute-done.7.refs_2_, ...), custom_call_target="tpu_custom_call", output_to_operand_aliasing={{}: (4, {})} | custom-call | flops 1996488704 | bytes 4456448 | tf_op jit(solution)/shard_map/pallas_call | solution.py:69
  198.9 0.0 collective-permute-done.4.refs_1_
  198.9 3.4 %shard_map.26.refs_3_ = f32[1,3,3584,3584]{3,2,1,0:T(8,128)} custom-call(bf16[512,1024]{1,0:T(8,128)(2,1)} %collective-permute-done.1.refs_1_.refs_0_, bf16[192,1024]{1,0:T(8,128)(2,1)} %collective-permute-done.4.refs_1_, bf16[1024,3584]{1,0:T(8,128)(2,1)S(1)} %get-tuple-element.16.refs_2_.refs_3_, ...), custom_call_target="tpu_custom_call", output_to_operand_aliasing={{}: (3, {})} | custom-call | flops 1409286144 | bytes 3145728 | tf_op jit(solution)/shard_map/pallas_call | solution.py:69
  202.3 0.0 collective-permute-done.3.refs_1_
  202.3 3.2 %shard_map.27.refs_3_ = f32[1,3,3584,3584]{3,2,1,0:T(8,128)} custom-call(bf16[512,1024]{1,0:T(8,128)(2,1)} %collective-permute-done.1.refs_1_.refs_0_, bf16[160,1024]{1,0:T(8,128)(2,1)} %collective-permute-done.3.refs_1_, bf16[1024,3584]{1,0:T(8,128)(2,1)S(1)} %get-tuple-element.16.refs_2_.refs_3_, ...), custom_call_target="tpu_custom_call", output_to_operand_aliasing={{}: (3, {})} | custom-call | flops 1174405120 | bytes 2621440 | tf_op jit(solution)/shard_map/pallas_call | solution.py:69
  205.5 0.0 collective-permute-done.2.refs_1_
  205.5 3.0 %shard_map.28 = f32[1,3,3584,3584]{3,2,1,0:T(8,128)} custom-call(bf16[512,1024]{1,0:T(8,128)(2,1)} %collective-permute-done.1.refs_1_.refs_0_, bf16[144,1024]{1,0:T(8,128)(2,1)} %collective-permute-done.2.refs_1_, bf16[1024,3584]{1,0:T(8,128)(2,1)S(1)} %get-tuple-element.16.refs_2_.refs_3_, ...), custom_call_target="tpu_custom_call", output_to_operand_aliasing={{}: (3, {})} | custom-call | flops 1056964608 | bytes 2359296 | tf_op jit(solution)/shard_map/pallas_call | solution.py:69
Async XLA Ops:
  3.1 2.9 %copy-start = (bf16[3584,1024]{1,0:T(8,128)(2,1)}, bf16[3584,1024]{1,0:T(8,128)(2,1)S(1)}, u32[]{:S(2)}) copy-start(bf16[3584,1024]{1,0:T(8,128)(2,1)S(1)} %bring.2.own_ref.refs_2_.refs_1_.refs_4_.refs_3_) | copy-start | bytes 22020100
  8.3 49.1 %collective-permute-start.9 = (bf16[1856,1024]{1,0:T(8,128)(2,1)}, bf16[1856,1024]{1,0:T(8,128)(2,1)}, u32[]{:S(2)}, u32[]{:S(2)}) collective-permute-start(bf16[1856,1024]{1,0:T(8,128)(2,1)} %slice.14), channel_id=1, source_target_pairs={{1,0},{2,1},{3,2},{0,3},{5,4},{6,5},{7,6},{4,7}} | collective-permute-start | bytes 11403272 | tf_op jit(solution)/shard_map/ppermute | solution.py:264
  9.3 91.5 %collective-permute-start.13 = (bf16[192,1024]{1,0:T(8,128)(2,1)S(1)}, bf16[192,1024]{1,0:T(8,128)(2,1)S(1)}, u32[]{:S(2)}, u32[]{:S(2)}) collective-permute-start(bf16[192,1024]{1,0:T(8,128)(2,1)S(1)} %bring.3), channel_id=1, source_target_pairs={{1,0},{2,1},{3,2},{0,3},{5,4},{6,5},{7,6},{4,7}} | collective-permute-start | bytes 1179656 | tf_op jit(solution)/shard_map/ppermute | solution.py:264
  11.8 90.4 %collective-permute-start.15 = (bf16[192,1024]{1,0:T(8,128)(2,1)S(1)}, bf16[192,1024]{1,0:T(8,128)(2,1)S(1)}, u32[]{:S(2)}, u32[]{:S(2)}) collective-permute-start(bf16[192,1024]{1,0:T(8,128)(2,1)S(1)} %bring.3), channel_id=1, source_target_pairs={{3,1},{1,0},{0,2},{2,3},{7,5},{5,4},{4,6},{6,7}} | collective-permute-start | bytes 1179656 | tf_op jit(solution)/shard_map/ppermute | solution.py:264
  15.6 111.6 %collective-permute-start.5 = (bf16[1024,1024]{1,0:T(8,128)(2,1)}, bf16[1024,1024]{1,0:T(8,128)(2,1)}, u32[]{:S(2)}, u32[]{:S(2)}) collective-permute-start(bf16[1024,1024]{1,0:T(8,128)(2,1)} %slice.13), channel_id=1, source_target_pairs={{1,0},{2,1},{3,2},{0,3},{5,4},{6,5},{7,6},{4,7}} | collective-permute-start | bytes 6291464 | tf_op jit(solution)/shard_map/ppermute | solution.py:264
  17.9 108.0 %collective-permute-start = (bf16[512,1024]{1,0:T(8,128)(2,1)}, bf16[512,1024]{1,0:T(8,128)(2,1)}, u32[]{:S(2)}, u32[]{:S(2)}) collective-permute-start(bf16[512,1024]{1,0:T(8,128)(2,1)} %slice.12), channel_id=1, source_target_pairs={{1,0},{2,1},{3,2},{0,3},{5,4},{6,5},{7,6},{4,7}} | collective-permute-start | bytes 3145736 | tf_op jit(solution)/shard_map/ppermute | solution.py:264
  57.4 93.3 %collective-permute-start.10 = (bf16[1856,1024]{1,0:T(8,128)(2,1)}, bf16[1856,1024]{1,0:T(8,128)(2,1)}, u32[]{:S(2)}, u32[]{:S(2)}) collective-permute-start(bf16[1856,1024]{1,0:T(8,128)(2,1)} %collective-permute-done.9.refs_1_), channel_id=1, source_target_pairs={{1,0},{5,4}} | collective-permute-start | bytes 11403272 | tf_op jit(solution)/shard_map/ppermute | solution.py:264
  60.7 3.1 %copy-start.1 = (bf16[3584,1024]{1,0:T(8,128)(2,1)S(1)}, bf16[3584,1024]{1,0:T(8,128)(2,1)}, u32[]{:S(2)}) copy-start(bf16[3584,1024]{1,0:T(8,128)(2,1)} %copy-done) | copy-start | bytes 22020100
  95.5 3.1 %copy-start.2 = (bf16[3584,1024]{1,0:T(8,128)(2,1)S(1)}, bf16[3584,1024]{1,0:T(8,128)(2,1)}, u32[]{:S(2)}) copy-start(bf16[3584,1024]{1,0:T(8,128)(2,1)} %copy-done) | copy-start | bytes 22020100
  100.9 48.6 %collective-permute-start.16 = (bf16[624,1024]{1,0:T(8,128)(2,1)}, bf16[624,1024]{1,0:T(8,128)(2,1)}, u32[]{:S(2)}, u32[]{:S(2)}) collective-permute-start(bf16[624,1024]{1,0:T(8,128)(2,1)} %get-tuple-element.23), channel_id=1, source_target_pairs={{3,1},{7,5}} | collective-permute-start | bytes 3833864 | tf_op jit(solution)/shard_map/ppermute | solution.py:264
  102.2 22.4 %collective-permute-start.14 = (bf16[192,1024]{1,0:T(8,128)(2,1)S(1)}, bf16[192,1024]{1,0:T(8,128)(2,1)S(1)}, u32[]{:S(2)}, u32[]{:S(2)}) collective-permute-start(bf16[192,1024]{1,0:T(8,128)(2,1)S(1)} %collective-permute-done.13.refs_0_), channel_id=1, source_target_pairs={{1,0},{5,4}} | collective-permute-start | bytes 1179656 | tf_op jit(solution)/shard_map/ppermute | solution.py:264
  124.6 17.3 %copy-start.3 = (bf16[192,1024]{1,0:T(8,128)(2,1)}, bf16[192,1024]{1,0:T(8,128)(2,1)S(1)}, u32[]{:S(2)}) copy-start(bf16[192,1024]{1,0:T(8,128)(2,1)S(1)} %collective-permute-done.14.refs_0_) | copy-start | bytes 1179652
  124.6 38.5 %collective-permute-start.12 = (bf16[768,1024]{1,0:T(8,128)(2,1)}, bf16[768,1024]{1,0:T(8,128)(2,1)}, u32[]{:S(2)}, u32[]{:S(2)}) collective-permute-start(bf16[768,1024]{1,0:T(8,128)(2,1)} %get-tuple-element.22), channel_id=1, source_target_pairs={{3,1},{7,5}} | collective-permute-start | bytes 4718600 | tf_op jit(solution)/shard_map/ppermute | solution.py:264
  125.9 49.2 %collective-permute-start.11 = (bf16[768,1024]{1,0:T(8,128)(2,1)}, bf16[768,1024]{1,0:T(8,128)(2,1)}, u32[]{:S(2)}, u32[]{:S(2)}) collective-permute-start(bf16[768,1024]{1,0:T(8,128)(2,1)} %get-tuple-element.21), channel_id=1, source_target_pairs={{3,1},{7,5}} | collective-permute-start | bytes 4718600 | tf_op jit(solution)/shard_map/ppermute | solution.py:264
  127.2 49.2 %collective-permute-start.6 = (bf16[1024,1024]{1,0:T(8,128)(2,1)}, bf16[1024,1024]{1,0:T(8,128)(2,1)}, u32[]{:S(2)}, u32[]{:S(2)}) collective-permute-start(bf16[1024,1024]{1,0:T(8,128)(2,1)} %collective-permute-done.5.refs_0_), channel_id=1, source_target_pairs={{1,0},{5,4}} | collective-permute-start | bytes 6291464 | tf_op jit(solution)/shard_map/ppermute | solution.py:264
  149.4 38.1 %collective-permute-start.8 = (bf16[464,1024]{1,0:T(8,128)(2,1)}, bf16[464,1024]{1,0:T(8,128)(2,1)}, u32[]{:S(2)}, u32[]{:S(2)}) collective-permute-start(bf16[464,1024]{1,0:T(8,128)(2,1)} %get-tuple-element.20), channel_id=1, source_target_pairs={{3,1},{7,5}} | collective-permute-start | bytes 2850824 | tf_op jit(solution)/shard_map/ppermute | solution.py:264
  150.7 44.0 %collective-permute-start.7 = (bf16[272,1024]{1,0:T(8,128)(2,1)}, bf16[272,1024]{1,0:T(8,128)(2,1)}, u32[]{:S(2)}, u32[]{:S(2)}) collective-permute-start(bf16[272,1024]{1,0:T(8,128)(2,1)} %get-tuple-element.19), channel_id=1, source_target_pairs={{3,1},{7,5}} | collective-permute-start | bytes 1671176 | tf_op jit(solution)/shard_map/ppermute | solution.py:264
  152.0 1.0 copy-start.4
  163.1 31.6 %collective-permute-start.1 = (bf16[512,1024]{1,0:T(8,128)(2,1)}, bf16[512,1024]{1,0:T(8,128)(2,1)}, u32[]{:S(2)}, u32[]{:S(2)}) collective-permute-start(bf16[512,1024]{1,0:T(8,128)(2,1)} %collective-permute-done.refs_0_), channel_id=1, source_target_pairs={{1,0},{5,4}} | collective-permute-start | bytes 3145736 | tf_op jit(solution)/shard_map/ppermute | solution.py:264
  175.2 23.7 %collective-permute-start.4 = (bf16[192,1024]{1,0:T(8,128)(2,1)}, bf16[192,1024]{1,0:T(8,128)(2,1)}, u32[]{:S(2)}, u32[]{:S(2)}) collective-permute-start(bf16[192,1024]{1,0:T(8,128)(2,1)} %get-tuple-element.18), channel_id=1, source_target_pairs={{3,1},{7,5}} | collective-permute-start | bytes 1179656 | tf_op jit(solution)/shard_map/ppermute | solution.py:264
  176.5 25.8 %collective-permute-start.3 = (bf16[160,1024]{1,0:T(8,128)(2,1)}, bf16[160,1024]{1,0:T(8,128)(2,1)}, u32[]{:S(2)}, u32[]{:S(2)}) collective-permute-start(bf16[160,1024]{1,0:T(8,128)(2,1)} %get-tuple-element.17), channel_id=1, source_target_pairs={{3,1},{7,5}} | collective-permute-start | bytes 983048 | tf_op jit(solution)/shard_map/ppermute | solution.py:264
  187.6 17.9 %collective-permute-start.2 = (bf16[144,1024]{1,0:T(8,128)(2,1)}, bf16[144,1024]{1,0:T(8,128)(2,1)}, u32[]{:S(2)}, u32[]{:S(2)}) collective-permute-start(bf16[144,1024]{1,0:T(8,128)(2,1)} %get-tuple-element.15), channel_id=1, source_target_pairs={{3,1},{7,5}} | collective-permute-start | bytes 884744 | tf_op jit(solution)/shard_map/ppermute | solution.py:264

commit v11 on v10

--- a/solution.py
+++ b/solution.py
@@ -12,8 +12,8 @@
 FAR = [(3, 1)]
 FAR_HEAD = [(3, 1), (1, 0), (0, 2), (2, 3)]
 PASS = [(1, 0)]
-PARTS = [(0, 192), (192, 1856), (2048, 1024), (3072, 512)]
-GROUPS = [[0, 1], [2], [3]]
+PARTS = [(0, 144), (144, 1904), (2048, 1024), (3072, 512)]
+GROUPS = [[0, 1], [2, 3]]
 FARS = [(0, 816), (816, 768), (1584, 768), (2352, 464), (2816, 272), (3088, 192), (3280, 160), (3440, 144)]
 HEAD = PARTS[0][1]
 SENDS = [(HEAD, FARS[0][1] - HEAD)] + FARS[1:]
@@ -218,7 +218,9 @@
         def _():
             if len(far) > 1:
                 held[:HEAD, :] = far_refs[0][...]
-            load(far_refs[-1], held.at[pl.ds(size - far[-1].shape[0], far[-1].shape[0]), :], load_sem)
+                held[HEAD:, :] = far_refs[1][...]
+            else:
+                load(far_refs[0], held, load_sem)
 
         if size > FEW:
 
@@ -253,7 +255,7 @@
 
     bufs = DEPTH if size > FEW else rows // WIDE
     scratch = [pltpu.VMEM((size, depth), jnp.bfloat16), pltpu.VMEM((bufs, size, WIDE), jnp.float32)]
-    refs = [(part, pl.ANY) for part, *_ in near] + [(part, pltpu.VMEM) for part in far[:-1]] + [(far[-1], pl.ANY), (own, pltpu.VMEM)]
+    refs = [(part, pl.ANY) for part, *_ in near] + [(part, pltpu.VMEM if len(far) > 1 else pl.ANY) for part in far] + [(own, pltpu.VMEM)]
     return call(kernel, size, rows, depth, out, refs, scratch)
 
 

time: 210 us -> 206 us (0.981)
  Pallas kernels: 128 us -> 125 us
    pallas_call x12 -> x11, Pallas kernels: 121 us -> 118 us  [call(): pl.pallas_call(kernel, in_specs=[pl.BlockSpec(memory_space=space) for _,...]
    unnamed x10 -> x6, local copies, waits for them, and re-layouts: 9.98 us -> 9 us
where the time goes in v11:
time: 206 us; the launch traced here: 205 us
  Pallas kernels  125 us (61%)
  waiting for transfers between devices  38.4 us (19%)
  starting transfers between devices  24.2 us (12%)
  local copies, waits for them, and re-layouts  16.7 us (8%)
    pallas_call x11, Pallas kernels, call(): pl.pallas_call(kernel, in_specs=[pl.BlockSpec(memory_space=space) for _,...  118 us
    ppermute x17, waiting for transfers between devices, send(): return lax.ppermute(a, 'row', pairs)  38.4 us
    ppermute x17, starting transfers between devices, send(): return lax.ppermute(a, 'row', pairs)  24.2 us
    unnamed x6, local copies, waits for them, and re-layouts  9 us
    slice x3, local copies, waits for them, and re-layouts, rows_of(): return a[chunk[0]:chunk[0] + chunk[1]]  7.73 us
  transfers between devices with their start and end apart: 17, of which 1 were waited for; matrix products, arithmetic and copies ran while one was open for 3% of the time, Pallas kernels for 58%

profile of v11, /device:TPU:1, one launch (start us, length us, event | category | flops | bytes accessed | tf_op | source)
XLA Modules:
  0.0 204.7 jit_solution(3499260207687335638)
XLA Ops:
  0.0 3.1 %bring.2.own_ref.refs_2_.refs_4_.refs_3_ = bf16[3584,1024]{1,0:T(8,128)(2,1)S(1)} custom-call(bf16[3584,1024]{1,0:T(8,128)(2,1)} %a_ref.3), custom_call_target="tpu_custom_call" | custom-call | bytes 14680064 | tf_op jit(solution)/shard_map/bring/pallas_call | solution.py:87
  3.1 0.0 copy-start
  3.1 2.9 %copy-done = bf16[3584,1024]{1,0:T(8,128)(2,1)} copy-done((bf16[3584,1024]{1,0:T(8,128)(2,1)}, bf16[3584,1024]{1,0:T(8,128)(2,1)S(1)}, u32[]{:S(2)}) %copy-start) | copy-done | bytes 7340056
  6.1 2.3 %slice.14 = bf16[1904,1024]{1,0:T(8,128)(2,1)} slice(bf16[3584,1024]{1,0:T(8,128)(2,1)S(1)} %bring.2.own_ref.refs_2_.refs_4_.refs_3_), slice={[144:2048], [0:1024]} | slice | bytes 7798784 | tf_op jit(solution)/shard_map/slice | solution.py:269
  8.4 0.0 collective-permute-start.9
  8.4 1.0 bring.3
  9.3 2.4 %collective-permute-start.13 = (bf16[144,1024]{1,0:T(8,128)(2,1)S(1)}, bf16[144,1024]{1,0:T(8,128)(2,1)S(1)}, u32[]{:S(2)}, u32[]{:S(2)}) collective-permute-start(bf16[144,1024]{1,0:T(8,128)(2,1)S(1)} %bring.3), channel_id=1, source_target_pairs={{1,0},{2,1},{3,2},{0,3},{5,4},{6,5},{7,6},{4,7}} | collective-permute-start | bytes 884744 | tf_op jit(solution)/shard_map/ppermute | solution.py:266
  11.8 0.7 collective-permute-start.15
  12.5 3.1 %slice.13 = bf16[1024,1024]{1,0:T(8,128)(2,1)} slice(bf16[3584,1024]{1,0:T(8,128)(2,1)} %copy-done), slice={[2048:3072], [0:1024]} | slice | bytes 4194304 | tf_op jit(solution)/shard_map/slice | solution.py:269
  15.6 0.0 collective-permute-start.5
  15.6 2.3 %slice.12 = bf16[512,1024]{1,0:T(8,128)(2,1)} slice(bf16[3584,1024]{1,0:T(8,128)(2,1)} %copy-done), slice={[3072:3584], [0:1024]} | slice | bytes 2097152 | tf_op jit(solution)/shard_map/slice | solution.py:269
  17.9 1.2 collective-permute-start
  19.1 38.4 %collective-permute-done.9.refs_1_ = bf16[1904,1024]{1,0:T(8,128)(2,1)} collective-permute-done((bf16[1904,1024]{1,0:T(8,128)(2,1)}, bf16[1904,1024]{1,0:T(8,128)(2,1)}, u32[]{:S(2)}, u32[]{:S(2)}) %collective-permute-start.9) | collective-permute-done | bytes 3899424 | tf_op jit(solution)/shard_map/ppermute | solution.py:266
  57.5 3.3 %collective-permute-start.10 = (bf16[1904,1024]{1,0:T(8,128)(2,1)}, bf16[1904,1024]{1,0:T(8,128)(2,1)}, u32[]{:S(2)}, u32[]{:S(2)}) collective-permute-start(bf16[1904,1024]{1,0:T(8,128)(2,1)} %collective-permute-done.9.refs_1_), channel_id=1, source_target_pairs={{1,0},{5,4}} | collective-permute-start | bytes 11698184 | tf_op jit(solution)/shard_map/ppermute | solution.py:266
  60.7 0.0 copy-start.1
  60.7 3.1 %copy-done.1 = bf16[3584,1024]{1,0:T(8,128)(2,1)S(1)} copy-done((bf16[3584,1024]{1,0:T(8,128)(2,1)S(1)}, bf16[3584,1024]{1,0:T(8,128)(2,1)}, u32[]{:S(2)}) %copy-start.1) | copy-done | bytes 7340056
  63.8 31.7 %shard_map.17._ = f32[1,3,3584,3584]{3,2,1,0:T(8,128)} custom-call(bf16[3584,1024]{1,0:T(8,128)(2,1)S(1)} %copy-done.1), custom_call_target="tpu_custom_call" | custom-call | flops 26306674688 | bytes 58720256 | tf_op jit(solution)/shard_map/pallas_call | solution.py:69
  95.6 0.0 copy-start.2
  95.6 0.1 cut.1
  95.7 3.0 %copy-done.2 = bf16[3584,1024]{1,0:T(8,128)(2,1)S(1)} copy-done((bf16[3584,1024]{1,0:T(8,128)(2,1)S(1)}, bf16[3584,1024]{1,0:T(8,128)(2,1)}, u32[]{:S(2)}) %copy-start.2) | copy-done | bytes 7340056
  98.7 2.3 %turn.1 = (bf16[1024,3584]{1,0:T(8,128)(2,1)S(1)}, f32[1,3,3584,3584]{3,2,1,0:T(8,128)}) custom-call(bf16[3584,1024]{1,0:T(8,128)(2,1)S(1)} %copy-done.2, f32[1,3,3584,3584]{3,2,1,0:T(8,128)} %shard_map.17._), custom_call_target="tpu_custom_call", output_to_operand_aliasing={{1}: (1, {})} | custom-call | bytes 14680064 | tf_op jit(solution)/shard_map/turn/pallas_call | solution.py:138
  100.9 0.0 collective-permute-done.13.refs_0_
  101.0 1.3 collective-permute-start.16
  102.3 0.0 collective-permute-done.15.refs_2_
  102.3 1.3 collective-permute-start.14
  103.6 21.0 %shard_map.18.refs_3_ = f32[1,3,3584,3584]{3,2,1,0:T(8,128)} custom-call(bf16[144,1024]{1,0:T(8,128)(2,1)S(1)} %collective-permute-done.13.refs_0_, bf16[1904,1024]{1,0:T(8,128)(2,1)} %collective-permute-done.9.refs_1_, bf16[3584,1024]{1,0:T(8,128)(2,1)S(1)} %copy-done.2, f32[1,3,3584,3584]{3,2,1,0:T(8,128)} %get-tuple-element.24.refs_3_), custom_call_target="tpu_custom_call", output_to_operand_aliasing={{}: (3, {})} | custom-call | flops 15032385536 | bytes 33554432 | tf_op jit(solution)/shard_map/pallas_call | solution.py:69
  124.6 0.0 collective-permute-done.14.refs_0_
  124.6 1.3 collective-permute-start.12
  125.9 0.0 collective-permute-done.refs_1_
  125.9 1.3 collective-permute-start.11
  127.2 0.0 collective-permute-done.5.refs_0_
  127.2 2.6 %collective-permute-start.6 = (bf16[1024,1024]{1,0:T(8,128)(2,1)}, bf16[1024,1024]{1,0:T(8,128)(2,1)}, u32[]{:S(2)}, u32[]{:S(2)}) collective-permute-start(bf16[1024,1024]{1,0:T(8,128)(2,1)} %collective-permute-done.5.refs_0_), channel_id=1, source_target_pairs={{1,0},{5,4}} | collective-permute-start | bytes 6291464 | tf_op jit(solution)/shard_map/ppermute | solution.py:266
  129.8 16.5 %shard_map.19.refs_5_ = f32[1,3,3584,3584]{3,2,1,0:T(8,128)} custom-call(bf16[1024,1024]{1,0:T(8,128)(2,1)} %collective-permute-done.5.refs_0_, bf16[512,1024]{1,0:T(8,128)(2,1)} %collective-permute-done.refs_1_, bf16[3584,1024]{1,0:T(8,128)(2,1)S(1)} %copy-done.2, f32[1,3,3584,3584]{3,2,1,0:T(8,128)} %shard_map.18.refs_3_), custom_call_target="tpu_custom_call", output_to_operand_aliasing={{}: (3, {})} | custom-call | flops 11274289152 | bytes 25165824 | tf_op jit(solution)/shard_map/pallas_call | solution.py:69
  146.3 0.0 collective-permute-done.16.refs_3_
  146.4 1.3 collective-permute-start.8
  147.7 0.0 collective-permute-done.10.refs_1_.refs_0_
  147.7 1.3 collective-permute-start.7
  149.0 10.2 %shard_map.20.refs_3_ = f32[1,3,3584,3584]{3,2,1,0:T(8,128)} custom-call(bf16[144,1024]{1,0:T(8,128)(2,1)S(1)} %collective-permute-done.14.refs_0_, bf16[1904,1024]{1,0:T(8,128)(2,1)} %collective-permute-done.10.refs_1_.refs_0_, bf16[144,1024]{1,0:T(8,128)(2,1)S(1)} %collective-permute-done.15.refs_2_, ...), custom_call_target="tpu_custom_call", output_to_operand_aliasing={{}: (5, {})} | custom-call | flops 5989466112 | bytes 13369344 | tf_op jit(solution)/shard_map/pallas_call | solution.py:69
  159.2 0.0 collective-permute-done.12.refs_1_
  159.2 2.3 %collective-permute-start.1 = (bf16[512,1024]{1,0:T(8,128)(2,1)}, bf16[512,1024]{1,0:T(8,128)(2,1)}, u32[]{:S(2)}, u32[]{:S(2)}) collective-permute-start(bf16[512,1024]{1,0:T(8,128)(2,1)} %collective-permute-done.refs_1_), channel_id=1, source_target_pairs={{1,0},{5,4}} | collective-permute-start | bytes 3145736 | tf_op jit(solution)/shard_map/ppermute | solution.py:266
  161.4 9.8 %shard_map.21.refs_4_ = f32[1,3,3584,3584]{3,2,1,0:T(8,128)} custom-call(bf16[1904,1024]{1,0:T(8,128)(2,1)} %collective-permute-done.10.refs_1_.refs_0_, bf16[768,1024]{1,0:T(8,128)(2,1)} %collective-permute-done.12.refs_1_, bf16[3584,1024]{1,0:T(8,128)(2,1)S(1)} %copy-done.2, f32[1,3,3584,3584]{3,2,1,0:T(8,128)} %shard_map.20.refs_3_), custom_call_target="tpu_custom_call", output_to_operand_aliasing={{}: (3, {})} | custom-call | flops 5637144576 | bytes 12582912 | tf_op jit(solution)/shard_map/pallas_call | solution.py:69
  171.2 0.0 collective-permute-done.11.refs_2_
  171.2 1.3 collective-permute-start.4
  172.5 0.0 collective-permute-done.6.refs_1_.refs_0_
  172.5 1.3 collective-permute-start.3
  173.8 9.8 %shard_map.22.refs_3_ = f32[1,3,3584,3584]{3,2,1,0:T(8,128)} custom-call(bf16[1904,1024]{1,0:T(8,128)(2,1)} %collective-permute-done.10.refs_1_.refs_0_, bf16[1024,1024]{1,0:T(8,128)(2,1)} %collective-permute-done.6.refs_1_.refs_0_, bf16[768,1024]{1,0:T(8,128)(2,1)} %collective-permute-done.11.refs_2_, ...), custom_call_target="tpu_custom_call", output_to_operand_aliasing={{}: (4, {})} | custom-call | flops 5637144576 | bytes 12582912 | tf_op jit(solution)/shard_map/pallas_call | solution.py:69
  183.6 0.0 collective-permute-done.8.refs_1_
  183.6 1.3 collective-permute-start.2
  184.9 5.8 %shard_map.23.refs_4_ = f32[1,3,3584,3584]{3,2,1,0:T(8,128)} custom-call(bf16[1024,1024]{1,0:T(8,128)(2,1)} %collective-permute-done.6.refs_1_.refs_0_, bf16[464,1024]{1,0:T(8,128)(2,1)} %collective-permute-done.8.refs_1_, bf16[1024,3584]{1,0:T(8,128)(2,1)S(1)} %get-tuple-element.16.refs_2_.refs_3_, ...), custom_call_target="tpu_custom_call", output_to_operand_aliasing={{}: (3, {})} | custom-call | flops 3405774848 | bytes 7602176 | tf_op jit(solution)/shard_map/pallas_call | solution.py:69
  190.8 0.0 collective-permute-done.7.refs_2_
  190.8 0.0 collective-permute-done.1.refs_1_.refs_0_
  190.8 4.1 %shard_map.24.refs_3_ = f32[1,3,3584,3584]{3,2,1,0:T(8,128)} custom-call(bf16[1024,1024]{1,0:T(8,128)(2,1)} %collective-permute-done.6.refs_1_.refs_0_, bf16[512,1024]{1,0:T(8,128)(2,1)} %collective-permute-done.1.refs_1_.refs_0_, bf16[272,1024]{1,0:T(8,128)(2,1)} %collective-permute-done.7.refs_2_, ...), custom_call_target="tpu_custom_call", output_to_operand_aliasing={{}: (4, {})} | custom-call | flops 1996488704 | bytes 4456448 | tf_op jit(solution)/shard_map/pallas_call | solution.py:69
  194.9 0.0 collective-permute-done.4.refs_1_
  194.9 3.4 %shard_map.25.refs_3_ = f32[1,3,3584,3584]{3,2,1,0:T(8,128)} custom-call(bf16[512,1024]{1,0:T(8,128)(2,1)} %collective-permute-done.1.refs_1_.refs_0_, bf16[192,1024]{1,0:T(8,128)(2,1)} %collective-permute-done.4.refs_1_, bf16[1024,3584]{1,0:T(8,128)(2,1)S(1)} %get-tuple-element.16.refs_2_.refs_3_, ...), custom_call_target="tpu_custom_call", output_to_operand_aliasing={{}: (3, {})} | custom-call | flops 1409286144 | bytes 3145728 | tf_op jit(solution)/shard_map/pallas_call | solution.py:69
  198.4 0.0 collective-permute-done.3.refs_1_
  198.4 3.2 %shard_map.26.refs_3_ = f32[1,3,3584,3584]{3,2,1,0:T(8,128)} custom-call(bf16[512,1024]{1,0:T(8,128)(2,1)} %collective-permute-done.1.refs_1_.refs_0_, bf16[160,1024]{1,0:T(8,128)(2,1)} %collective-permute-done.3.refs_1_, bf16[1024,3584]{1,0:T(8,128)(2,1)S(1)} %get-tuple-element.16.refs_2_.refs_3_, ...), custom_call_target="tpu_custom_call", output_to_operand_aliasing={{}: (3, {})} | custom-call | flops 1174405120 | bytes 2621440 | tf_op jit(solution)/shard_map/pallas_call | solution.py:69
  201.5 0.0 collective-permute-done.2.refs_1_
  201.6 3.0 %shard_map.27 = f32[1,3,3584,3584]{3,2,1,0:T(8,128)} custom-call(bf16[512,1024]{1,0:T(8,128)(2,1)} %collective-permute-done.1.refs_1_.refs_0_, bf16[144,1024]{1,0:T(8,128)(2,1)} %collective-permute-done.2.refs_1_, bf16[1024,3584]{1,0:T(8,128)(2,1)S(1)} %get-tuple-element.16.refs_2_.refs_3_, ...), custom_call_target="tpu_custom_call", output_to_operand_aliasing={{}: (3, {})} | custom-call | flops 1056964608 | bytes 2359296 | tf_op jit(solution)/shard_map/pallas_call | solution.py:69
Async XLA Ops:
  3.1 3.0 %copy-start = (bf16[3584,1024]{1,0:T(8,128)(2,1)}, bf16[3584,1024]{1,0:T(8,128)(2,1)S(1)}, u32[]{:S(2)}) copy-start(bf16[3584,1024]{1,0:T(8,128)(2,1)S(1)} %bring.2.own_ref.refs_2_.refs_4_.refs_3_) | copy-start | bytes 22020100
  8.4 49.1 %collective-permute-start.9 = (bf16[1904,1024]{1,0:T(8,128)(2,1)}, bf16[1904,1024]{1,0:T(8,128)(2,1)}, u32[]{:S(2)}, u32[]{:S(2)}) collective-permute-start(bf16[1904,1024]{1,0:T(8,128)(2,1)} %slice.14), channel_id=1, source_target_pairs={{1,0},{2,1},{3,2},{0,3},{5,4},{6,5},{7,6},{4,7}} | collective-permute-start | bytes 11698184 | tf_op jit(solution)/shard_map/ppermute | solution.py:266
  9.3 91.6 %collective-permute-start.13 = (bf16[144,1024]{1,0:T(8,128)(2,1)S(1)}, bf16[144,1024]{1,0:T(8,128)(2,1)S(1)}, u32[]{:S(2)}, u32[]{:S(2)}) collective-permute-start(bf16[144,1024]{1,0:T(8,128)(2,1)S(1)} %bring.3), channel_id=1, source_target_pairs={{1,0},{2,1},{3,2},{0,3},{5,4},{6,5},{7,6},{4,7}} | collective-permute-start | bytes 884744 | tf_op jit(solution)/shard_map/ppermute | solution.py:266
  11.8 90.5 %collective-permute-start.15 = (bf16[144,1024]{1,0:T(8,128)(2,1)S(1)}, bf16[144,1024]{1,0:T(8,128)(2,1)S(1)}, u32[]{:S(2)}, u32[]{:S(2)}) collective-permute-start(bf16[144,1024]{1,0:T(8,128)(2,1)S(1)} %bring.3), channel_id=1, source_target_pairs={{3,1},{1,0},{0,2},{2,3},{7,5},{5,4},{4,6},{6,7}} | collective-permute-start | bytes 884744 | tf_op jit(solution)/shard_map/ppermute | solution.py:266
  15.6 111.6 %collective-permute-start.5 = (bf16[1024,1024]{1,0:T(8,128)(2,1)}, bf16[1024,1024]{1,0:T(8,128)(2,1)}, u32[]{:S(2)}, u32[]{:S(2)}) collective-permute-start(bf16[1024,1024]{1,0:T(8,128)(2,1)} %slice.13), channel_id=1, source_target_pairs={{1,0},{2,1},{3,2},{0,3},{5,4},{6,5},{7,6},{4,7}} | collective-permute-start | bytes 6291464 | tf_op jit(solution)/shard_map/ppermute | solution.py:266
  17.9 108.0 %collective-permute-start = (bf16[512,1024]{1,0:T(8,128)(2,1)}, bf16[512,1024]{1,0:T(8,128)(2,1)}, u32[]{:S(2)}, u32[]{:S(2)}) collective-permute-start(bf16[512,1024]{1,0:T(8,128)(2,1)} %slice.12), channel_id=1, source_target_pairs={{1,0},{2,1},{3,2},{0,3},{5,4},{6,5},{7,6},{4,7}} | collective-permute-start | bytes 3145736 | tf_op jit(solution)/shard_map/ppermute | solution.py:266
  57.5 90.2 %collective-permute-start.10 = (bf16[1904,1024]{1,0:T(8,128)(2,1)}, bf16[1904,1024]{1,0:T(8,128)(2,1)}, u32[]{:S(2)}, u32[]{:S(2)}) collective-permute-start(bf16[1904,1024]{1,0:T(8,128)(2,1)} %collective-permute-done.9.refs_1_), channel_id=1, source_target_pairs={{1,0},{5,4}} | collective-permute-start | bytes 11698184 | tf_op jit(solution)/shard_map/ppermute | solution.py:266
  60.7 3.1 %copy-start.1 = (bf16[3584,1024]{1,0:T(8,128)(2,1)S(1)}, bf16[3584,1024]{1,0:T(8,128)(2,1)}, u32[]{:S(2)}) copy-start(bf16[3584,1024]{1,0:T(8,128)(2,1)} %copy-done) | copy-start | bytes 22020100
  95.6 3.1 %copy-start.2 = (bf16[3584,1024]{1,0:T(8,128)(2,1)S(1)}, bf16[3584,1024]{1,0:T(8,128)(2,1)}, u32[]{:S(2)}) copy-start(bf16[3584,1024]{1,0:T(8,128)(2,1)} %copy-done) | copy-start | bytes 22020100
  101.0 45.4 %collective-permute-start.16 = (bf16[672,1024]{1,0:T(8,128)(2,1)}, bf16[672,1024]{1,0:T(8,128)(2,1)}, u32[]{:S(2)}, u32[]{:S(2)}) collective-permute-start(bf16[672,1024]{1,0:T(8,128)(2,1)} %get-tuple-element.23), channel_id=1, source_target_pairs={{3,1},{7,5}} | collective-permute-start | bytes 4128776 | tf_op jit(solution)/shard_map/ppermute | solution.py:266
  102.3 22.3 %collective-permute-start.14 = (bf16[144,1024]{1,0:T(8,128)(2,1)S(1)}, bf16[144,1024]{1,0:T(8,128)(2,1)S(1)}, u32[]{:S(2)}, u32[]{:S(2)}) collective-permute-start(bf16[144,1024]{1,0:T(8,128)(2,1)S(1)} %collective-permute-done.13.refs_0_), channel_id=1, source_target_pairs={{1,0},{5,4}} | collective-permute-start | bytes 884744 | tf_op jit(solution)/shard_map/ppermute | solution.py:266
  124.6 34.6 %collective-permute-start.12 = (bf16[768,1024]{1,0:T(8,128)(2,1)}, bf16[768,1024]{1,0:T(8,128)(2,1)}, u32[]{:S(2)}, u32[]{:S(2)}) collective-permute-start(bf16[768,1024]{1,0:T(8,128)(2,1)} %get-tuple-element.22), channel_id=1, source_target_pairs={{3,1},{7,5}} | collective-permute-start | bytes 4718600 | tf_op jit(solution)/shard_map/ppermute | solution.py:266
  125.9 45.3 %collective-permute-start.11 = (bf16[768,1024]{1,0:T(8,128)(2,1)}, bf16[768,1024]{1,0:T(8,128)(2,1)}, u32[]{:S(2)}, u32[]{:S(2)}) collective-permute-start(bf16[768,1024]{1,0:T(8,128)(2,1)} %get-tuple-element.21), channel_id=1, source_target_pairs={{3,1},{7,5}} | collective-permute-start | bytes 4718600 | tf_op jit(solution)/shard_map/ppermute | solution.py:266
  127.2 45.3 %collective-permute-start.6 = (bf16[1024,1024]{1,0:T(8,128)(2,1)}, bf16[1024,1024]{1,0:T(8,128)(2,1)}, u32[]{:S(2)}, u32[]{:S(2)}) collective-permute-start(bf16[1024,1024]{1,0:T(8,128)(2,1)} %collective-permute-done.5.refs_0_), channel_id=1, source_target_pairs={{1,0},{5,4}} | collective-permute-start | bytes 6291464 | tf_op jit(solution)/shard_map/ppermute | solution.py:266
  146.4 37.3 %collective-permute-start.8 = (bf16[464,1024]{1,0:T(8,128)(2,1)}, bf16[464,1024]{1,0:T(8,128)(2,1)}, u32[]{:S(2)}, u32[]{:S(2)}) collective-permute-start(bf16[464,1024]{1,0:T(8,128)(2,1)} %get-tuple-element.20), channel_id=1, source_target_pairs={{3,1},{7,5}} | collective-permute-start | bytes 2850824 | tf_op jit(solution)/shard_map/ppermute | solution.py:266
  147.7 43.1 %collective-permute-start.7 = (bf16[272,1024]{1,0:T(8,128)(2,1)}, bf16[272,1024]{1,0:T(8,128)(2,1)}, u32[]{:S(2)}, u32[]{:S(2)}) collective-permute-start(bf16[272,1024]{1,0:T(8,128)(2,1)} %get-tuple-element.19), channel_id=1, source_target_pairs={{3,1},{7,5}} | collective-permute-start | bytes 1671176 | tf_op jit(solution)/shard_map/ppermute | solution.py:266
  159.2 31.6 %collective-permute-start.1 = (bf16[512,1024]{1,0:T(8,128)(2,1)}, bf16[512,1024]{1,0:T(8,128)(2,1)}, u32[]{:S(2)}, u32[]{:S(2)}) collective-permute-start(bf16[512,1024]{1,0:T(8,128)(2,1)} %collective-permute-done.refs_1_), channel_id=1, source_target_pairs={{1,0},{5,4}} | collective-permute-start | bytes 3145736 | tf_op jit(solution)/shard_map/ppermute | solution.py:266
  171.2 23.7 %collective-permute-start.4 = (bf16[192,1024]{1,0:T(8,128)(2,1)}, bf16[192,1024]{1,0:T(8,128)(2,1)}, u32[]{:S(2)}, u32[]{:S(2)}) collective-permute-start(bf16[192,1024]{1,0:T(8,128)(2,1)} %get-tuple-element.18), channel_id=1, source_target_pairs={{3,1},{7,5}} | collective-permute-start | bytes 1179656 | tf_op jit(solution)/shard_map/ppermute | solution.py:266
  172.5 25.8 %collective-permute-start.3 = (bf16[160,1024]{1,0:T(8,128)(2,1)}, bf16[160,1024]{1,0:T(8,128)(2,1)}, u32[]{:S(2)}, u32[]{:S(2)}) collective-permute-start(bf16[160,1024]{1,0:T(8,128)(2,1)} %get-tuple-element.17), channel_id=1, source_target_pairs={{3,1},{7,5}} | collective-permute-start | bytes 983048 | tf_op jit(solution)/shard_map/ppermute | solution.py:266
  183.6 17.9 %collective-permute-start.2 = (bf16[144,1024]{1,0:T(8,128)(2,1)}, bf16[144,1024]{1,0:T(8,128)(2,1)}, u32[]{:S(2)}, u32[]{:S(2)}) collective-permute-start(bf16[144,1024]{1,0:T(8,128)(2,1)} %get-tuple-element.15), channel_id=1, source_target_pairs={{3,1},{7,5}} | collective-permute-start | bytes 884744 | tf_op jit(solution)/shard_map/ppermute | solution.py:266
